TPU v7x, 32 devices: a whole 2x2x4 slice. The times are simulated.
32 devices in a mesh: data: 32 (over z, y, x, core).
Axes of the slice: x: 2, y: 2, z: 4, core: 2. Of those that a mesh axis runs over, the one named last changes fastest.
Arguments:
- x_in: bfloat16 [32, 384, 1024], P('data')
- grad_y: bfloat16 [32, 384, 1024], P('data')
- gain_one: float32 [2, 1024], replicated
- gain_two: float32 [2, 1024], replicated
- w_qkv: bfloat16 [2, 1024, 3072], replicated
- w_out: bfloat16 [2, 1024, 1024], replicated
- w_up: bfloat16 [2, 1024, 4096], replicated
- w_down: bfloat16 [2, 4096, 1024], replicated
Outputs:
- output 1: bfloat16 [32, 384, 1024], P('data')
- output 2: float32 [2, 1024], replicated
- output 3: float32 [2, 1024], replicated
- output 4: float32 [2, 1024, 3072], replicated
- output 5: float32 [2, 1024, 1024], replicated
- output 6: float32 [2, 1024, 4096], replicated
- output 7: float32 [2, 4096, 1024], replicated
All inputs are finite; a program needn't handle non-finite values.
Results may differ from a plain program's by a relative error of at most 0.02.
Values are sent between devices in bfloat16 or wider.
A program may use at most 1 GiB of HBM per device.

v0:
```python
import functools

import jax
import jax.numpy as jnp
from jax import lax
from jax.experimental import pallas as pl
from jax.experimental.pallas import tpu as pltpu
from jax.sharding import PartitionSpec as P


NORM_EPS = 1e-6
HEAD_DIM = 64
AXIS = 'data'
CHUNKS = ((3, 1, 0), (1, 1, 0), (0, 0, 0), (1, 1, 1), (1, 1, 2), (2, 1, 0), (0, 1, 0), (3, 0, 0), (3, 0, 1), (1, 1, 3), (3, 1, 1), (1, 0, 0), (0, 0, 1), (2, 0, 0), (1, 0, 1), (0, 1, 1))
ORDER = (
    'a9a0b9c9b0c0d0nfa1hff9e0b1g9f0a2d1h9c1g0h0b2a3e1f1i0j0b3d2h1',
    'b4l9d3g1k0l0c2a4b6i1n9m0d4e2j1n0f2c3a6e3a5h2k1o0d6m1p0b5n1f3',
    'g2l1a7a8d5i2b7h3c4b8p1j2e4g3o1f4k2i3d7c5j3d8c6h4m2e6e5n2k3g4',
    'f6f5i4l2m3j4h6n3h5c7e7c8l3e8p2g5m4o2g6i6p3f7l4f8o3i5j6h7k4h8',
    'j5p4m5n4g7g8k6m6o4l6i7n6i8l5k5j7j8p5p6k7k8m7n5m8o5l7o6n7n8l8',
    'p7o7p8o8',
)


def rms_gain(rows_f, gain_vec):
    return rows_f * lax.rsqrt(jnp.mean(rows_f * rows_f, axis=-1, keepdims=True) + NORM_EPS) * gain_vec


def gelu_tanh(pre_act):
    return jax.nn.gelu(pre_act, approximate=True)


def mix_lo(einsum_spec, lhs_arr, rhs_arr):
    return jnp.einsum(einsum_spec, lhs_arr, rhs_arr, preferred_element_type=jnp.float32).astype(jnp.bfloat16)


def block_forward(x_blk, gain_a, gain_b, w_qkv, w_out, w_up):
    norm_a, norm_a_back = jax.vjp(rms_gain, x_blk.astype(jnp.float32), gain_a)
    u_one = norm_a.astype(jnp.bfloat16)
    qkv_lo = mix_lo('sd,de->se', u_one, w_qkv)
    attn_out = attn_forward(qkv_lo)
    hidden = x_blk + mix_lo('sd,de->se', attn_out, w_out)
    norm_b, norm_b_back = jax.vjp(rms_gain, hidden.astype(jnp.float32), gain_b)
    u_two = norm_b.astype(jnp.bfloat16)
    pre_lo = mix_lo('sd,df->sf', u_two, w_up)
    act_f, gelu_back = jax.vjp(gelu_tanh, pre_lo.astype(jnp.float32))
    act_lo = act_f.astype(jnp.bfloat16)
    saved_vals = (norm_a_back, u_one, qkv_lo, attn_out, norm_b_back, u_two, gelu_back, act_lo)
    return hidden, act_lo, saved_vals


class Place:
    def __init__(self, n_dev):
        me = lax.axis_index(AXIS)
        self.core = me % 2
        self.x = (me // 2) % 2
        self.y = (me // 4) % 2
        self.swap = {name: [(i, i ^ bit) for i in range(n_dev)] for name, bit in (('core', 1), ('x', 2), ('y', 4))}

    def at(self, name):
        return {'core': self.core, 'x': self.x, 'y': self.y}[name]


def send(val, pairs):
    return lax.ppermute(val, AXIS, pairs)


def part(val, which, count, axis):
    size = val.shape[axis] // count
    return lax.dynamic_slice_in_dim(val, which * size, size, axis)


def neighbour_operands(place, axis, split, lhs, rhs):
    away = part(lhs if split == 0 else rhs, 1 - place.at(axis), 2, 1)
    if split == 1:
        away, rhs = lax.optimization_barrier((away, rhs))
    wide, thin = (lhs, rhs) if split == 0 else (rhs, lhs)
    wide_in = send(away, place.swap[axis])
    thin_in = send(thin, place.swap[axis])
    return rhs, (wide, thin, wide_in, thin_in)


PAIR = 2 * HEAD_DIM
Q_BLOCK = 128


def two_heads(rows):
    first = lax.broadcasted_iota(jnp.int32, rows.shape, 1) < HEAD_DIM
    zero = jnp.zeros_like(rows)
    return jnp.concatenate([jnp.where(first, rows, zero), jnp.where(first, zero, rows)], axis=0)


def one_pair(rows):
    half = rows.shape[0] // 2
    first = lax.broadcasted_iota(jnp.int32, (half, PAIR), 1) < HEAD_DIM
    return jnp.where(first, rows[:half], rows[half:])


def dot_f32(lhs, rhs, lhs_dim, rhs_dim):
    return lax.dot_general(lhs, rhs, (((lhs_dim,), (rhs_dim,)), ((), ())), preferred_element_type=jnp.float32)


def softmax_block(q_two, k_rows, block):
    scores = dot_f32(q_two, k_rows, 1, 1) * HEAD_DIM ** -0.5
    row = lax.rem(lax.broadcasted_iota(jnp.int32, scores.shape, 0), Q_BLOCK) + block * Q_BLOCK
    scores = jnp.where(row >= lax.broadcasted_iota(jnp.int32, scores.shape, 1), scores, -1e30)
    weights = jnp.exp(scores - jnp.max(scores, axis=-1, keepdims=True))
    return weights / jnp.sum(weights, axis=-1, keepdims=True)


def attn_forward_kernel(qkv_ref, out_ref):
    seq_len, width = out_ref.shape

    @pl.loop(0, width // PAIR)
    def _(pair):
        def lanes(which):
            return pl.ds(pl.multiple_of(which * width + pair * PAIR, PAIR), PAIR)

        for block in range(seq_len // Q_BLOCK):
            rows, keys = pl.ds(block * Q_BLOCK, Q_BLOCK), pl.ds(0, (block + 1) * Q_BLOCK)
            prob = softmax_block(two_heads(qkv_ref[rows, lanes(0)]), qkv_ref[keys, lanes(1)], block)
            mixed = dot_f32(prob.astype(jnp.bfloat16), qkv_ref[keys, lanes(2)], 1, 0)
            out_ref[rows, lanes(0)] = one_pair(mixed).astype(jnp.bfloat16)


def attn_backward_kernel(qkv_ref, grad_ref, out_ref, k_acc, v_acc):
    seq_len, width = grad_ref.shape

    @pl.loop(0, width // PAIR)
    def _(pair):
        def lanes(which):
            return pl.ds(pl.multiple_of(which * width + pair * PAIR, PAIR), PAIR)

        n_block = seq_len // Q_BLOCK
        for block in reversed(range(n_block)):
            rows, keys = pl.ds(block * Q_BLOCK, Q_BLOCK), pl.ds(0, (block + 1) * Q_BLOCK)
            q_two, g_two = two_heads(qkv_ref[rows, lanes(0)]), two_heads(grad_ref[rows, lanes(0)])
            k_rows = qkv_ref[keys, lanes(1)]
            prob = softmax_block(q_two, k_rows, block)
            grad_prob = dot_f32(g_two, qkv_ref[keys, lanes(2)], 1, 1)
            mean = jnp.sum(prob * grad_prob, axis=-1, keepdims=True)
            grad_s = (prob * (grad_prob - mean) * HEAD_DIM ** -0.5).astype(jnp.bfloat16)
            out_ref[rows, lanes(0)] = one_pair(dot_f32(grad_s, k_rows, 1, 0)).astype(jnp.bfloat16)
            k_part, v_part = dot_f32(grad_s, q_two, 0, 0), dot_f32(prob.astype(jnp.bfloat16), g_two, 0, 0)
            if block == n_block - 1:
                k_acc[...] = k_part
                v_acc[...] = v_part
            else:
                k_acc[keys, :] += k_part
                v_acc[keys, :] += v_part
        out_ref[:, lanes(1)] = k_acc[...].astype(jnp.bfloat16)
        out_ref[:, lanes(2)] = v_acc[...].astype(jnp.bfloat16)


def attn_forward(qkv):
    seq_len, width3 = qkv.shape
    width = width3 // 3
    vmem = pl.BlockSpec(memory_space=pltpu.VMEM)
    return pl.pallas_call(
        attn_forward_kernel, out_shape=jax.ShapeDtypeStruct((seq_len, width), jnp.bfloat16), in_specs=[vmem], out_specs=vmem,
        cost_estimate=pl.CostEstimate(flops=6 * seq_len * seq_len * width, bytes_accessed=8 * seq_len * width, transcendentals=0))(qkv)


def attn_backward(qkv, grad):
    seq_len, width = grad.shape
    vmem = pl.BlockSpec(memory_space=pltpu.VMEM)
    return pl.pallas_call(
        attn_backward_kernel, out_shape=jax.ShapeDtypeStruct(qkv.shape, jnp.bfloat16), in_specs=[vmem, vmem], out_specs=vmem,
        scratch_shapes=[pltpu.VMEM((seq_len, PAIR), jnp.float32)] * 2,
        cost_estimate=pl.CostEstimate(flops=16 * seq_len * seq_len * width, bytes_accessed=14 * seq_len * width, transcendentals=0))(qkv, grad)


MATRICES = (
    (1024, 1024, 'x', 0),
    (1024, 1024, 'y', 1),
    (256, 1024, 'x', 0),
    (1024, 768, 'y', 1),
)
Z_LAST = ((2, 0), (3, 1))

LATE = ((2, 0), (3, 0))
SEQ_LEN = 384
TOKENS = 4 * SEQ_LEN
TILE_ROWS = 256
N_SEMS = 16
ADD_ROWS = 32


def chunk_count(mat, layer):
    return sum(chunk[:2] == (mat, layer) for chunk in CHUNKS)


def add_rows(dst, src, cols, scale=None):
    rows = dst.shape[0]

    @pl.loop(0, rows // ADD_ROWS)
    def _(step):
        at = pl.ds(pl.multiple_of(step * ADD_ROWS, ADD_ROWS), ADD_ROWS)
        val = dst[at, cols] + src[at, :]
        dst[at, cols] = val if scale is None else val * scale


def flip(bit, by):
    return 1 - bit if by else bit


def combine_kernel(n_dev, n_layers, *refs):
    units = [(mat, layer) for layer in range(n_layers) for mat in range(len(MATRICES))]
    n_chunk = len(CHUNKS)
    refs = list(refs)

    def take(count):
        head, refs[:] = refs[:count], refs[count:]
        return head

    given = [take(2 if unit in LATE else 4) for unit in units]
    gain_in, = take(1)
    outs, (gain_out,) = take(len(MATRICES)), take(1)
    from_core, part_refs, from_chip = take(2 * len(units)), take(len(units)), take(2 * len(LATE))
    own, land_q, land_z, land_h = (take(n_chunk) for _ in range(4))
    row_op, col_op, product, gain_buf, gain_land, send_sems, recv_sems, local_sems, gain_send, gain_recv, op_send, op_recv, op_local = refs

    me = lax.axis_index(AXIS)
    core, x_at, y_at, z_at = lax.rem(me, 2), lax.rem(lax.div(me, 2), 2), lax.rem(lax.div(me, 4), 2), lax.div(me, 8)
    half = lax.div(z_at, 2)
    middle = lax.div(z_at + 1, 2) == 1
    edge = lax.div(z_at + 1, 2) != 1
    place = {'x': x_at, 'y': y_at}
    to = {'core': me + 1 - 2 * core, 'x': me + 2 * (1 - 2 * x_at), 'y': me + 4 * (1 - 2 * y_at),
          'mid': me + 8 * (1 - 2 * half), 'end': me - 8 * (1 - 2 * half)}

    def remote(src, dst, i, sem, dev):
        return pltpu.make_async_remote_copy(src_ref=src, dst_ref=dst, send_sem=send_sems.at[i, sem], recv_sem=recv_sems.at[i, sem],
                                            device_id=(dev,), device_id_type=pl.DeviceIdType.MESH)

    def out_block(i, p_at, c_at, q_at, h_at):
        mat, layer, k = CHUNKS[i]
        rows_all, cols, _, split = MATRICES[mat]
        rows = rows_all // chunk_count(mat, layer)
        row = k * rows
        col = 0
        if split == 0:
            row = row + (p_at * 2 + c_at) * rows_all
        else:
            col = (p_at * 2 + c_at) * cols
        n_rows, n_cols = rows, cols
        if q_at is not None:
            n_rows = rows // 2
            row = row + q_at * n_rows
        if h_at is not None:
            n_cols = cols // 2
            col = col + h_at * n_cols
        if not isinstance(row, int):
            row = pl.multiple_of(row, 8)
        if not isinstance(col, int):
            col = pl.multiple_of(col, 128)
        return outs[mat].at[layer, pl.ds(row, n_rows), pl.ds(col, n_cols)]

    def run(i, stage, pending):
        mat, layer, k = CHUNKS[i]
        rows_all, cols, p_name, _ = MATRICES[mat]
        z_last = (mat, layer) in Z_LAST
        q_name = 'y' if p_name == 'x' else 'x'
        p_at, q_at = place[p_name], place[q_name]
        rows = rows_all // chunk_count(mat, layer)
        part = part_refs[layer * len(MATRICES) + mat]

        def go(src, dst, sem, dest, cond=None):
            remote(src(), dst(), i, sem, to[dest]).start()
            pending.append((cond, src, i, sem))

        def block(dp=0, dq=0, dc=0, dh=None, q_whole=False):
            return lambda: out_block(i, flip(p_at, dp), flip(core, dc), None if q_whole else flip(q_at, dq), None if dh is None else flip(half, dh))

        def pass_on(blk, sems, cond=None):
            for dest, sem in sems:
                go(blk, blk, sem, dest, cond)

        def arrived(blk, sem):
            remote(blk(), blk(), i, sem, me).wait_recv()

        def half_cols(h):
            return pl.ds(pl.multiple_of(h * (cols // 2), 128), cols // 2)

        def own_half(by):
            return lambda: own[i].at[:, half_cols(flip(half, by))]

        def rows_of(q):
            return lambda: part.at[pl.ds(pl.multiple_of(k * rows + q * (rows // 2), 8), rows // 2), :]

        def load():
            return pltpu.make_async_copy(rows_of(q_at)(), own[i], local_sems.at[i, 0])

        def keep():
            return pltpu.make_async_copy(own_half(0)(), block(dh=0)(), local_sems.at[i, 1])

        def whole(buf):
            return lambda: buf[i]

        if stage == 0:
            go(rows_of(1 - q_at), whole(land_q), 0, q_name)
            load().start()
        elif stage == 1:
            load().wait()
            arrived(whole(land_q), 0)
            add_rows(own[i], land_q[i], slice(None))

            @pl.when(edge)
            def _():
                go(whole(own), whole(land_z), 1, 'mid', edge)
        elif stage == 2:
            @pl.when(middle)
            def _():
                arrived(whole(land_z), 1)
                add_rows(own[i], land_z[i], slice(None))
                go(own_half(1), whole(land_h), 2, 'mid', middle)
        elif stage == 3:
            @pl.when(middle)
            def _():
                arrived(whole(land_h), 2)
                add_rows(own[i], land_h[i], half_cols(half), 1.0 / n_dev)
                keep().start()
                go(own_half(0), block(dh=0), 3, q_name if z_last else 'mid', middle)
        elif not z_last:
            if stage == 4:
                @pl.when(middle)
                def _():
                    keep().wait()
                    arrived(block(dh=1), 3)
                    pass_on(block(), (('end', 4),), middle)

                @pl.when(edge)
                def _():
                    arrived(block(), 4)

                pass_on(block(), ((q_name, 5), (p_name, 6), ('core', 8)))
            elif stage == 5:
                arrived(block(dq=1), 5)
                pass_on(block(dq=1), ((p_name, 7), ('core', 9)))
            elif stage == 6:
                arrived(block(dp=1), 6)
                pass_on(block(dp=1), (('core', 10),))
            elif stage == 7:
                arrived(block(dp=1, dq=1), 7)
                pass_on(block(dp=1, dq=1), (('core', 11),))
            else:
                for dp in range(2):
                    for dq in range(2):
                        arrived(block(dp=dp, dq=dq, dc=1), 8 + 2 * dp + dq)
        else:
            spots = {4: dict(dp=0, dh=0), 5: dict(dp=1, dh=0), 6: dict(dp=0, dh=1), 7: dict(dp=1, dh=1)}
            if stage < 8:
                blk = block(q_whole=True, **spots[stage])
                onward = {4: ((p_name, 4), ('mid', 5), ('end', 7)), 5: (('mid', 6), ('end', 8)), 6: (('end', 9),), 7: (('end', 10),)}[stage]

                @pl.when(middle)
                def _():
                    if stage == 4:
                        keep().wait()
                        arrived(block(dq=1, dh=0), 3)
                    else:
                        arrived(blk, stage - 1)
                    pass_on(blk, onward, middle)

                @pl.when(edge)
                def _():
                    arrived(blk, stage + 3)

                pass_on(blk, (('core', stage + 7),))
            else:
                for order, spot in enumerate((spots[4], spots[5], spots[6], spots[7])):
                    arrived(block(q_whole=True, dc=1, **spot), 11 + order)

    def unit_sizes(unit):
        rows, cols, p_name, split = MATRICES[unit[0]]
        return (rows, cols, p_name, split) + ((rows, cols) if split == 0 else (cols, rows))

    def operand_copy(u, which, src, dst, dest):
        return pltpu.make_async_remote_copy(src_ref=src, dst_ref=dst, send_sem=op_send.at[u, which], recv_sem=op_recv.at[u, which],
                                            device_id=(to[dest],), device_id_type=pl.DeviceIdType.MESH)

    def operand_copies(u):
        unit = units[u]
        _, _, p_name, split, wide_w, _ = unit_sizes(unit)
        p_at = place[p_name]
        wide, thin = given[u][:2]
        core_wide, core_thin = from_core[2 * u:2 * u + 2]
        if unit in LATE:
            late = LATE.index(unit)
            chip_wide, chip_thin = from_chip[2 * late:2 * late + 2]
        else:
            chip_wide, chip_thin = given[u][2:]
        first, second = pl.ds(0, SEQ_LEN), pl.ds(SEQ_LEN, SEQ_LEN)

        def lanes(at, count):
            return pl.ds(pl.multiple_of(at, 128), count)

        other = 1 - core
        copies = {
            'own': (operand_copy(u, 0, wide.at[:, lanes((p_at * 2 + other) * wide_w, wide_w)], core_wide.at[first, :], 'core'),
                    operand_copy(u, 1, thin, core_thin.at[first, :], 'core')),
            'next': (operand_copy(u, 2, chip_wide.at[:, lanes(other * wide_w, wide_w)], core_wide.at[second, :], 'core'),
                     operand_copy(u, 3, chip_thin, core_thin.at[second, :], 'core')),
        }
        if unit in LATE:
            copies['chip'] = (operand_copy(u, 4, wide.at[:, lanes((1 - p_at) * 2 * wide_w, 2 * wide_w)], chip_wide, p_name),
                              operand_copy(u, 5, thin, chip_thin, p_name))
        wide_op, thin_op = (row_op, col_op) if split == 0 else (col_op, row_op)
        thin_w = thin.shape[1]
        loads = []
        for start, src in ((0, wide.at[:, lanes((p_at * 2 + core) * wide_w, wide_w)]), (SEQ_LEN, chip_wide.at[:, lanes(core * wide_w, wide_w)]),
                           (2 * SEQ_LEN, core_wide)):
            loads.append((src, wide_op.at[pl.ds(start, src.shape[0]), pl.ds(0, wide_w)]))
        for start, src in ((0, thin), (SEQ_LEN, chip_thin), (2 * SEQ_LEN, core_thin)):
            loads.append((src, thin_op.at[pl.ds(start, src.shape[0]), pl.ds(0, thin_w)]))
        copies['load'] = tuple(pltpu.make_async_copy(src, dst, op_local.at[u, n]) for n, (src, dst) in enumerate(loads))
        return copies

    def start_operands(u):
        copies = operand_copies(u)
        if units[u] in LATE:
            for copy in copies['chip']:
                copy.start()
        for copy in copies['own']:
            copy.start()
        if units[u] not in LATE:
            for copy in copies['next']:
                copy.start()

    def forward_operands(u):
        copies = operand_copies(u)
        for copy in copies['chip']:
            copy.wait_recv()
        for copy in copies['next']:
            copy.start()

    def multiply(u):
        rows, cols, _, _, _, _ = unit_sizes(units[u])
        copies = operand_copies(u)
        for copy in copies['own'] + copies['next']:
            copy.wait_recv()
        for copy in copies['load']:
            copy.start()
        for copy in copies['load']:
            copy.wait()
        tile = min(TILE_ROWS, rows)
        half_w = cols // 2

        @pl.loop(0, rows // tile)
        def _(step):
            at = pl.ds(pl.multiple_of(step * tile, tile), tile)
            for side in range(2):
                lanes = pl.ds(side * half_w, half_w)
                product[at, lanes] = dot_f32(row_op[:, at], col_op[:, lanes], 0, 0)

        store = pltpu.make_async_copy(product.at[pl.ds(0, rows), pl.ds(0, cols)], part_refs[u], op_local.at[u, 6])
        store.start()
        store.wait()

    def finish_operands(u):
        copies = operand_copies(u)
        for copy in copies['own'] + copies['next'] + copies.get('chip', ()):
            copy.wait_send()

    gain_steps = ('core', 'x', 'y', 'mid', 'far')
    far = lax.rem(z_at + 2, 4)
    gain_to = dict(to, mid=me + 8 * (1 - 2 * lax.rem(z_at, 2)), far=me + 8 * (far - z_at))

    def gain_copy(step):
        return pltpu.make_async_remote_copy(src_ref=gain_buf.at[step], dst_ref=gain_land.at[step], send_sem=gain_send.at[step],
                                            recv_sem=gain_recv.at[step], device_id=(gain_to[gain_steps[step]],), device_id_type=pl.DeviceIdType.MESH)

    def gain_next(step):
        copy = gain_copy(step)
        copy.wait()
        total = gain_buf[step] + gain_land[step]
        if step + 1 < len(gain_steps):
            gain_buf[step + 1] = total
            gain_copy(step + 1).start()
        else:
            gain_out[...] = total * (1.0 / n_dev)

    pending = []
    gain_buf[0] = gain_in[...]
    step = 0
    first_use = []
    for mat, layer, _ in CHUNKS:
        if units.index((mat, layer)) not in first_use:
            first_use.append(units.index((mat, layer)))
    for u in first_use:
        start_operands(u)
    for count, (letter, digit) in enumerate(zip(*[iter(''.join(ORDER))] * 2)):
        i, stage = ord(letter) - ord('a'), int(digit, 16)
        u = units.index(CHUNKS[i][:2])
        if stage == 9:
            multiply(u)
        elif stage == 15:
            forward_operands(u)
        else:
            run(i, stage, pending)
        if count == 1:
            gain_copy(0).start()
        if count >= 8 and count % 6 == 0 and step < len(gain_steps):
            gain_next(step)
            step += 1
    for u in range(len(units)):
        finish_operands(u)
    for cond, src, i, sem in pending:
        def finish(src=src, i=i, sem=sem):
            remote(src(), src(), i, sem, me).wait_send()

        if cond is None:
            finish()
        else:
            pl.when(cond)(finish)


def combine(operands, gains, n_dev, n_layers):
    f32, bf16 = jnp.float32, jnp.bfloat16
    units = [(mat, layer) for layer in range(n_layers) for mat in range(len(MATRICES))]
    outs = []
    for rows, cols, _, split in MATRICES:
        outs.append(jax.ShapeDtypeStruct((n_layers, rows * (4 if split == 0 else 1), cols * (4 if split == 1 else 1)), f32))
    outs.append(jax.ShapeDtypeStruct(gains.shape, f32))
    widths = [MATRICES[mat][:2] if MATRICES[mat][3] == 0 else MATRICES[mat][1::-1] for mat, _ in units]
    for wide_w, thin_w in widths:
        outs += [jax.ShapeDtypeStruct((2 * SEQ_LEN, wide_w), bf16), jax.ShapeDtypeStruct((2 * SEQ_LEN, thin_w), bf16)]
    outs += [jax.ShapeDtypeStruct(MATRICES[mat][:2], f32) for mat, _ in units]
    for unit in LATE:
        wide_w, thin_w = widths[units.index(unit)]
        outs += [jax.ShapeDtypeStruct((SEQ_LEN, 2 * wide_w), bf16), jax.ShapeDtypeStruct((SEQ_LEN, thin_w), bf16)]
    halves = [(MATRICES[mat][0] // chunk_count(mat, layer) // 2, MATRICES[mat][1]) for mat, layer, _ in CHUNKS]
    scratch = [pltpu.VMEM(s, f32) for _ in range(3) for s in halves] + [pltpu.VMEM((r, c // 2), f32) for r, c in halves]
    n_chunk, n_unit = len(CHUNKS), len(units)
    most_rows, most_cols = max(m[0] for m in MATRICES), max(m[1] for m in MATRICES)
    scratch += [pltpu.VMEM((TOKENS, most_rows), bf16), pltpu.VMEM((TOKENS, most_cols), bf16), pltpu.VMEM((most_rows, most_cols), f32),
                pltpu.VMEM((5,) + gains.shape, f32), pltpu.VMEM((5,) + gains.shape, f32),
                pltpu.SemaphoreType.DMA((n_chunk, N_SEMS)), pltpu.SemaphoreType.DMA((n_chunk, N_SEMS)), pltpu.SemaphoreType.DMA((n_chunk, 2)),
                pltpu.SemaphoreType.DMA((5,)), pltpu.SemaphoreType.DMA((5,)),
                pltpu.SemaphoreType.DMA((n_unit, 6)), pltpu.SemaphoreType.DMA((n_unit, 6)), pltpu.SemaphoreType.DMA((n_unit, 7))]
    hbm, vmem = pl.BlockSpec(memory_space=pl.ANY), pl.BlockSpec(memory_space=pltpu.VMEM)
    flat = [val for group in operands for val in group]
    results = pl.pallas_call(
        functools.partial(combine_kernel, n_dev, n_layers),
        out_shape=tuple(outs),
        in_specs=[hbm] * len(flat) + [vmem],
        out_specs=tuple([hbm] * 4 + [vmem] + [hbm] * (len(outs) - 5)),
        scratch_shapes=scratch,
        compiler_params=pltpu.CompilerParams(has_side_effects=True, vmem_limit_bytes=63 * 1024 * 1024),
    )(*flat, gains)
    return results[:5]


def solution(mesh):
    n_dev = mesh.shape[AXIS]

    def whole_step(x_loc, grad_y_loc, gain_one, gain_two, w_qkv, w_out, w_up, w_down):
        place = Place(n_dev)
        n_layers = w_qkv.shape[0]
        hidden_x = x_loc[0]
        saved_all = []
        for layer_idx in range(n_layers):
            hidden, act_lo, saved_vals = block_forward(hidden_x, gain_one[layer_idx], gain_two[layer_idx], w_qkv[layer_idx], w_out[layer_idx], w_up[layer_idx])
            saved_all.append(saved_vals)
            if layer_idx + 1 < n_layers:
                hidden_x = hidden + mix_lo('sf,fd->sd', act_lo, w_down[layer_idx])
        operands = [None] * (n_layers * len(MATRICES))

        def reduce_grad(mat, layer_idx, lhs, rhs):
            _, _, color, split = MATRICES[mat]
            if (mat, layer_idx) in LATE:
                operands[layer_idx * len(MATRICES) + mat] = (lhs, rhs) if split == 0 else (rhs, lhs)
            else:
                rhs, operands[layer_idx * len(MATRICES) + mat] = neighbour_operands(place, color, split, lhs, rhs)
            return rhs

        gain_grads = [None] * (2 * n_layers)
        grad_blk = grad_y_loc[0]
        for layer_idx in reversed(range(n_layers)):
            (norm_a_back, u_one, qkv_lo, attn_out, norm_b_back, u_two, gelu_back, act_lo) = saved_all[layer_idx]
            grad_blk = reduce_grad(0, layer_idx, act_lo, grad_blk)
            grad_act = mix_lo('sd,fd->sf', grad_blk, w_down[layer_idx])
            (grad_pre_f,) = gelu_back(grad_act.astype(jnp.float32))
            grad_pre = grad_pre_f.astype(jnp.bfloat16)
            grad_pre = reduce_grad(1, layer_idx, u_two, grad_pre)
            grad_u_two = mix_lo('sf,df->sd', grad_pre, w_up[layer_idx])
            grad_h_norm, gain_grads[n_layers + layer_idx] = norm_b_back(grad_u_two.astype(jnp.float32))
            grad_hidden = (grad_blk.astype(jnp.float32) + grad_h_norm).astype(jnp.bfloat16)
            grad_hidden = reduce_grad(2, layer_idx, attn_out, grad_hidden)
            grad_attn = mix_lo('se,de->sd', grad_hidden, w_out[layer_idx])
            grad_qkv = attn_backward(qkv_lo, grad_attn)
            grad_qkv = reduce_grad(3, layer_idx, u_one, grad_qkv)
            grad_u_one = mix_lo('se,de->sd', grad_qkv, w_qkv[layer_idx])
            grad_x_norm, gain_grads[layer_idx] = norm_a_back(grad_u_one.astype(jnp.float32))
            grad_blk = (grad_hidden.astype(jnp.float32) + grad_x_norm).astype(jnp.bfloat16)
        gains = jnp.concatenate([jnp.stack(gain_grads), jnp.zeros((8 - 2 * n_layers, gain_grads[0].shape[0]), jnp.float32)])
        down, up, out, qkv, gains = combine(operands, gains, n_dev, n_layers)
        return (grad_blk[None], gains[:n_layers], gains[n_layers:2 * n_layers], qkv, out, up, down)

    batch_spec = P(AXIS)
    full_spec = P()
    return jax.shard_map(whole_step, mesh=mesh, in_specs=(batch_spec, batch_spec) + (full_spec,) * 6, out_specs=(batch_spec,) + (full_spec,) * 6, check_vma=False)
```

profile of v0, /device:TPU:1, one launch (start us, length us, event | category | flops | bytes accessed | tf_op | source)
XLA Modules:
  0.0 921.4 jit_solution(8657867021415568598)
XLA Ops:
  0.6 2.1 collective-permute-start.5
  6.2 7.1 fusion.67.qkv_ref
  13.4 13.1 %shard_map.135.refs_8_ = bf16[384,1024]{1,0:T(8,128)(2,1)} custom-call(bf16[384,3072]{1,0:T(8,128)(2,1)} %fusion.67.qkv_ref), custom_call_target="tpu_custom_call" | custom-call | flops 905969664 | bytes 3145728 | tf_op jit(solution)/shard_map/pallas_call | solution.py:159
  26.4 2.9 fusion.115
  31.8 9.2 fusion.34
  41.1 4.3 fusion.117
  46.8 7.1 fusion.70.qkv_ref
  53.9 12.9 %shard_map.136.refs_20_ = bf16[384,1024]{1,0:T(8,128)(2,1)} custom-call(bf16[384,3072]{1,0:T(8,128)(2,1)} %fusion.70.qkv_ref), custom_call_target="tpu_custom_call" | custom-call | flops 905969664 | bytes 3145728 | tf_op jit(solution)/shard_map/pallas_call | solution.py:159
  66.8 1.8 constant_dynamic-slice_fusion
  68.6 2.9 fusion.119
  75.1 9.3 %fusion.42 = (bf16[384,4096]{1,0:T(8,128)(2,1)}, bf16[384,4096]{1,0:T(8,128)(2,1)}) fusion(bf16[384,1024]{1,0:T(8,128)(2,1)} %fusion.97.refs_17_, bf16[2,1024,4096]{2,1,0:T(8,128)(2,1)} %param.14), kind=kOutput, calls=%fused_computation.54 | convolution fusion | flops 3238526976 | bytes 15466496 | tf_op jit(solution)/shard_map/sd,df->sf/dot_general | solution.py:34
  84.4 9.9 %fusion.25.refs_16_ = bf16[384,4096]{1,0:T(8,128)(2,1)S(1)} fusion(bf16[384,4096]{1,0:T(8,128)(2,1)} %get-tuple-element.58, bf16[2,4096,1024]{2,1,0:T(8,128)(2,1)} %param.15, bf16[1,384,1024]{2,1,0:T(8,128)(2,1)} %param.9), kind=kOutput, calls=%fused_computation.37 | convolution fusion | flops 3257401344 | bytes 15466496 | tf_op jit(solution)/shard_map/sd,fd->sf/dot_general | solution.py:34
  96.0 7.9 fusion.101
  104.5 1.9 fusion.145.grad_ref
  106.5 18.3 %shard_map.137.refs_24_ = bf16[384,3072]{1,0:T(8,128)(2,1)} custom-call(bf16[384,3072]{1,0:T(8,128)(2,1)} %fusion.70.qkv_ref, bf16[384,1024]{1,0:T(8,128)(2,1)} %fusion.145.grad_ref), custom_call_target="tpu_custom_call" | custom-call | flops 2415919104 | bytes 5505024 | tf_op jit(solution)/shard_map/pallas_call | solution.py:167
  124.8 2.4 constant_dynamic-slice_fusion.4
  127.1 7.2 fusion.102
  136.2 9.8 %fusion.28.refs_4_ = bf16[384,4096]{1,0:T(8,128)(2,1)S(1)} fusion(bf16[384,4096]{1,0:T(8,128)(2,1)S(1)} %copy-done.39, bf16[384,1024]{1,0:T(8,128)(2,1)S(1)} %fusion.108.refs_1_, bf16[2,4096,1024]{2,1,0:T(8,128)(2,1)} %param.15), kind=kOutput, calls=%fused_computation.40 | convolution fusion | flops 3257401344 | bytes 15466496 | tf_op jit(solution)/shard_map/sd,fd->sf/dot_general | solution.py:34
  147.7 5.2 fusion.103
  152.9 1.8 fusion.110.refs_9_
  159.0 3.5 fusion.139.grad_ref
  165.3 6.7 collective-permute-done.9.refs_23_
  174.1 18.0 %shard_map.138.refs_10_ = bf16[384,3072]{1,0:T(8,128)(2,1)} custom-call(bf16[384,3072]{1,0:T(8,128)(2,1)} %fusion.67.qkv_ref, bf16[384,1024]{1,0:T(8,128)(2,1)} %fusion.139.grad_ref), custom_call_target="tpu_custom_call" | custom-call | flops 2415919104 | bytes 5505024 | tf_op jit(solution)/shard_map/pallas_call | solution.py:167
  192.4 6.4 fusion.104
  199.6 1.8 fusion.100
  201.4 54.7 %collective-permute-done.10.refs_26_ = bf16[384,1536]{1,0:T(8,128)(2,1)} collective-permute-done((bf16[384,1536]{1,0:T(8,128)(2,1)}, bf16[384,1536]{1,0:T(8,128)(2,1)}, u32[]{:S(2)}, u32[]{:S(2)}) %collective-permute-start.10) | collective-permute-done | bytes 1179680 | tf_op jit(solution)/shard_map/ppermute | solution.py:65
  256.3 596.0 %shard_map.139 = (f32[2,4096,1024]{2,1,0:T(8,128)}, f32[2,1024,4096]{2,1,0:T(8,128)}, f32[2,1024,1024]{2,1,0:T(8,128)}, f32[2,1024,3072]{2,1,0:T(8,128)}, f32[8,...) custom-call(bf16[384,4096]{1,0:T(8,128)(2,1)} %get-tuple-element.55., ...), custom_call_target="tpu_custom_call" | custom-call | tf_op jit(solution)/shard_map/pallas_call | solution.py:543
  853.7 17.7 %copy.19 = f32[2,1024,3072]{2,1,0:T(8,128)} copy(f32[2,1024,3072]{2,1,0:T(8,128)} %get-tuple-element.69) | data formatting | bytes 50331648
  871.5 8.6 copy.20
  880.1 26.7 %copy.21 = f32[2,1024,4096]{2,1,0:T(8,128)} copy(f32[2,1024,4096]{2,1,0:T(8,128)} %get-tuple-element.71) | data formatting | bytes 67108864
  906.8 1.6 slice-done.6
  909.5 11.7 %copy.22 = f32[2,4096,1024]{2,1,0:T(8,128)} copy(f32[2,4096,1024]{2,1,0:T(8,128)S(1)} %bitcast.133) | data formatting | bytes 67108864
  (158 shorter events, 29.5 us)
Async XLA Ops:
  0.6 156.8 %collective-permute-start.5 = (bf16[384,1024]{1,0:T(8,128)(2,1)}, bf16[384,1024]{1,0:T(8,128)(2,1)}, u32[]{:S(2)}, u32[]{:S(2)}) collective-permute-start(bf16[384,1024]{1,0:T(8,128)(2,1)} %bitcast.134), channel_id=1, source_target_pairs={{0,2},{1,3},{2,0},{3,1},{4,6},{5,7},{6,4},{7,5},{8,10},{9,11},{10,... | collective-permute-start | bytes 2359304 | tf_op jit(solution)/shard_map/ppermute | solution.py:65
  13.4 13.1 %copy-start.13 = (bf16[1,384,1024]{2,1,0:T(8,128)(2,1)S(1)}, bf16[1,384,1024]{2,1,0:T(8,128)(2,1)}, u32[]{:S(2)}) copy-start(bf16[1,384,1024]{2,1,0:T(8,128)(2,1)} %param.8) | copy-start | bytes 2359300
  30.6 131.9 %collective-permute-start.3 = (bf16[384,1024]{1,0:T(8,128)(2,1)}, bf16[384,1024]{1,0:T(8,128)(2,1)}, u32[]{:S(2)}, u32[]{:S(2)}) collective-permute-start(bf16[384,1024]{1,0:T(8,128)(2,1)} %fusion.99.refs_5_), channel_id=1, source_target_pairs={{0,4},{1,5},{2,6},{3,7},{4,0},{5,1},{6,2},{7,3},{8,12},{9,13},{10,... | collective-permute-start | bytes 2359304 | tf_op jit(solution)/shard_map/ppermute | solution.py:65
  45.4 23.2 %copy-start.9 = (bf16[384,1024]{1,0:T(8,128)(2,1)}, bf16[384,1024]{1,0:T(8,128)(2,1)S(1)}, u32[]{:S(2)}) copy-start(bf16[384,1024]{1,0:T(8,128)(2,1)S(1)} %get-tuple-element.48) | copy-start | bytes 2359300
  46.6 117.2 %collective-permute-start.11 = (bf16[384,1024]{1,0:T(8,128)(2,1)}, bf16[384,1024]{1,0:T(8,128)(2,1)}, u32[]{:S(2)}, u32[]{:S(2)}) collective-permute-start(bf16[384,1024]{1,0:T(8,128)(2,1)} %fusion.98.refs_25_), channel_id=1, source_target_pairs={{0,4},{1,5},{2,6},{3,7},{4,0},{5,1},{6,2},{7,3},{8,12},{9,13},{10,... | collective-permute-start | bytes 2359304 | tf_op jit(solution)/shard_map/ppermute | solution.py:65
  68.5 86.2 %collective-permute-start.8 = (bf16[384,512]{1,0:T(8,128)(2,1)}, bf16[384,512]{1,0:T(8,128)(2,1)S(1)}, u32[]{:S(2)}, u32[]{:S(2)}) collective-permute-start(bf16[384,512]{1,0:T(8,128)(2,1)} %constant_dynamic-slice_fusion), channel_id=1, source_target_pairs={{0,2},{1,3},{2,0},{3,1},{4,6},{5,7},{6,4},{7,5},{8,10},{9,11},{10,... | collective-permute-start | bytes 1179656 | tf_op jit(solution)/shard_map/ppermute | solution.py:65
  73.6 90.4 %collective-permute-start.7 = (bf16[384,1024]{1,0:T(8,128)(2,1)}, bf16[384,1024]{1,0:T(8,128)(2,1)}, u32[]{:S(2)}, u32[]{:S(2)}) collective-permute-start(bf16[384,1024]{1,0:T(8,128)(2,1)} %fusion.97.refs_17_), channel_id=1, source_target_pairs={{0,4},{1,5},{2,6},{3,7},{4,0},{5,1},{6,2},{7,3},{8,12},{9,13},{10,... | collective-permute-start | bytes 2359304 | tf_op jit(solution)/shard_map/ppermute | solution.py:65
  104.5 50.3 %copy-start = (bf16[384,1024]{1,0:T(8,128)(2,1)}, bf16[384,1024]{1,0:T(8,128)(2,1)S(1)}, u32[]{:S(2)}) copy-start(bf16[384,1024]{1,0:T(8,128)(2,1)S(1)} %fusion.106.refs_21_) | copy-start | bytes 2359300
  106.5 20.7 %copy-start.10 = (bf16[384,1024]{1,0:T(8,128)(2,1)S(1)}, bf16[384,1024]{1,0:T(8,128)(2,1)}, u32[]{:S(2)}) copy-start(bf16[384,1024]{1,0:T(8,128)(2,1)} %copy-done.9) | copy-start | bytes 2359300
  106.5 20.7 %copy-start.19 = (f32[384]{0:T(512)S(1)}, f32[384]{0:T(512)}, u32[]{:S(2)}) copy-start(f32[384]{0:T(512)} %copy-done.18) | copy-start | bytes 4612
  127.1 20.3 %slice-start.12 = ((s8[16777216]{0:T(1024)(128)(4,1)}), s8[4194304]{0:T(1024)(128)(4,1)S(1)}, s32[]{:S(2)}) async-start(s8[16777216]{0:T(1024)(128)(4,1)} %bitcast.154), calls=%async_computation.12 | async-start | bytes 8388608
  134.3 13.1 %slice-start.13 = ((s8[16777216]{0:T(1024)(128)(4,1)}), s8[4194304]{0:T(1024)(128)(4,1)S(1)}, s32[]{:S(2)}) async-start(s8[16777216]{0:T(1024)(128)(4,1)} %bitcast.154), calls=%async_computation.13 | async-start | bytes 8388608
  136.2 21.2 %copy-start.1 = (bf16[384,1024]{1,0:T(8,128)(2,1)}, bf16[384,1024]{1,0:T(8,128)(2,1)S(1)}, u32[]{:S(2)}) copy-start(bf16[384,1024]{1,0:T(8,128)(2,1)S(1)} %fusion.108.refs_1_) | copy-start | bytes 2359300
  154.8 44.8 %copy-start.2 = (bf16[384,1024]{1,0:T(8,128)(2,1)}, bf16[384,1024]{1,0:T(8,128)(2,1)S(1)}, u32[]{:S(2)}) copy-start(bf16[384,1024]{1,0:T(8,128)(2,1)S(1)} %fusion.110.refs_9_) | copy-start | bytes 2359300
  154.8 17.2 %collective-permute-start.9 = (bf16[384,1024]{1,0:T(8,128)(2,1)S(1)}, bf16[384,1024]{1,0:T(8,128)(2,1)S(1)}, u32[]{:S(2)}, u32[]{:S(2)}) collective-permute-start(bf16[384,1024]{1,0:T(8,128)(2,1)S(1)} %fusion.106.refs_21_), channel_id=1, source_target_pairs={{0,2},{1,3},{2,0},{3,1},{4,6},{5,7},{6,4},{7,5},{8,10},{9,11},{10,... | collective-permute-start | bytes 2359304 | tf_op jit(solution)/shard_map/ppermute | solution.py:65
  157.4 34.8 %collective-permute-start.1 = (bf16[384,1024]{1,0:T(8,128)(2,1)S(1)}, bf16[384,1024]{1,0:T(8,128)(2,1)}, u32[]{:S(2)}, u32[]{:S(2)}) collective-permute-start(bf16[384,1024]{1,0:T(8,128)(2,1)S(1)} %fusion.108.refs_1_), channel_id=1, source_target_pairs={{0,2},{1,3},{2,0},{3,1},{4,6},{5,7},{6,4},{7,5},{8,10},{9,11},{10,... | collective-permute-start | bytes 2359304 | tf_op jit(solution)/shard_map/ppermute | solution.py:65
  162.5 29.9 %copy-start.14 = (bf16[1,384,1024]{2,1,0:T(8,128)(2,1)S(1)}, bf16[1,384,1024]{2,1,0:T(8,128)(2,1)}, u32[]{:S(2)}) copy-start(bf16[1,384,1024]{2,1,0:T(8,128)(2,1)} %param.8) | copy-start | bytes 2359300
  162.5 29.9 %copy-start.25 = (f32[1,1024]{1,0:T(1,128)S(1)}, f32[1,1024]{1,0:T(1,128)}, u32[]{:S(2)}) copy-start(f32[1,1024]{1,0:T(1,128)} %copy-done.24) | copy-start | bytes 12292
  162.5 29.9 %copy-start.27 = (f32[384]{0:T(512)S(1)}, f32[384]{0:T(512)}, u32[]{:S(2)}) copy-start(f32[384]{0:T(512)} %copy-done.26) | copy-start | bytes 4612
  162.5 93.6 %collective-permute-start = (bf16[384,2048]{1,0:T(8,128)(2,1)}, bf16[384,2048]{1,0:T(8,128)(2,1)}, u32[]{:S(2)}, u32[]{:S(2)}) collective-permute-start(bf16[384,2048]{1,0:T(8,128)(2,1)} %constant_dynamic-slice_fusion.2), channel_id=1, source_target_pairs={{0,2},{1,3},{2,0},{3,1},{4,6},{5,7},{6,4},{7,5},{8,10},{9,11},{10,... | collective-permute-start | bytes 4718600 | tf_op jit(solution)/shard_map/ppermute | solution.py:65
  163.8 92.4 %collective-permute-start.2 = (bf16[384,2048]{1,0:T(8,128)(2,1)}, bf16[384,2048]{1,0:T(8,128)(2,1)}, u32[]{:S(2)}, u32[]{:S(2)}) collective-permute-start(bf16[384,2048]{1,0:T(8,128)(2,1)} %constant_dynamic-slice_fusion.3), channel_id=1, source_target_pairs={{0,4},{1,5},{2,6},{3,7},{4,0},{5,1},{6,2},{7,3},{8,12},{9,13},{10,... | collective-permute-start | bytes 4718600 | tf_op jit(solution)/shard_map/ppermute | solution.py:65
  164.0 92.1 %collective-permute-start.6 = (bf16[384,2048]{1,0:T(8,128)(2,1)}, bf16[384,2048]{1,0:T(8,128)(2,1)}, u32[]{:S(2)}, u32[]{:S(2)}) collective-permute-start(bf16[384,2048]{1,0:T(8,128)(2,1)} %constant_dynamic-slice_fusion.5), channel_id=1, source_target_pairs={{0,4},{1,5},{2,6},{3,7},{4,0},{5,1},{6,2},{7,3},{8,12},{9,13},{10,... | collective-permute-start | bytes 4718600 | tf_op jit(solution)/shard_map/ppermute | solution.py:65
  172.9 83.4 %collective-permute-start.4 = (bf16[384,2048]{1,0:T(8,128)(2,1)}, bf16[384,2048]{1,0:T(8,128)(2,1)}, u32[]{:S(2)}, u32[]{:S(2)}) collective-permute-start(bf16[384,2048]{1,0:T(8,128)(2,1)} %constant_dynamic-slice_fusion.1), channel_id=1, source_target_pairs={{0,2},{1,3},{2,0},{3,1},{4,6},{5,7},{6,4},{7,5},{8,10},{9,11},{10,... | collective-permute-start | bytes 4718600 | tf_op jit(solution)/shard_map/ppermute | solution.py:65
  192.2 64.0 %collective-permute-start.10 = (bf16[384,1536]{1,0:T(8,128)(2,1)}, bf16[384,1536]{1,0:T(8,128)(2,1)}, u32[]{:S(2)}, u32[]{:S(2)}) collective-permute-start(bf16[384,1536]{1,0:T(8,128)(2,1)} %constant_dynamic-slice_fusion.4), channel_id=1, source_target_pairs={{0,4},{1,5},{2,6},{3,7},{4,0},{5,1},{6,2},{7,3},{8,12},{9,13},{10,... | collective-permute-start | bytes 3538952 | tf_op jit(solution)/shard_map/ppermute | solution.py:65
  871.5 35.3 %slice-start = ((s8[33554432]{0:T(1024)(128)(4,1)}), s8[4194304]{0:T(1024)(128)(4,1)S(1)}, s32[]{:S(2)}) async-start(s8[33554432]{0:T(1024)(128)(4,1)} %bitcast.132), calls=%async_computation | async-start | bytes 8388608
  871.5 35.3 %slice-start.1 = ((s8[33554432]{0:T(1024)(128)(4,1)}), s8[4194304]{0:T(1024)(128)(4,1)S(1)}, s32[]{:S(2)}) async-start(s8[33554432]{0:T(1024)(128)(4,1)} %bitcast.132), calls=%async_computation.1 | async-start | bytes 8388608
  880.0 26.7 %slice-start.2 = ((s8[33554432]{0:T(1024)(128)(4,1)}), s8[4194304]{0:T(1024)(128)(4,1)S(1)}, s32[]{:S(2)}) async-start(s8[33554432]{0:T(1024)(128)(4,1)} %bitcast.132), calls=%async_computation.2 | async-start | bytes 8388608
  880.0 26.7 %slice-start.3 = ((s8[33554432]{0:T(1024)(128)(4,1)}), s8[4194304]{0:T(1024)(128)(4,1)S(1)}, s32[]{:S(2)}) async-start(s8[33554432]{0:T(1024)(128)(4,1)} %bitcast.132), calls=%async_computation.3 | async-start | bytes 8388608
  880.0 26.7 %slice-start.4 = ((s8[33554432]{0:T(1024)(128)(4,1)}), s8[4194304]{0:T(1024)(128)(4,1)S(1)}, s32[]{:S(2)}) async-start(s8[33554432]{0:T(1024)(128)(4,1)} %bitcast.132), calls=%async_computation.4 | async-start | bytes 8388608
  880.1 26.7 %slice-start.5 = ((s8[33554432]{0:T(1024)(128)(4,1)}), s8[4194304]{0:T(1024)(128)(4,1)S(1)}, s32[]{:S(2)}) async-start(s8[33554432]{0:T(1024)(128)(4,1)} %bitcast.132), calls=%async_computation.5 | async-start | bytes 8388608
  880.1 28.3 %slice-start.6 = ((s8[33554432]{0:T(1024)(128)(4,1)}), s8[4194304]{0:T(1024)(128)(4,1)S(1)}, s32[]{:S(2)}) async-start(s8[33554432]{0:T(1024)(128)(4,1)} %bitcast.132), calls=%async_computation.6 | async-start | bytes 8388608
  880.1 29.5 %slice-start.7 = ((s8[33554432]{0:T(1024)(128)(4,1)}), s8[4194304]{0:T(1024)(128)(4,1)S(1)}, s32[]{:S(2)}) async-start(s8[33554432]{0:T(1024)(128)(4,1)} %bitcast.132), calls=%async_computation.7 | async-start | bytes 8388608
  (36 other events, 229.8 us)
where the time goes:
time: 930 us; the launch traced here: 921 us
  Pallas kernels  658 us (71%)
  matrix products  94.7 us (10%)
  local copies, waits for them, and re-layouts  85.1 us (9%)
  waiting for transfers between devices  61.6 us (7%)
  starting transfers between devices  10.8 us (1%)
  other arithmetic  9.63 us (1%)
    pallas_call x1, Pallas kernels, combine(): pl.pallas_call(functools.partial(combine_kernel, n_dev, n_layers), out_sh...  596 us
    dot_general x15, matrix products, mix_lo(): jnp.einsum(einsum_spec, lhs_arr, rhs_arr, preferred_element_type=jnp.floa...  94.7 us
    unnamed x116, local copies, waits for them, and re-layouts  72 us
    ppermute x12, waiting for transfers between devices, send(): return lax.ppermute(val, AXIS, pairs)  61.6 us
    pallas_call x2, Pallas kernels, attn_backward(): pl.pallas_call(attn_backward_kernel, out_shape=jax.ShapeDtypeStruct(qkv.s...  36.3 us
    pallas_call x2, Pallas kernels, attn_forward(): pl.pallas_call(attn_forward_kernel, out_shape=jax.ShapeDtypeStruct((seq_l...  26 us
  transfers between devices with their start and end apart: 12, of which 3 were waited for; matrix products, arithmetic and copies ran while one was open for 13% of the time, Pallas kernels for 7%

commit v1 on v0

v1 whole, which is shorter than its diff:
```python
import functools

import jax
import jax.numpy as jnp
from jax import lax
from jax.experimental import pallas as pl
from jax.experimental.pallas import tpu as pltpu
from jax.sharding import PartitionSpec as P


NORM_EPS = 1e-6
HEAD_DIM = 64
AXIS = 'data'
CHUNK_UNITS = '003010111100300001102000313110102101'
ORDER = (
    'a9a0c9d9kaa1c0d0e0baa2c1f0b9b0a3c2f1g0d1a4i9c3h0f2b1i0f3c4e1',
    'k9g1j0k0d2f4a5h1a6d3b2i1m9l0m0c5j1b3e2d4n0c6k1o0f5g2f6b4e3l1',
    'q9p0h2g3a7a8m1q0h3i2e4c7c8j2d5k2g4l2n1f7h4f8r0d6i3b6j3o1k3l3',
    'm2b5o2p1k4e5i4p2j4n2o3m3l4q1p3e6g6n3m4h6r1o4d7n4r2d8p4g5b7r3',
    'b8h5i5r4q2j6q3i6e7q4k5e8l6m5j5o6k7l5n5m7p6o5g7g8p5n7h7h8r6i7',
    'q5i8r5k6q7j7j8m6kel7l8n6mem8o7k8o8p7p8q6ner7n8r8qeq8',
)


class Place:
    def __init__(self, n_dev):
        me = lax.axis_index(AXIS)
        self.core = me % 2
        self.x = (me // 2) % 2
        self.y = (me // 4) % 2
        self.z = (me // 8) % 2
        self.swap = {name: [(i, i ^ bit) for i in range(n_dev)] for name, bit in (('core', 1), ('x', 2), ('y', 4), ('z', 8))}

    def at(self, name):
        return {'core': self.core, 'x': self.x, 'y': self.y, 'z': self.z}[name]


def send(val, pairs):
    return lax.ppermute(val, AXIS, pairs)


def part(val, which, count, axis):
    size = val.shape[axis] // count
    return lax.dynamic_slice_in_dim(val, which * size, size, axis)


def neighbour_operands(place, axis, split, lhs, rhs):
    away = part(lhs if split == 0 else rhs, 1 - place.at(axis), 2, 1)
    wide, thin = (lhs, rhs) if split == 0 else (rhs, lhs)
    wide_in = send(away, place.swap[axis])
    thin_in = send(thin, place.swap[axis])
    return wide, thin, wide_in, thin_in


PAIR = 2 * HEAD_DIM
GROUP = 2 * PAIR
Q_BLOCK = 128
FF_BLOCK = 512
GELU_C = 0.7978845608028654
GELU_D = 0.044715


def dot_with(dims):
    return lambda lhs, rhs: lax.dot_general(lhs, rhs, (dims, ((), ())), preferred_element_type=jnp.float32)


dot_nn, dot_nt, dot_tn = (dot_with(((left,), (right,))) for left, right in ((1, 0), (1, 1), (0, 0)))


def rounded(val):
    return val.astype(jnp.bfloat16)


def inverse_rms(rows_f):
    return lax.rsqrt(jnp.mean(rows_f * rows_f, axis=-1, keepdims=True) + NORM_EPS)


def norm_forward(src, gain, dst):
    @pl.loop(0, src.shape[0] // 64)
    def _(step):
        at = pl.ds(pl.multiple_of(step * 64, 64), 64)
        rows_f = src[at, :].astype(jnp.float32)
        dst[at, :] = (rows_f * inverse_rms(rows_f) * gain[...]).astype(jnp.bfloat16)


def norm_backward(src, gain, grad_norm, grad_res, dst, gain_dst):
    gain_dst[...] = jnp.zeros_like(gain_dst)

    @pl.loop(0, src.shape[0] // 64)
    def _(step):
        at = pl.ds(pl.multiple_of(step * 64, 64), 64)
        rows_f = src[at, :].astype(jnp.float32)
        scale = inverse_rms(rows_f)
        unit = rows_f * scale
        grad = grad_norm[at, :].astype(jnp.bfloat16).astype(jnp.float32)
        gain_dst[...] += jnp.sum(grad * unit, axis=0, keepdims=True)
        grad = grad * gain[...]
        grad = scale * (grad - unit * jnp.mean(grad * unit, axis=-1, keepdims=True))
        dst[at, :] = (grad_res[at, :].astype(jnp.float32) + grad).astype(jnp.bfloat16)


def two_heads(rows):
    first = lax.broadcasted_iota(jnp.int32, rows.shape, 1) < HEAD_DIM
    zero = jnp.zeros_like(rows)
    return jnp.concatenate([jnp.where(first, rows, zero), jnp.where(first, zero, rows)], axis=0)


def one_pair(rows):
    half = rows.shape[0] // 2
    first = lax.broadcasted_iota(jnp.int32, (half, PAIR), 1) < HEAD_DIM
    return jnp.where(first, rows[:half], rows[half:])


def softmax_block(q_two, k_rows, block):
    n_keys = k_rows.shape[0]
    scores = dot_nt(q_two, k_rows) * HEAD_DIM ** -0.5
    last = scores[:, n_keys - Q_BLOCK:]
    row = lax.rem(lax.broadcasted_iota(jnp.int32, last.shape, 0), Q_BLOCK)
    last = jnp.where(row >= lax.broadcasted_iota(jnp.int32, last.shape, 1), last, -1e30)
    scores = last if block == 0 else jnp.concatenate([scores[:, :n_keys - Q_BLOCK], last], axis=1)
    weights = jnp.exp(scores - jnp.max(scores, axis=-1, keepdims=True))
    return weights * (1.0 / jnp.sum(weights, axis=-1, keepdims=True))


def attn_forward_kernel(x_ref, gain_ref, wq_ref, wk_ref, wv_ref, wo_ref, u_ref, q_ref, k_ref, v_ref, o_ref, h_ref, acc):
    step = pl.program_id(0)

    @pl.when(step == 0)
    def _():
        norm_forward(x_ref, gain_ref, u_ref)
        acc[...] = jnp.zeros_like(acc)

    for dst, weight in ((q_ref, wq_ref), (k_ref, wk_ref), (v_ref, wv_ref)):
        dst[...] = rounded(dot_nn(u_ref[...], weight[...]))
    for block in range(x_ref.shape[0] // Q_BLOCK):
        rows, keys = pl.ds(block * Q_BLOCK, Q_BLOCK), pl.ds(0, (block + 1) * Q_BLOCK)
        for pair in range(GROUP // PAIR):
            lanes = pl.ds(pair * PAIR, PAIR)
            prob = softmax_block(two_heads(q_ref[rows, lanes]), k_ref[keys, lanes], block)
            o_ref[rows, lanes] = one_pair(dot_nn(prob.astype(jnp.bfloat16), v_ref[keys, lanes])).astype(jnp.bfloat16)
    acc[...] += dot_nn(o_ref[...], wo_ref[...])

    @pl.when(step == pl.num_programs(0) - 1)
    def _():
        h_ref[...] = x_ref[...] + acc[...].astype(jnp.bfloat16)


def attn_backward_kernel(grad_ref, x_ref, gain_ref, q_ref, k_ref, v_ref, wo_ref, wq_ref, wk_ref, wv_ref, out_ref, dx_ref, dgain_ref, do_ref, k_acc, v_acc, acc):
    step = pl.program_id(0)
    seq_len, width = grad_ref.shape

    @pl.when(step == 0)
    def _():
        acc[...] = jnp.zeros_like(acc)

    do_ref[...] = rounded(dot_nt(grad_ref[...], wo_ref[...]))
    n_block = seq_len // Q_BLOCK

    def dest(which, lane, count):
        return pl.ds(pl.multiple_of(which * width + step * GROUP + lane, PAIR), count)

    for pair in range(GROUP // PAIR):
        lanes = pl.ds(pair * PAIR, PAIR)
        for block in reversed(range(n_block)):
            rows, keys = pl.ds(block * Q_BLOCK, Q_BLOCK), pl.ds(0, (block + 1) * Q_BLOCK)
            q_two, g_two = two_heads(q_ref[rows, lanes]), two_heads(do_ref[rows, lanes])
            k_rows = k_ref[keys, lanes]
            prob = softmax_block(q_two, k_rows, block)
            grad_prob = dot_nt(g_two, v_ref[keys, lanes])
            mean = jnp.sum(prob * grad_prob, axis=-1, keepdims=True)
            grad_s = (prob * (grad_prob - mean) * HEAD_DIM ** -0.5).astype(jnp.bfloat16)
            out_ref[rows, dest(0, pair * PAIR, PAIR)] = one_pair(dot_nn(grad_s, k_rows)).astype(jnp.bfloat16)
            k_part, v_part = dot_tn(grad_s, q_two), dot_tn(prob.astype(jnp.bfloat16), g_two)
            if block == n_block - 1:
                k_acc[:, lanes] = k_part
                v_acc[:, lanes] = v_part
            else:
                k_acc[keys, lanes] += k_part
                v_acc[keys, lanes] += v_part
    out_ref[:, dest(1, 0, GROUP)] = k_acc[...].astype(jnp.bfloat16)
    out_ref[:, dest(2, 0, GROUP)] = v_acc[...].astype(jnp.bfloat16)
    for which, weight in enumerate((wq_ref, wk_ref, wv_ref)):
        acc[...] += dot_nt(out_ref[:, dest(which, 0, GROUP)], weight[...])

    @pl.when(step == pl.num_programs(0) - 1)
    def _():
        norm_backward(x_ref, gain_ref, acc, grad_ref, dx_ref, dgain_ref)


def mlp_forward_kernel(has_down, h_ref, gain_ref, w1_ref, *refs):
    w2_ref, refs = (refs[0], refs[1:]) if has_down else (None, refs)
    u_ref, z_ref, a_ref = refs[:3]

    @pl.when(pl.program_id(0) == 0)
    def _():
        norm_forward(h_ref, gain_ref, u_ref)

    z_ref[...] = rounded(dot_nn(u_ref[...], w1_ref[...]))
    rows_f = z_ref[...].astype(jnp.float32)
    bend = jnp.tanh(GELU_C * (rows_f + GELU_D * (rows_f * rows_f * rows_f)))
    a_ref[...] = (rows_f * (0.5 * (1.0 + bend))).astype(jnp.bfloat16)
    if has_down:
        y_ref, acc = refs[3:]

        @pl.when(pl.program_id(0) == 0)
        def _():
            acc[...] = jnp.zeros_like(acc)

        acc[...] += dot_nn(a_ref[...], w2_ref[...])

        @pl.when(pl.program_id(0) == pl.num_programs(0) - 1)
        def _():
            y_ref[...] = h_ref[...] + acc[...].astype(jnp.bfloat16)


def mlp_backward_kernel(grad_ref, h_ref, gain_ref, z_ref, w2_ref, w1_ref, dz_ref, dh_ref, dgain_ref, acc):
    @pl.when(pl.program_id(0) == 0)
    def _():
        acc[...] = jnp.zeros_like(acc)

    grad_a = rounded(dot_nt(grad_ref[...], w2_ref[...])).astype(jnp.float32)
    rows_f = z_ref[...].astype(jnp.float32)
    square = rows_f * rows_f
    bend = jnp.tanh(GELU_C * (rows_f + GELU_D * (square * rows_f)))
    slope = 0.5 * (1.0 + bend) + (0.5 * GELU_C) * rows_f * (1.0 - bend * bend) * (1.0 + (3.0 * GELU_D) * square)
    dz_ref[...] = (slope * grad_a).astype(jnp.bfloat16)
    acc[...] += dot_nt(dz_ref[...], w1_ref[...])

    @pl.when(pl.program_id(0) == pl.num_programs(0) - 1)
    def _():
        norm_backward(h_ref, gain_ref, acc, grad_ref, dh_ref, dgain_ref)


def whole_spec(shape):
    return pl.BlockSpec(shape, lambda step: (0,) * len(shape))


def cols_spec(rows, cols):
    return pl.BlockSpec((rows, cols), lambda step: (0, step))


def weight_cols(layer, rows, cols, shift=0):
    return pl.BlockSpec((None, rows, cols), lambda step: (layer, 0, shift + step))


def weight_rows(layer, rows, cols):
    return pl.BlockSpec((None, rows, cols), lambda step: (layer, step, 0))


def lo(*shape):
    return jax.ShapeDtypeStruct(shape, jnp.bfloat16)


def block_call(kernel, grid, in_specs, out_specs, out_shape, scratch, flops, *args):
    return pl.pallas_call(kernel, grid=(grid,), in_specs=in_specs, out_specs=out_specs, out_shape=out_shape,
                          scratch_shapes=[pltpu.VMEM(shape, jnp.float32) if isinstance(shape, tuple) else shape for shape in scratch],
                          cost_estimate=pl.CostEstimate(flops=flops, bytes_accessed=flops // 500, transcendentals=0),
                          compiler_params=pltpu.CompilerParams(dimension_semantics=('arbitrary',), vmem_limit_bytes=48 * 1024 * 1024))(*args)


def attn_forward(layer, x_rows, gain, w_qkv, w_out):
    seq_len, width = x_rows.shape
    full, cols, steps = whole_spec((seq_len, width)), cols_spec(seq_len, GROUP), width // GROUP
    weights = [weight_cols(layer, width, GROUP, which * steps) for which in range(3)]
    return block_call(attn_forward_kernel, steps, [full, whole_spec((1, width))] + weights + [weight_rows(layer, GROUP, width)],
                      [full, cols, cols, cols, cols, full], [lo(seq_len, width)] * 6, [(seq_len, width)], 8 * seq_len * width * width,
                      x_rows, gain[None], w_qkv, w_qkv, w_qkv, w_out)


def attn_backward(layer, grad, x_rows, gain, q_rows, k_rows, v_rows, w_qkv, w_out):
    seq_len, width = grad.shape
    full, cols, steps = whole_spec((seq_len, width)), cols_spec(seq_len, GROUP), width // GROUP
    weights = [weight_cols(layer, width, GROUP, which * steps) for which in range(3)]
    return block_call(attn_backward_kernel, steps,
                      [full, full, whole_spec((1, width)), cols, cols, cols, weight_rows(layer, GROUP, width)] + weights,
                      [whole_spec((seq_len, 3 * width)), full, whole_spec((1, width))],
                      [lo(seq_len, 3 * width), lo(seq_len, width), jax.ShapeDtypeStruct((1, width), jnp.float32)],
                      [pltpu.VMEM((seq_len, GROUP), jnp.bfloat16), (seq_len, GROUP), (seq_len, GROUP), (seq_len, width)], 11 * seq_len * width * width,
                      grad, x_rows, gain[None], q_rows, k_rows, v_rows, w_out, w_qkv, w_qkv, w_qkv)


def mlp_forward(layer, h_rows, gain, w_up, w_down, has_down):
    seq_len, width = h_rows.shape
    inner = w_up.shape[2]
    full, cols = whole_spec((seq_len, width)), cols_spec(seq_len, FF_BLOCK)
    more = [weight_rows(layer, FF_BLOCK, width)] if has_down else []
    return block_call(functools.partial(mlp_forward_kernel, has_down), inner // FF_BLOCK, [full, whole_spec((1, width)), weight_cols(layer, width, FF_BLOCK)] + more,
                      [full, cols, cols] + [full] * has_down, [lo(seq_len, width), lo(seq_len, inner), lo(seq_len, inner)] + [lo(seq_len, width)] * has_down,
                      [(seq_len, width)] * has_down, (4 if has_down else 2) * seq_len * width * inner,
                      h_rows, gain[None], w_up, *([w_down] * has_down))


def mlp_backward(layer, grad, h_rows, gain, z_rows, w_up, w_down):
    seq_len, width = grad.shape
    inner = w_up.shape[2]
    full, cols = whole_spec((seq_len, width)), cols_spec(seq_len, FF_BLOCK)
    return block_call(mlp_backward_kernel, inner // FF_BLOCK,
                      [full, full, whole_spec((1, width)), cols, weight_rows(layer, FF_BLOCK, width), weight_cols(layer, width, FF_BLOCK)],
                      [cols, full, whole_spec((1, width))],
                      [lo(seq_len, inner), lo(seq_len, width), jax.ShapeDtypeStruct((1, width), jnp.float32)], [(seq_len, width)], 4 * seq_len * width * inner,
                      grad, h_rows, gain[None], z_rows, w_down, w_up)


MATRICES = ((1024, 1024, 0), (1024, 1024, 1), (256, 1024, 0), (1024, 768, 1))
KIND = ('yyYy', 'xxXX')
LATE = ((2, 0), (3, 0))
SEQ_LEN = 384
TOKENS = 4 * SEQ_LEN
TILE_ROWS = 256
STREAM_ROWS = 64
N_SEMS = 12
ADD_ROWS = 32


def read_chunks(text):
    found = []
    for mat, layer in zip(*[map(int, text)] * 2):
        found.append((mat, layer, sum(chunk[:2] == (mat, layer) for chunk in found)))
    return tuple(found)


CHUNKS = read_chunks(CHUNK_UNITS)


def first_axis(mat, layer):
    kind = KIND[layer][mat]
    return kind if kind in 'xy' else 'z'


def chunk_count(mat, layer):
    return sum(chunk[:2] == (mat, layer) for chunk in CHUNKS)


def add_rows(dst, src, cols, scale=None):
    rows = dst.shape[0]

    @pl.loop(0, rows // ADD_ROWS)
    def _(step):
        at = pl.ds(pl.multiple_of(step * ADD_ROWS, ADD_ROWS), ADD_ROWS)
        val = dst[at, cols] + src[at, :]
        dst[at, cols] = val if scale is None else val * scale


def flip(bit, by):
    return 1 - bit if by else bit


def combine_kernel(n_dev, n_layers, *refs):
    units = [(mat, layer) for layer in range(n_layers) for mat in range(len(MATRICES))]
    n_chunk = len(CHUNKS)
    refs = list(refs)

    def take(count):
        head, refs[:] = refs[:count], refs[count:]
        return head

    given = [take(2 if unit in LATE else 4) for unit in units]
    gain_in, = take(1)
    outs, (gain_out,) = take(len(MATRICES)), take(1)
    from_core, part_refs, from_chip = take(2 * len(units)), take(len(units)), take(2 * len(LATE))
    land_q, land_z, land_h = (take(n_chunk) for _ in range(3))
    row_op, col_op, product, stream, gain_buf, gain_land, send_sems, recv_sems, local_sems, stream_sems, gain_send, gain_recv, op_send, op_recv, op_local = refs

    me = lax.axis_index(AXIS)
    core, x_at, y_at, z_at = lax.rem(me, 2), lax.rem(lax.div(me, 2), 2), lax.rem(lax.div(me, 4), 2), lax.div(me, 8)
    half = lax.div(z_at, 2)
    middle = lax.div(z_at + 1, 2) == 1
    edge = lax.div(z_at + 1, 2) != 1
    place = {'x': x_at, 'y': y_at, 'z': lax.rem(z_at, 2)}
    to = {'core': me + 1 - 2 * core, 'x': me + 2 * (1 - 2 * x_at), 'y': me + 4 * (1 - 2 * y_at),
          'mid': me + 8 * (1 - 2 * half), 'end': me - 8 * (1 - 2 * half),
          'z': me + 8 * (1 - 2 * place['z']), 'far': me + 16 * (1 - 2 * half)}

    def remote(src, dst, i, sem, dev):
        return pltpu.make_async_remote_copy(src_ref=src, dst_ref=dst, send_sem=send_sems.at[i, sem], recv_sem=recv_sems.at[i, sem],
                                            device_id=(dev,), device_id_type=pl.DeviceIdType.MESH)

    def out_block(i, p_at, c_at, row, n_rows, h_at):
        mat, layer, k = CHUNKS[i]
        rows_all, cols, split = MATRICES[mat]
        quarter = p_at * 2 + c_at
        row = row + k * (rows_all // chunk_count(mat, layer)) + (quarter * rows_all if split == 0 else 0)
        col, n_cols = (0, cols) if h_at is None else (h_at * (cols // 2), cols // 2)
        if split == 1:
            col = col + quarter * cols
        return outs[mat].at[layer, pl.ds(pl.multiple_of(row, 8), n_rows), pl.ds(col if isinstance(col, int) else pl.multiple_of(col, 128), n_cols)]

    def stream_add(dst, src):
        rows, cols = dst.shape
        size = min(STREAM_ROWS, rows)
        steps = rows // size

        def fetch(step, slot):
            return pltpu.make_async_copy(src.at[pl.ds(pl.multiple_of(step * size, size), size), :], stream.at[slot, pl.ds(0, size), pl.ds(0, cols)], stream_sems.at[slot])

        fetch(0, 0).start()

        @pl.loop(0, steps)
        def _(step):
            slot = lax.rem(step, 2)

            @pl.when(step + 1 < steps)
            def _():
                fetch(step + 1, 1 - slot).start()

            fetch(step, slot).wait()
            at = pl.ds(pl.multiple_of(step * size, size), size)
            dst[at, :] = dst[at, :] + stream[slot, pl.ds(0, size), pl.ds(0, cols)]

    def run(i, stage, pending):
        mat, layer, k = CHUNKS[i]
        rows_all, cols, _ = MATRICES[mat]
        kind, p_name = KIND[layer][mat], first_axis(mat, layer)
        by_pairs = p_name == 'z'
        q_name = kind.lower() if by_pairs else 'xy'.replace(kind, '')
        r_name = 'xy'.replace(q_name, '')
        rows = rows_all // chunk_count(mat, layer)
        part = part_refs[layer * len(MATRICES) + mat]
        p_at, q_at, r_at = place[p_name], place[q_name], place[r_name]

        def go(src, dst, sem, dest, cond=None):
            remote(src(), dst(), i, sem, to[dest]).start()
            pending.append((cond, src, i, sem))

        def block(dp=0, dq=0, dc=0, dr=None, dh=None):
            def ref():
                row, count = flip(q_at, dq) * (rows // 2), rows // 2
                if dr is not None:
                    row, count = row + flip(r_at, dr) * (rows // 4), rows // 4
                return out_block(i, flip(p_at, dp), flip(core, dc), row, count, None if dh is None else flip(half, dh))

            return ref

        def pass_on(blk, sems, cond=None):
            for dest, sem in sems:
                go(blk, blk, sem, dest, cond)

        def arrived(blk, sem):
            remote(blk(), blk(), i, sem, me).wait_recv()

        def half_cols(by):
            return pl.ds(pl.multiple_of(flip(half, by) * (cols // 2), 128), cols // 2)

        def own_rows(by):
            return land_q[i].at[pl.ds(pl.multiple_of(flip(r_at, by) * (rows // 4), 8), rows // 4), :] if by_pairs else land_q[i]

        def own_half(by):
            return lambda: (land_q[i].at[pl.ds(pl.multiple_of(r_at * (rows // 4), 8), rows // 4), half_cols(by)] if by_pairs
                            else land_q[i].at[:, half_cols(by)])

        def rows_of(by):
            return lambda: part.at[pl.ds(pl.multiple_of(k * rows + flip(q_at, by) * (rows // 2), 8), rows // 2), :]

        last = dict(dr=0) if by_pairs else {}

        def keep():
            return pltpu.make_async_copy(own_half(0)(), block(dh=0, **last)(), local_sems.at[i])

        def whole(buf):
            return lambda: buf[i]

        def scale_and_send(dest):
            add_rows(own_rows(0), land_h[i], half_cols(0), 1.0 / n_dev)
            keep().start()
            go(own_half(0), block(dh=0, **last), 3, dest, None if by_pairs else middle)

        def spread(turn):
            if turn == 0:
                pass_on(block(), ((q_name, 5), (p_name, 6), ('core', 8)))
            elif turn == 1:
                arrived(block(dq=1), 5)
                pass_on(block(dq=1), ((p_name, 7), ('core', 9)))
            else:
                dq = turn - 2
                arrived(block(dp=1, dq=dq), turn + 4)
                pass_on(block(dp=1, dq=dq), (('core', turn + 8),))

        if stage == 0:
            go(rows_of(1), whole(land_q), 0, q_name)
        elif stage == 8:
            for turn in range(4):
                arrived(block(dp=turn // 2, dq=turn % 2, dc=1), 8 + turn)
        elif by_pairs:
            if stage == 1:
                arrived(whole(land_q), 0)
                stream_add(land_q[i], rows_of(0)())
                go(lambda: own_rows(1), whole(land_z), 1, r_name)
            elif stage == 2:
                arrived(whole(land_z), 1)
                add_rows(own_rows(0), land_z[i], slice(None))
                go(own_half(1), whole(land_h), 2, 'far')
            elif stage == 3:
                arrived(whole(land_h), 2)
                scale_and_send('far')
            elif stage == 4:
                keep().wait()
                arrived(block(dr=0, dh=1), 3)
                go(block(dr=0), block(dr=0), 4, r_name)
            else:
                if stage == 5:
                    arrived(block(dr=1), 4)
                spread(min(stage - 5, 3))
        elif stage == 1:
            arrived(whole(land_q), 0)
            stream_add(land_q[i], rows_of(0)())

            @pl.when(edge)
            def _():
                go(whole(land_q), whole(land_z), 1, 'mid', edge)
        elif stage in (2, 3):
            @pl.when(middle)
            def _():
                arrived(whole((land_z, land_h)[stage - 2]), stage - 1)
                if stage == 2:
                    add_rows(land_q[i], land_z[i], slice(None))
                    go(own_half(1), whole(land_h), 2, 'mid', middle)
                else:
                    scale_and_send('mid')
        else:
            if stage == 4:
                @pl.when(middle)
                def _():
                    keep().wait()
                    arrived(block(dh=1), 3)
                    pass_on(block(), (('end', 4),), middle)

                @pl.when(edge)
                def _():
                    arrived(block(), 4)
            spread(stage - 4)

    def unit_sizes(unit):
        rows, cols, split = MATRICES[unit[0]]
        p_name = first_axis(*unit)
        return (rows, cols, p_name, split) + ((rows, cols) if split == 0 else (cols, rows))

    def operand_copy(u, which, src, dst, dest):
        return pltpu.make_async_remote_copy(src_ref=src, dst_ref=dst, send_sem=op_send.at[u, which], recv_sem=op_recv.at[u, which],
                                            device_id=(to[dest],), device_id_type=pl.DeviceIdType.MESH)

    def operand_copies(u):
        unit = units[u]
        _, _, p_name, split, wide_w, _ = unit_sizes(unit)
        p_at = place[p_name]
        wide, thin = given[u][:2]
        core_wide, core_thin = from_core[2 * u:2 * u + 2]
        if unit in LATE:
            late = LATE.index(unit)
            chip_wide, chip_thin = from_chip[2 * late:2 * late + 2]
        else:
            chip_wide, chip_thin = given[u][2:]
        first, second = pl.ds(0, SEQ_LEN), pl.ds(SEQ_LEN, SEQ_LEN)

        def lanes(at, count):
            return pl.ds(pl.multiple_of(at, 128), count)

        other = 1 - core
        copies = {
            'own': (operand_copy(u, 0, wide.at[:, lanes((p_at * 2 + other) * wide_w, wide_w)], core_wide.at[first, :], 'core'),
                    operand_copy(u, 1, thin, core_thin.at[first, :], 'core')),
            'next': (operand_copy(u, 2, chip_wide.at[:, lanes(other * wide_w, wide_w)], core_wide.at[second, :], 'core'),
                     operand_copy(u, 3, chip_thin, core_thin.at[second, :], 'core')),
        }
        if unit in LATE:
            copies['chip'] = (operand_copy(u, 4, wide.at[:, lanes((1 - p_at) * 2 * wide_w, 2 * wide_w)], chip_wide, p_name),
                              operand_copy(u, 5, thin, chip_thin, p_name))
        wide_op, thin_op = (row_op, col_op) if split == 0 else (col_op, row_op)
        thin_w = thin.shape[1]
        loads = []
        for start, src in ((0, wide.at[:, lanes((p_at * 2 + core) * wide_w, wide_w)]), (SEQ_LEN, chip_wide.at[:, lanes(core * wide_w, wide_w)]),
                           (2 * SEQ_LEN, core_wide)):
            loads.append((src, wide_op.at[pl.ds(start, src.shape[0]), pl.ds(0, wide_w)]))
        for start, src in ((0, thin), (SEQ_LEN, chip_thin), (2 * SEQ_LEN, core_thin)):
            loads.append((src, thin_op.at[pl.ds(start, src.shape[0]), pl.ds(0, thin_w)]))
        copies['load'] = tuple(pltpu.make_async_copy(src, dst, op_local.at[u, n]) for n, (src, dst) in enumerate(loads))
        return copies

    def start_operands(u):
        copies = operand_copies(u)
        if units[u] in LATE:
            for copy in copies['chip']:
                copy.start()
        for copy in copies['own']:
            copy.start()
        if units[u] not in LATE:
            for copy in copies['next']:
                copy.start()

    def forward_operands(u):
        copies = operand_copies(u)
        for copy in copies['chip']:
            copy.wait_recv()
        for copy in copies['next']:
            copy.start()

    def multiply(u):
        rows, cols, _, _, _, _ = unit_sizes(units[u])
        copies = operand_copies(u)
        for copy in copies['own'] + copies['next']:
            copy.wait_recv()
        for copy in copies['load']:
            copy.start()
        for copy in copies['load']:
            copy.wait()
        tile = min(TILE_ROWS, rows)
        half_w = cols // 2

        @pl.loop(0, rows // tile)
        def _(step):
            at = pl.ds(pl.multiple_of(step * tile, tile), tile)
            for side in range(2):
                lanes = pl.ds(side * half_w, half_w)
                product[at, lanes] = dot_tn(row_op[:, at], col_op[:, lanes])

        store = pltpu.make_async_copy(product.at[pl.ds(0, rows), pl.ds(0, cols)], part_refs[u], op_local.at[u, 6])
        store.start()
        store.wait()

    def finish_operands(u):
        copies = operand_copies(u)
        for copy in copies['own'] + copies['next'] + copies.get('chip', ()):
            copy.wait_send()

    gain_steps = ('core', 'x', 'y', 'z', 'far')

    def gain_copy(step):
        return pltpu.make_async_remote_copy(src_ref=gain_buf.at[step], dst_ref=gain_land.at[step], send_sem=gain_send.at[step],
                                            recv_sem=gain_recv.at[step], device_id=(to[gain_steps[step]],), device_id_type=pl.DeviceIdType.MESH)

    def gain_next(step):
        copy = gain_copy(step)
        copy.wait()
        total = gain_buf[step] + gain_land[step]
        if step + 1 < len(gain_steps):
            gain_buf[step + 1] = total
            gain_copy(step + 1).start()
        else:
            gain_out[...] = total * (1.0 / n_dev)

    pending = []
    gain_buf[0] = gain_in[...]
    step = 0
    first_use = []
    for mat, layer, _ in CHUNKS:
        if units.index((mat, layer)) not in first_use:
            first_use.append(units.index((mat, layer)))
    for u in first_use:
        start_operands(u)
    for count, (letter, digit) in enumerate(zip(*[iter(''.join(ORDER))] * 2)):
        i, stage = ord(letter) - ord('a'), int(digit, 16)
        u = units.index(CHUNKS[i][:2])
        if stage == 9:
            multiply(u)
        elif stage == 10:
            forward_operands(u)
        else:
            run(i, stage, pending)
        if count == 1:
            gain_copy(0).start()
        if count >= 8 and count % 6 == 0 and step < len(gain_steps):
            gain_next(step)
            step += 1
    for u in range(len(units)):
        finish_operands(u)
    for cond, src, i, sem in pending:
        def finish(src=src, i=i, sem=sem):
            remote(src(), src(), i, sem, me).wait_send()

        if cond is None:
            finish()
        else:
            pl.when(cond)(finish)


def combine(operands, gains, n_dev, n_layers):
    f32, bf16 = jnp.float32, jnp.bfloat16
    units = [(mat, layer) for layer in range(n_layers) for mat in range(len(MATRICES))]
    outs = []
    for rows, cols, split in MATRICES:
        outs.append(jax.ShapeDtypeStruct((n_layers, rows * (4 if split == 0 else 1), cols * (4 if split == 1 else 1)), f32))
    outs.append(jax.ShapeDtypeStruct(gains.shape, f32))
    widths = [MATRICES[mat][:2] if MATRICES[mat][2] == 0 else MATRICES[mat][1::-1] for mat, _ in units]
    for wide_w, thin_w in widths:
        outs += [jax.ShapeDtypeStruct((2 * SEQ_LEN, wide_w), bf16), jax.ShapeDtypeStruct((2 * SEQ_LEN, thin_w), bf16)]
    outs += [jax.ShapeDtypeStruct(MATRICES[mat][:2], f32) for mat, _ in units]
    for unit in LATE:
        wide_w, thin_w = widths[units.index(unit)]
        outs += [jax.ShapeDtypeStruct((SEQ_LEN, 2 * wide_w), bf16), jax.ShapeDtypeStruct((SEQ_LEN, thin_w), bf16)]
    sizes = [(MATRICES[mat][0] // chunk_count(mat, layer) // 2, MATRICES[mat][1], first_axis(mat, layer) == 'z') for mat, layer, _ in CHUNKS]
    scratch = [pltpu.VMEM((r, c), f32) for r, c, _ in sizes]
    scratch += [pltpu.VMEM((r // 2 if pairs else r, c), f32) for r, c, pairs in sizes]
    scratch += [pltpu.VMEM((r // 2 if pairs else r, c // 2), f32) for r, c, pairs in sizes]
    n_chunk, n_unit = len(CHUNKS), len(units)
    most_rows, most_cols = max(m[0] for m in MATRICES), max(m[1] for m in MATRICES)
    scratch += [pltpu.VMEM((TOKENS, most_rows), bf16), pltpu.VMEM((TOKENS, most_cols), bf16), pltpu.VMEM((most_rows, most_cols), f32),
                pltpu.VMEM((2, STREAM_ROWS, most_cols), f32),
                pltpu.VMEM((5,) + gains.shape, f32), pltpu.VMEM((5,) + gains.shape, f32),
                pltpu.SemaphoreType.DMA((n_chunk, N_SEMS)), pltpu.SemaphoreType.DMA((n_chunk, N_SEMS)), pltpu.SemaphoreType.DMA((n_chunk,)), pltpu.SemaphoreType.DMA((2,)),
                pltpu.SemaphoreType.DMA((5,)), pltpu.SemaphoreType.DMA((5,)),
                pltpu.SemaphoreType.DMA((n_unit, 6)), pltpu.SemaphoreType.DMA((n_unit, 6)), pltpu.SemaphoreType.DMA((n_unit, 7))]
    hbm, vmem = pl.BlockSpec(memory_space=pl.ANY), pl.BlockSpec(memory_space=pltpu.VMEM)
    flat = [val for group in operands for val in group]
    results = pl.pallas_call(
        functools.partial(combine_kernel, n_dev, n_layers),
        out_shape=tuple(outs),
        in_specs=[hbm] * len(flat) + [vmem],
        out_specs=tuple([hbm] * 4 + [vmem] + [hbm] * (len(outs) - 5)),
        scratch_shapes=scratch,
        compiler_params=pltpu.CompilerParams(has_side_effects=True, vmem_limit_bytes=63 * 1024 * 1024),
    )(*flat, gains)
    return results[:5]


def solution(mesh):
    n_dev = mesh.shape[AXIS]

    def whole_step(x_loc, grad_y_loc, gain_one, gain_two, w_qkv, w_out, w_up, w_down):
        place = Place(n_dev)
        n_layers = w_qkv.shape[0]
        rows, saved = x_loc[0], []
        for layer in range(n_layers):
            u_one, q_all, k_all, v_all, mixed, hidden = attn_forward(layer, rows, gain_one[layer], w_qkv, w_out)
            u_two, pre, act, *after = mlp_forward(layer, hidden, gain_two[layer], w_up, w_down, layer + 1 < n_layers)
            saved.append((rows, u_one, q_all, k_all, v_all, mixed, hidden, u_two, pre, act))
            rows = after[0] if after else None
        operands = [None] * (n_layers * len(MATRICES))

        def reduce_grad(mat, layer_idx, lhs, rhs):
            color, split = first_axis(mat, layer_idx), MATRICES[mat][2]
            if (mat, layer_idx) in LATE:
                operands[layer_idx * len(MATRICES) + mat] = (lhs, rhs) if split == 0 else (rhs, lhs)
            else:
                operands[layer_idx * len(MATRICES) + mat] = neighbour_operands(place, color, split, lhs, rhs)

        gain_grads = [None] * (2 * n_layers)
        grad = grad_y_loc[0]
        for layer in reversed(range(n_layers)):
            rows, u_one, q_all, k_all, v_all, mixed, hidden, u_two, pre, act = saved[layer]
            reduce_grad(0, layer, act, grad)
            grad_pre, grad_hidden, gain_grads[n_layers + layer] = mlp_backward(layer, grad, hidden, gain_two[layer], pre, w_up, w_down)
            reduce_grad(1, layer, u_two, grad_pre)
            reduce_grad(2, layer, mixed, grad_hidden)
            grad_qkv, grad, gain_grads[layer] = attn_backward(layer, grad_hidden, rows, gain_one[layer], q_all, k_all, v_all, w_qkv, w_out)
            reduce_grad(3, layer, u_one, grad_qkv)
        gains = jnp.concatenate(gain_grads + [jnp.zeros((8 - 2 * n_layers, gain_grads[0].shape[1]), jnp.float32)])
        down, up, out, qkv, gains = combine(operands, gains, n_dev, n_layers)
        return (grad[None], gains[:n_layers], gains[n_layers:2 * n_layers], qkv, out, up, down)

    batch_spec = P(AXIS)
    full_spec = P()
    return jax.shard_map(whole_step, mesh=mesh, in_specs=(batch_spec, batch_spec) + (full_spec,) * 6, out_specs=(batch_spec,) + (full_spec,) * 6, check_vma=False)
```

time: 930 us -> 878 us (0.944)
  matrix products: 94.7 us -> 0 us
  Pallas kernels: 658 us -> 717 us
  waiting for transfers between devices: 61.6 us -> 50.1 us
  other arithmetic: 9.63 us -> 0.01 us
  local copies, waits for them, and re-layouts: 85.1 us -> 94.5 us
    dot_general x15 -> x0, matrix products: 94.7 us -> none  [mix_lo(): jnp.einsum(einsum_spec, lhs_arr, rhs_arr, preferred_element_type=jnp.floa...]
    pallas_call x4 -> x8, Pallas kernels: 62.3 us -> 141 us  [block_call(): pl.pallas_call(kernel, grid=(grid,), in_specs=in_specs, out_specs=out_spe...]
    pallas_call x1, Pallas kernels: 596 us -> 576 us  [combine(): pl.pallas_call(functools.partial(combine_kernel, n_dev, n_layers), out_sh...]
    ppermute x12, waiting for transfers between devices: 61.6 us -> 50.1 us  [send(): return lax.ppermute(val, AXIS, pairs)]
    unnamed x116 -> x70, local copies, waits for them, and re-layouts: 72 us -> 80.8 us
  transfers between devices with their start and end apart: 12 -> 12, of which waited for: 3 -> 3; matrix products, arithmetic and copies ran while one was open for 13% -> 1% of each run, Pallas kernels for 7% -> 16%
where the time goes in v1:
time: 878 us; the launch traced here: 872 us
  Pallas kernels  717 us (82%)
  local copies, waits for them, and re-layouts  94.5 us (11%)
  waiting for transfers between devices  50.1 us (6%)
  starting transfers between devices  9.68 us (1%)
    pallas_call x1, Pallas kernels, combine(): pl.pallas_call(functools.partial(combine_kernel, n_dev, n_layers), out_sh...  576 us
    pallas_call x8, Pallas kernels, block_call(): pl.pallas_call(kernel, grid=(grid,), in_specs=in_specs, out_specs=out_spe...  141 us
    unnamed x70, local copies, waits for them, and re-layouts  80.8 us
    ppermute x12, waiting for transfers between devices, send(): return lax.ppermute(val, AXIS, pairs)  50.1 us
  transfers between devices with their start and end apart: 12, of which 3 were waited for; matrix products, arithmetic and copies ran while one was open for 1% of the time, Pallas kernels for 16%

profile of v1, /device:TPU:1, one launch (start us, length us, event | category | flops | bytes accessed | tf_op | source)
XLA Modules:
  0.0 872.5 jit_solution(824655730932663867)
XLA Ops:
  0.6 2.1 collective-permute-start.5
  5.4 16.2 %shard_map.135 = (bf16[384,1024]{1,0:T(8,128)(2,1)S(1)}, bf16[384,1024]{1,0:T(8,128)(2,1)S(1)}, bf16[384,1024]{1,0:T(8,128)(2,1)S(1)}, bf16[384,1024]{1,0:T(8,12...) custom-call(bf16[384,1024]{1,0:T(8,128)(2,1)S(1)} %bitcast.3, ...), custom_call_target="tpu_custom_call" | custom-call | flops 3221225472 | bytes 6442450 | tf_op jit(solution)/shard_map/pallas_call | solution.py:255
  26.1 15.9 %shard_map.136 = (bf16[384,1024]{1,0:T(8,128)(2,1)}, bf16[384,4096]{1,0:T(8,128)(2,1)S(1)}, bf16[384,4096]{1,0:T(8,128)(2,1)}, bf16[384,1024]{1,0:T(8,128)(2,1)S(1)}) custom-call(bf16[384,1024]{1,0:T(8,128)(2,1)S(1)} %get-tuple-element.43.h_ref, f32[1,1024]{1,0:T(1,128)S(1)} %get-tuple-element.82.gain_ref, bf16[2,1024,4096]{2,1,0:T(8,128)(2,1)} %w1_ref.7, ...), custom_call_target="tpu_custom_call" | custom-call | flops 6442450944 | bytes 12884901 | tf_op jit(solution)/shard_map/pallas_call | solution.py:255
  42.0 1.7 copy-done.3
  43.7 1.2 collective-permute-start.3
  44.9 16.2 %shard_map.137 = (bf16[384,1024]{1,0:T(8,128)(2,1)S(1)}, bf16[384,1024]{1,0:T(8,128)(2,1)S(1)}, bf16[384,1024]{1,0:T(8,128)(2,1)S(1)}, bf16[384,1024]{1,0:T(8,12...) custom-call(bf16[384,1024]{1,0:T(8,128)(2,1)S(1)} %get-tuple-element.44.x_ref, ...), custom_call_target="tpu_custom_call" | custom-call | flops 3221225472 | bytes 6442450 | tf_op jit(solution)/shard_map/pallas_call | solution.py:255
  63.0 1.3 collective-permute-start.8
  64.3 11.1 %shard_map.138 = (bf16[384,1024]{1,0:T(8,128)(2,1)}, bf16[384,4096]{1,0:T(8,128)(2,1)S(1)}, bf16[384,4096]{1,0:T(8,128)(2,1)}) custom-call(bf16[384,1024]{1,0:T(8,128)(2,1)S(1)} %get-tuple-element.45.h_ref, f32[1,1024]{1,0:T(1,128)S(1)} %get-tuple-element.81.gain_ref, bf16[2,1024,4096]{2,1,0:T(8,128)(2,1)} %w1_ref.7), custom_call_target="tpu_custom_call" | custom-call | flops 3221225472 | bytes 6442450 | tf_op jit(solution)/shard_map/pallas_call | solution.py:255
  75.3 1.7 copy-done.4
  77.0 16.4 %shard_map.139 = (bf16[384,4096]{1,0:T(8,128)(2,1)S(1)}, bf16[384,1024]{1,0:T(8,128)(2,1)}, f32[1,1024]{1,0:T(1,128)S(1)}) custom-call(bf16[384,1024]{1,0:T(8,128)(2,1)S(1)} %bitcast.7, bf16[384,1024]{1,0:T(8,128)(2,1)S(1)} %get-tuple-element.45.h_ref, f32[1,1024]{1,0:T(1,128)S(1)} %get-tuple-element.81.gain_ref, bf16[384,4096]{1,0:T(8,128)(2,1)} %copy-done.4, ...), custom_call_target="tpu_custom_call" | custom-call | flops 6442450944 | bytes 12884901 | tf_op jit(solution)/shard_map/pallas_call | solution.py:255
  93.6 25.4 %shard_map.140 = (bf16[384,3072]{1,0:T(8,128)(2,1)}, bf16[384,1024]{1,0:T(8,128)(2,1)}, f32[1,1024]{1,0:T(1,128)S(1)}) custom-call(bf16[384,1024]{1,0:T(8,128)(2,1)} %get-tuple-element.47.grad_ref.refs_21_, bf16[384,1024]{1,0:T(8,128)(2,1)S(1)} %copy-done.13, f32[1,1024]{1,0:T(1,128)S(1)} %get-tuple-element.83.gain_ref, ...), custom_call_target="tpu_custom_call" | custom-call | flops 4429185024 | bytes 8858370 | tf_op jit(solution)/shard_map/pallas_call | solution.py:255
  119.4 16.0 %shard_map.141 = (bf16[384,4096]{1,0:T(8,128)(2,1)S(1)}, bf16[384,1024]{1,0:T(8,128)(2,1)S(1)}, f32[1,1024]{1,0:T(1,128)S(1)}) custom-call(bf16[384,1024]{1,0:T(8,128)(2,1)} %get-tuple-element.51.grad_ref.refs_1_, bf16[384,1024]{1,0:T(8,128)(2,1)S(1)} %copy-done.11, f32[1,1024]{1,0:T(1,128)S(1)} %get-tuple-element.82.gain_ref, bf16[384,4096]{1,0:T(8,128)(2,1)} %copy-done.3, ...), custom_call_target="tpu_custom_call" | custom-call | flops 6442450944 | bytes 12884901 | tf_op jit(solution)/shard_map/pallas_call | solution.py:255
  135.4 1.7 copy-done.1
  137.9 2.9 constant_dynamic-slice_fusion.5
  141.2 1.2 constant_dynamic-slice_fusion.4
  142.7 1.3 constant_dynamic-slice_fusion.2
  144.9 1.3 constant_dynamic-slice_fusion.3
  146.2 1.2 collective-permute-start
  147.4 11.1 %collective-permute-done.11.refs_27_ = bf16[384,1024]{1,0:T(8,128)(2,1)} collective-permute-done((bf16[384,1024]{1,0:T(8,128)(2,1)}, bf16[384,1024]{1,0:T(8,128)(2,1)}, u32[]{:S(2)}, u32[]{:S(2)}) %collective-permute-start.11) | collective-permute-done | bytes 786464 | tf_op jit(solution)/shard_map/ppermute | solution.py:39
  158.7 1.3 collective-permute-start.6
  161.1 2.4 constant_dynamic-slice_fusion
  163.7 24.2 %shard_map.142 = (bf16[384,3072]{1,0:T(8,128)(2,1)}, bf16[384,1024]{1,0:T(8,128)(2,1)}, f32[1,1024]{1,0:T(1,128)S(1)}) custom-call(bf16[384,1024]{1,0:T(8,128)(2,1)S(1)} %copy-done.9, bf16[384,1024]{1,0:T(8,128)(2,1)S(1)} %bitcast.4, f32[1,1024]{1,0:T(1,128)S(1)} %get-tuple-element.84.gain_ref, bf16[384,1024]{1,0:T(8,128)(2,1)S(1)} %copy-done.18, ...), custom_call_target="tpu_custom_call" | custom-call | flops 4429185024 | bytes 8858370 | tf_op jit(solution)/shard_map/pallas_call | solution.py:255
  188.5 5.3 collective-permute-done.4.refs_14_
  193.8 33.7 %collective-permute-done.6.refs_18_ = bf16[384,2048]{1,0:T(8,128)(2,1)} collective-permute-done((bf16[384,2048]{1,0:T(8,128)(2,1)}, bf16[384,2048]{1,0:T(8,128)(2,1)}, u32[]{:S(2)}, u32[]{:S(2)}) %collective-permute-start.6) | collective-permute-done | bytes 1572896 | tf_op jit(solution)/shard_map/ppermute | solution.py:39
  227.5 575.9 %shard_map.143 = (f32[2,4096,1024]{2,1,0:T(8,128)}, f32[2,1024,4096]{2,1,0:T(8,128)}, f32[2,1024,1024]{2,1,0:T(8,128)}, f32[2,1024,3072]{2,1,0:T(8,128)}, f32[8,...) custom-call(bf16[384,4096]{1,0:T(8,128)(2,1)} %get-tuple-element.58., ...), custom_call_target="tpu_custom_call" | custom-call | tf_op jit(solution)/shard_map/pallas_call | solution.py:703
  803.4 1.4 fusion
  804.9 17.8 %copy.19 = f32[2,1024,3072]{2,1,0:T(8,128)} copy(f32[2,1024,3072]{2,1,0:T(8,128)} %get-tuple-element.95) | data formatting | bytes 50331648
  822.7 8.6 copy.20
  831.3 26.7 %copy.21 = f32[2,1024,4096]{2,1,0:T(8,128)} copy(f32[2,1024,4096]{2,1,0:T(8,128)} %get-tuple-element.97) | data formatting | bytes 67108864
  858.0 1.6 slice-done.6
  859.6 1.2 slice-done.7
  860.8 11.7 %copy.22 = f32[2,4096,1024]{2,1,0:T(8,128)} copy(f32[2,4096,1024]{2,1,0:T(8,128)S(1)} %bitcast.9) | data formatting | bytes 67108864
  (83 shorter events, 14.0 us)
Async XLA Ops:
  0.6 141.8 %collective-permute-start.5 = (bf16[384,1024]{1,0:T(8,128)(2,1)}, bf16[384,1024]{1,0:T(8,128)(2,1)}, u32[]{:S(2)}, u32[]{:S(2)}) collective-permute-start(bf16[384,1024]{1,0:T(8,128)(2,1)} %bitcast.5), channel_id=1, source_target_pairs={{0,2},{1,3},{2,0},{3,1},{4,6},{5,7},{6,4},{7,5},{8,10},{9,11},{10,... | collective-permute-start | bytes 2359304 | tf_op jit(solution)/shard_map/ppermute | solution.py:39
  26.1 15.9 %copy-start.10 = (bf16[384,1024]{1,0:T(8,128)(2,1)}, bf16[384,1024]{1,0:T(8,128)(2,1)S(1)}, u32[]{:S(2)}) copy-start(bf16[384,1024]{1,0:T(8,128)(2,1)S(1)} %get-tuple-element.43.h_ref) | copy-start | bytes 2359300
  43.7 17.5 %copy-start.12 = (bf16[384,1024]{1,0:T(8,128)(2,1)}, bf16[384,1024]{1,0:T(8,128)(2,1)S(1)}, u32[]{:S(2)}) copy-start(bf16[384,1024]{1,0:T(8,128)(2,1)S(1)} %get-tuple-element.44.x_ref) | copy-start | bytes 2359300
  43.7 102.5 %collective-permute-start.3 = (bf16[384,1024]{1,0:T(8,128)(2,1)}, bf16[384,1024]{1,0:T(8,128)(2,1)}, u32[]{:S(2)}, u32[]{:S(2)}) collective-permute-start(bf16[384,1024]{1,0:T(8,128)(2,1)} %get-tuple-element.60.refs_5_), channel_id=1, source_target_pairs={{0,4},{1,5},{2,6},{3,7},{4,0},{5,1},{6,2},{7,3},{8,12},{9,13},{10,... | collective-permute-start | bytes 2359304 | tf_op jit(solution)/shard_map/ppermute | solution.py:39
  63.0 77.8 %collective-permute-start.8 = (bf16[384,512]{1,0:T(8,128)(2,1)}, bf16[384,512]{1,0:T(8,128)(2,1)}, u32[]{:S(2)}, u32[]{:S(2)}) collective-permute-start(bf16[384,512]{1,0:T(8,128)(2,1)} %constant_dynamic-slice_fusion.1), channel_id=1, source_target_pairs={{0,8},{1,9},{2,10},{3,11},{4,12},{5,13},{6,14},{7,15},{8,0},{9,1},... | collective-permute-start | bytes 1179656 | tf_op jit(solution)/shard_map/ppermute | solution.py:39
  64.3 12.7 %copy-start.7 = (bf16[1,384,1024]{2,1,0:T(8,128)(2,1)S(1)}, bf16[1,384,1024]{2,1,0:T(8,128)(2,1)}, u32[]{:S(2)}) copy-start(bf16[1,384,1024]{2,1,0:T(8,128)(2,1)} %param.9) | copy-start | bytes 2359300
  77.0 16.6 %copy-start.13 = (bf16[384,1024]{1,0:T(8,128)(2,1)S(1)}, bf16[384,1024]{1,0:T(8,128)(2,1)}, u32[]{:S(2)}) copy-start(bf16[384,1024]{1,0:T(8,128)(2,1)} %copy-done.12) | copy-start | bytes 2359300
  93.4 49.3 %copy-start = (bf16[384,4096]{1,0:T(8,128)(2,1)}, bf16[384,4096]{1,0:T(8,128)(2,1)S(1)}, u32[]{:S(2)}) copy-start(bf16[384,4096]{1,0:T(8,128)(2,1)S(1)} %get-tuple-element.65.refs_16_) | copy-start | bytes 9437188
  93.4 66.5 %collective-permute-start.9 = (bf16[384,1024]{1,0:T(8,128)(2,1)}, bf16[384,1024]{1,0:T(8,128)(2,1)}, u32[]{:S(2)}, u32[]{:S(2)}) collective-permute-start(bf16[384,1024]{1,0:T(8,128)(2,1)} %get-tuple-element.47.grad_ref.refs_21_), channel_id=1, source_target_pairs={{0,8},{1,9},{2,10},{3,11},{4,12},{5,13},{6,14},{7,15},{8,0},{9,1},... | collective-permute-start | bytes 2359304 | tf_op jit(solution)/shard_map/ppermute | solution.py:39
  93.6 25.7 %copy-start.11 = (bf16[384,1024]{1,0:T(8,128)(2,1)S(1)}, bf16[384,1024]{1,0:T(8,128)(2,1)}, u32[]{:S(2)}) copy-start(bf16[384,1024]{1,0:T(8,128)(2,1)} %copy-done.10) | copy-start | bytes 2359300
  119.1 39.6 %collective-permute-start.1 = (bf16[384,1024]{1,0:T(8,128)(2,1)}, bf16[384,1024]{1,0:T(8,128)(2,1)}, u32[]{:S(2)}, u32[]{:S(2)}) collective-permute-start(bf16[384,1024]{1,0:T(8,128)(2,1)} %get-tuple-element.51.grad_ref.refs_1_), channel_id=1, source_target_pairs={{0,4},{1,5},{2,6},{3,7},{4,0},{5,1},{6,2},{7,3},{8,12},{9,13},{10,... | collective-permute-start | bytes 2359304 | tf_op jit(solution)/shard_map/ppermute | solution.py:39
  137.9 3.3 copy-start.2
  140.8 17.7 %collective-permute-start.11 = (bf16[384,1024]{1,0:T(8,128)(2,1)}, bf16[384,1024]{1,0:T(8,128)(2,1)}, u32[]{:S(2)}, u32[]{:S(2)}) collective-permute-start(bf16[384,1024]{1,0:T(8,128)(2,1)} %copy-done.23), channel_id=1, source_target_pairs={{0,8},{1,9},{2,10},{3,11},{4,12},{5,13},{6,14},{7,15},{8,0},{9,1},... | collective-permute-start | bytes 2359304 | tf_op jit(solution)/shard_map/ppermute | solution.py:39
  142.4 21.1 %collective-permute-start.7 = (bf16[384,1024]{1,0:T(8,128)(2,1)}, bf16[384,1024]{1,0:T(8,128)(2,1)}, u32[]{:S(2)}, u32[]{:S(2)}) collective-permute-start(bf16[384,1024]{1,0:T(8,128)(2,1)} %get-tuple-element.66.refs_17_), channel_id=1, source_target_pairs={{0,2},{1,3},{2,0},{3,1},{4,6},{5,7},{6,4},{7,5},{8,10},{9,11},{10,... | collective-permute-start | bytes 2359304 | tf_op jit(solution)/shard_map/ppermute | solution.py:39
  144.9 18.8 %copy-start.6 = (bf16[1,384,1024]{2,1,0:T(8,128)(2,1)S(1)}, bf16[1,384,1024]{2,1,0:T(8,128)(2,1)}, u32[]{:S(2)}) copy-start(bf16[1,384,1024]{2,1,0:T(8,128)(2,1)} %param.8) | copy-start | bytes 2359300
  144.9 18.8 %copy-start.9 = (bf16[384,1024]{1,0:T(8,128)(2,1)S(1)}, bf16[384,1024]{1,0:T(8,128)(2,1)}, u32[]{:S(2)}) copy-start(bf16[384,1024]{1,0:T(8,128)(2,1)} %copy-done.8) | copy-start | bytes 2359300
  144.9 18.8 %copy-start.18 = (bf16[384,1024]{1,0:T(8,128)(2,1)S(1)}, bf16[384,1024]{1,0:T(8,128)(2,1)}, u32[]{:S(2)}) copy-start(bf16[384,1024]{1,0:T(8,128)(2,1)} %copy-done.17) | copy-start | bytes 2359300
  144.9 18.8 %copy-start.20 = (bf16[384,1024]{1,0:T(8,128)(2,1)S(1)}, bf16[384,1024]{1,0:T(8,128)(2,1)}, u32[]{:S(2)}) copy-start(bf16[384,1024]{1,0:T(8,128)(2,1)} %copy-done.19) | copy-start | bytes 2359300
  146.2 42.3 %collective-permute-start = (bf16[384,2048]{1,0:T(8,128)(2,1)}, bf16[384,2048]{1,0:T(8,128)(2,1)}, u32[]{:S(2)}, u32[]{:S(2)}) collective-permute-start(bf16[384,2048]{1,0:T(8,128)(2,1)} %constant_dynamic-slice_fusion.5), channel_id=1, source_target_pairs={{0,4},{1,5},{2,6},{3,7},{4,0},{5,1},{6,2},{7,3},{8,12},{9,13},{10,... | collective-permute-start | bytes 4718600 | tf_op jit(solution)/shard_map/ppermute | solution.py:39
  158.5 35.3 %collective-permute-start.4 = (bf16[384,2048]{1,0:T(8,128)(2,1)}, bf16[384,2048]{1,0:T(8,128)(2,1)}, u32[]{:S(2)}, u32[]{:S(2)}) collective-permute-start(bf16[384,2048]{1,0:T(8,128)(2,1)} %constant_dynamic-slice_fusion.3), channel_id=1, source_target_pairs={{0,2},{1,3},{2,0},{3,1},{4,6},{5,7},{6,4},{7,5},{8,10},{9,11},{10,... | collective-permute-start | bytes 4718600 | tf_op jit(solution)/shard_map/ppermute | solution.py:39
  158.7 68.8 %collective-permute-start.6 = (bf16[384,2048]{1,0:T(8,128)(2,1)}, bf16[384,2048]{1,0:T(8,128)(2,1)}, u32[]{:S(2)}, u32[]{:S(2)}) collective-permute-start(bf16[384,2048]{1,0:T(8,128)(2,1)} %constant_dynamic-slice_fusion.2), channel_id=1, source_target_pairs={{0,2},{1,3},{2,0},{3,1},{4,6},{5,7},{6,4},{7,5},{8,10},{9,11},{10,... | collective-permute-start | bytes 4718600 | tf_op jit(solution)/shard_map/ppermute | solution.py:39
  160.0 67.6 %collective-permute-start.2 = (bf16[384,2048]{1,0:T(8,128)(2,1)}, bf16[384,2048]{1,0:T(8,128)(2,1)}, u32[]{:S(2)}, u32[]{:S(2)}) collective-permute-start(bf16[384,2048]{1,0:T(8,128)(2,1)} %constant_dynamic-slice_fusion.4), channel_id=1, source_target_pairs={{0,4},{1,5},{2,6},{3,7},{4,0},{5,1},{6,2},{7,3},{8,12},{9,13},{10,... | collective-permute-start | bytes 4718600 | tf_op jit(solution)/shard_map/ppermute | solution.py:39
  161.1 2.5 copy-start.22
  163.6 25.0 %collective-permute-start.10 = (bf16[384,1536]{1,0:T(8,128)(2,1)}, bf16[384,1536]{1,0:T(8,128)(2,1)}, u32[]{:S(2)}, u32[]{:S(2)}) collective-permute-start(bf16[384,1536]{1,0:T(8,128)(2,1)} %constant_dynamic-slice_fusion), channel_id=1, source_target_pairs={{0,8},{1,9},{2,10},{3,11},{4,12},{5,13},{6,14},{7,15},{8,0},{9,1},... | collective-permute-start | bytes 3538952 | tf_op jit(solution)/shard_map/ppermute | solution.py:39
  822.7 35.3 %slice-start = ((s8[33554432]{0:T(1024)(128)(4,1)}), s8[4194304]{0:T(1024)(128)(4,1)S(1)}, s32[]{:S(2)}) async-start(s8[33554432]{0:T(1024)(128)(4,1)} %bitcast.8), calls=%async_computation | async-start | bytes 8388608
  822.7 35.3 %slice-start.1 = ((s8[33554432]{0:T(1024)(128)(4,1)}), s8[4194304]{0:T(1024)(128)(4,1)S(1)}, s32[]{:S(2)}) async-start(s8[33554432]{0:T(1024)(128)(4,1)} %bitcast.8), calls=%async_computation.1 | async-start | bytes 8388608
  831.3 26.7 %slice-start.2 = ((s8[33554432]{0:T(1024)(128)(4,1)}), s8[4194304]{0:T(1024)(128)(4,1)S(1)}, s32[]{:S(2)}) async-start(s8[33554432]{0:T(1024)(128)(4,1)} %bitcast.8), calls=%async_computation.2 | async-start | bytes 8388608
  831.3 26.7 %slice-start.3 = ((s8[33554432]{0:T(1024)(128)(4,1)}), s8[4194304]{0:T(1024)(128)(4,1)S(1)}, s32[]{:S(2)}) async-start(s8[33554432]{0:T(1024)(128)(4,1)} %bitcast.8), calls=%async_computation.3 | async-start | bytes 8388608
  831.3 26.7 %slice-start.4 = ((s8[33554432]{0:T(1024)(128)(4,1)}), s8[4194304]{0:T(1024)(128)(4,1)S(1)}, s32[]{:S(2)}) async-start(s8[33554432]{0:T(1024)(128)(4,1)} %bitcast.8), calls=%async_computation.4 | async-start | bytes 8388608
  831.3 26.7 %slice-start.5 = ((s8[33554432]{0:T(1024)(128)(4,1)}), s8[4194304]{0:T(1024)(128)(4,1)S(1)}, s32[]{:S(2)}) async-start(s8[33554432]{0:T(1024)(128)(4,1)} %bitcast.8), calls=%async_computation.5 | async-start | bytes 8388608
  831.3 28.3 %slice-start.6 = ((s8[33554432]{0:T(1024)(128)(4,1)}), s8[4194304]{0:T(1024)(128)(4,1)S(1)}, s32[]{:S(2)}) async-start(s8[33554432]{0:T(1024)(128)(4,1)} %bitcast.8), calls=%async_computation.6 | async-start | bytes 8388608
  831.3 29.5 %slice-start.7 = ((s8[33554432]{0:T(1024)(128)(4,1)}), s8[4194304]{0:T(1024)(128)(4,1)S(1)}, s32[]{:S(2)}) async-start(s8[33554432]{0:T(1024)(128)(4,1)} %bitcast.8), calls=%async_computation.7 | async-start | bytes 8388608
  (13 other events, 17.0 us)

commit v2 on v1

--- a/solution.py
+++ b/solution.py
@@ -6,7 +6,6 @@
 from jax.experimental import pallas as pl
 from jax.experimental.pallas import tpu as pltpu
 from jax.sharding import PartitionSpec as P
-
 
 NORM_EPS = 1e-6
 HEAD_DIM = 64
@@ -20,42 +19,44 @@
     'b8h5i5r4q2j6q3i6e7q4k5e8l6m5j5o6k7l5n5m7p6o5g7g8p5n7h7h8r6i7',
     'q5i8r5k6q7j7j8m6kel7l8n6mem8o7k8o8p7p8q6ner7n8r8qeq8',
 )
-
-
-class Place:
-    def __init__(self, n_dev):
-        me = lax.axis_index(AXIS)
-        self.core = me % 2
-        self.x = (me // 2) % 2
-        self.y = (me // 4) % 2
-        self.z = (me // 8) % 2
-        self.swap = {name: [(i, i ^ bit) for i in range(n_dev)] for name, bit in (('core', 1), ('x', 2), ('y', 4), ('z', 8))}
-
-    def at(self, name):
-        return {'core': self.core, 'x': self.x, 'y': self.y, 'z': self.z}[name]
-
-
-def send(val, pairs):
-    return lax.ppermute(val, AXIS, pairs)
-
-
-def part(val, which, count, axis):
-    size = val.shape[axis] // count
-    return lax.dynamic_slice_in_dim(val, which * size, size, axis)
-
-
-def neighbour_operands(place, axis, split, lhs, rhs):
-    away = part(lhs if split == 0 else rhs, 1 - place.at(axis), 2, 1)
-    wide, thin = (lhs, rhs) if split == 0 else (rhs, lhs)
-    wide_in = send(away, place.swap[axis])
-    thin_in = send(thin, place.swap[axis])
-    return wide, thin, wide_in, thin_in
+VMEM_LIMIT = 63 * 1024 * 1024
+
+
+MATRICES = ((1024, 1024, 0), (1024, 1024, 1), (256, 1024, 0), (1024, 768, 1))
+KIND = ('yyYy', 'xxXX')
+LATE = ((2, 0), (3, 0))
+SEQ_LEN = 384
+TOKENS = 4 * SEQ_LEN
+TILE_ROWS = 256
+STREAM_ROWS = 64
+N_SEMS = 12
+ADD_ROWS = 32
+
+
+def read_chunks(text):
+    found = []
+    for mat, layer in zip(*[map(int, text)] * 2):
+        found.append((mat, layer, sum(chunk[:2] == (mat, layer) for chunk in found)))
+    return tuple(found)
+
+
+CHUNKS = read_chunks(CHUNK_UNITS)
+
+
+def first_axis(mat, layer):
+    kind = KIND[layer][mat]
+    return kind if kind in 'xy' else 'z'
+
+
+def chunk_count(mat, layer):
+    return sum(chunk[:2] == (mat, layer) for chunk in CHUNKS)
 
 
 PAIR = 2 * HEAD_DIM
 GROUP = 2 * PAIR
 Q_BLOCK = 128
 FF_BLOCK = 512
+NORM_ROWS = 64
 GELU_C = 0.7978845608028654
 GELU_D = 0.044715
 
@@ -71,32 +72,42 @@
     return val.astype(jnp.bfloat16)
 
 
+def wide_float(val):
+    return val.astype(jnp.float32)
+
+
+def row_blocks(count):
+    def wrap(body):
+        @pl.loop(0, count // NORM_ROWS)
+        def _(step):
+            body(pl.ds(pl.multiple_of(step * NORM_ROWS, NORM_ROWS), NORM_ROWS))
+    return wrap
+
+
 def inverse_rms(rows_f):
     return lax.rsqrt(jnp.mean(rows_f * rows_f, axis=-1, keepdims=True) + NORM_EPS)
 
 
 def norm_forward(src, gain, dst):
-    @pl.loop(0, src.shape[0] // 64)
-    def _(step):
-        at = pl.ds(pl.multiple_of(step * 64, 64), 64)
-        rows_f = src[at, :].astype(jnp.float32)
-        dst[at, :] = (rows_f * inverse_rms(rows_f) * gain[...]).astype(jnp.bfloat16)
+    @row_blocks(src.shape[0])
+    def _(at):
+        rows_f = wide_float(src[at, :])
+        dst[at, :] = rounded(rows_f * inverse_rms(rows_f) * gain[...])
 
 
 def norm_backward(src, gain, grad_norm, grad_res, dst, gain_dst):
     gain_dst[...] = jnp.zeros_like(gain_dst)
 
-    @pl.loop(0, src.shape[0] // 64)
-    def _(step):
-        at = pl.ds(pl.multiple_of(step * 64, 64), 64)
-        rows_f = src[at, :].astype(jnp.float32)
+    @row_blocks(src.shape[0])
+    def _(at):
+        rows_f = wide_float(src[at, :])
         scale = inverse_rms(rows_f)
         unit = rows_f * scale
-        grad = grad_norm[at, :].astype(jnp.bfloat16).astype(jnp.float32)
+        grad = wide_float(rounded(grad_norm[at, :]))
         gain_dst[...] += jnp.sum(grad * unit, axis=0, keepdims=True)
         grad = grad * gain[...]
         grad = scale * (grad - unit * jnp.mean(grad * unit, axis=-1, keepdims=True))
-        dst[at, :] = (grad_res[at, :].astype(jnp.float32) + grad).astype(jnp.bfloat16)
+        dst[at, :] = rounded(wide_float(grad_res[at, :]) + grad)
 
 
 def two_heads(rows):
@@ -122,43 +133,17 @@
     return weights * (1.0 / jnp.sum(weights, axis=-1, keepdims=True))
 
 
-def attn_forward_kernel(x_ref, gain_ref, wq_ref, wk_ref, wv_ref, wo_ref, u_ref, q_ref, k_ref, v_ref, o_ref, h_ref, acc):
-    step = pl.program_id(0)
-
-    @pl.when(step == 0)
-    def _():
-        norm_forward(x_ref, gain_ref, u_ref)
-        acc[...] = jnp.zeros_like(acc)
-
-    for dst, weight in ((q_ref, wq_ref), (k_ref, wk_ref), (v_ref, wv_ref)):
-        dst[...] = rounded(dot_nn(u_ref[...], weight[...]))
-    for block in range(x_ref.shape[0] // Q_BLOCK):
+def attend(q_ref, k_ref, v_ref, o_ref):
+    for block in range(q_ref.shape[0] // Q_BLOCK):
         rows, keys = pl.ds(block * Q_BLOCK, Q_BLOCK), pl.ds(0, (block + 1) * Q_BLOCK)
         for pair in range(GROUP // PAIR):
             lanes = pl.ds(pair * PAIR, PAIR)
             prob = softmax_block(two_heads(q_ref[rows, lanes]), k_ref[keys, lanes], block)
-            o_ref[rows, lanes] = one_pair(dot_nn(prob.astype(jnp.bfloat16), v_ref[keys, lanes])).astype(jnp.bfloat16)
-    acc[...] += dot_nn(o_ref[...], wo_ref[...])
-
-    @pl.when(step == pl.num_programs(0) - 1)
-    def _():
-        h_ref[...] = x_ref[...] + acc[...].astype(jnp.bfloat16)
-
-
-def attn_backward_kernel(grad_ref, x_ref, gain_ref, q_ref, k_ref, v_ref, wo_ref, wq_ref, wk_ref, wv_ref, out_ref, dx_ref, dgain_ref, do_ref, k_acc, v_acc, acc):
-    step = pl.program_id(0)
-    seq_len, width = grad_ref.shape
-
-    @pl.when(step == 0)
-    def _():
-        acc[...] = jnp.zeros_like(acc)
-
-    do_ref[...] = rounded(dot_nt(grad_ref[...], wo_ref[...]))
-    n_block = seq_len // Q_BLOCK
-
-    def dest(which, lane, count):
-        return pl.ds(pl.multiple_of(which * width + step * GROUP + lane, PAIR), count)
-
+            o_ref[rows, lanes] = rounded(one_pair(dot_nn(rounded(prob), v_ref[keys, lanes])))
+
+
+def attend_backward(do_ref, q_ref, k_ref, v_ref, k_acc, v_acc):
+    n_block = q_ref.shape[0] // Q_BLOCK
     for pair in range(GROUP // PAIR):
         lanes = pl.ds(pair * PAIR, PAIR)
         for block in reversed(range(n_block)):
@@ -168,167 +153,272 @@
             prob = softmax_block(q_two, k_rows, block)
             grad_prob = dot_nt(g_two, v_ref[keys, lanes])
             mean = jnp.sum(prob * grad_prob, axis=-1, keepdims=True)
-            grad_s = (prob * (grad_prob - mean) * HEAD_DIM ** -0.5).astype(jnp.bfloat16)
-            out_ref[rows, dest(0, pair * PAIR, PAIR)] = one_pair(dot_nn(grad_s, k_rows)).astype(jnp.bfloat16)
-            k_part, v_part = dot_tn(grad_s, q_two), dot_tn(prob.astype(jnp.bfloat16), g_two)
+            grad_s = rounded(prob * (grad_prob - mean) * HEAD_DIM ** -0.5)
+            q_ref[rows, lanes] = rounded(one_pair(dot_nn(grad_s, k_rows)))
+            k_part, v_part = dot_tn(grad_s, q_two), dot_tn(rounded(prob), g_two)
             if block == n_block - 1:
                 k_acc[:, lanes] = k_part
                 v_acc[:, lanes] = v_part
             else:
                 k_acc[keys, lanes] += k_part
                 v_acc[keys, lanes] += v_part
-    out_ref[:, dest(1, 0, GROUP)] = k_acc[...].astype(jnp.bfloat16)
-    out_ref[:, dest(2, 0, GROUP)] = v_acc[...].astype(jnp.bfloat16)
-    for which, weight in enumerate((wq_ref, wk_ref, wv_ref)):
-        acc[...] += dot_nt(out_ref[:, dest(which, 0, GROUP)], weight[...])
-
-    @pl.when(step == pl.num_programs(0) - 1)
-    def _():
-        norm_backward(x_ref, gain_ref, acc, grad_ref, dx_ref, dgain_ref)
-
-
-def mlp_forward_kernel(has_down, h_ref, gain_ref, w1_ref, *refs):
-    w2_ref, refs = (refs[0], refs[1:]) if has_down else (None, refs)
-    u_ref, z_ref, a_ref = refs[:3]
-
-    @pl.when(pl.program_id(0) == 0)
-    def _():
-        norm_forward(h_ref, gain_ref, u_ref)
-
-    z_ref[...] = rounded(dot_nn(u_ref[...], w1_ref[...]))
-    rows_f = z_ref[...].astype(jnp.float32)
-    bend = jnp.tanh(GELU_C * (rows_f + GELU_D * (rows_f * rows_f * rows_f)))
-    a_ref[...] = (rows_f * (0.5 * (1.0 + bend))).astype(jnp.bfloat16)
-    if has_down:
-        y_ref, acc = refs[3:]
-
-        @pl.when(pl.program_id(0) == 0)
-        def _():
-            acc[...] = jnp.zeros_like(acc)
-
-        acc[...] += dot_nn(a_ref[...], w2_ref[...])
-
-        @pl.when(pl.program_id(0) == pl.num_programs(0) - 1)
-        def _():
-            y_ref[...] = h_ref[...] + acc[...].astype(jnp.bfloat16)
-
-
-def mlp_backward_kernel(grad_ref, h_ref, gain_ref, z_ref, w2_ref, w1_ref, dz_ref, dh_ref, dgain_ref, acc):
-    @pl.when(pl.program_id(0) == 0)
-    def _():
+    k_ref[...] = rounded(k_acc[...])
+    v_ref[...] = rounded(v_acc[...])
+
+
+KEPT = {'u_one': 1, 'mixed': 1, 'u_two': 1, 'act': 4, 'grad_pre': 4, 'grad_hidden': 1, 'grad_qkv': 3, 'grad': 1}
+FACTORS = (('act', 'grad'), ('u_two', 'grad_pre'), ('mixed', 'grad_hidden'), ('u_one', 'grad_qkv'))
+
+
+def own_place(me):
+    core, x_at, y_at, z_at = lax.rem(me, 2), lax.rem(lax.div(me, 2), 2), lax.rem(lax.div(me, 4), 2), lax.div(me, 8)
+    half = lax.div(z_at, 2)
+    place = {'core': core, 'x': x_at, 'y': y_at, 'z': lax.rem(z_at, 2), 'half': half}
+    to = {}
+    for name, stride in (('core', 1), ('x', 2), ('y', 4), ('z', 8)):
+        to[name] = me + stride * (1 - 2 * place[name])
+    inward = 8 * (1 - 2 * half)
+    to.update(mid=me + inward, end=me - inward, far=me + 2 * inward)
+    return place, to, lax.div(z_at + 1, 2) == 1, lax.div(z_at + 1, 2) != 1
+
+
+def compute_kernel(n_layers, x_in, grad_in, gain_one, gain_two, w_qkv, w_out, w_up, w_down, *refs):
+    refs = list(refs)
+
+    def take(count):
+        head, refs[:] = refs[:count], refs[count:]
+        return head
+
+    grad_out, gain_out = take(2)
+    kept = [dict(zip(KEPT, take(len(KEPT)))) for _ in range(n_layers)]
+    units = [(mat, layer) for layer in range(n_layers) for mat in range(len(MATRICES))]
+    early = [unit for unit in units if unit not in LATE]
+    from_chip = dict(zip(early, zip(take(len(early)), take(len(early)))))
+    rows, hidden, qkv, pre = (take(n_layers) for _ in range(4))
+    unit_rows, mixed, act, grad_hidden, grad, do_ref, k_acc, v_acc, acc, s_qkv, s_out, s_up, s_down = take(13)
+    sem_qkv, sem_out, sem_up, sem_down, sem_in, sem_put, sem_send, sem_recv = refs
+    place, to, _, _ = own_place(lax.axis_index(AXIS))
+    n_group, n_ff = s_out.shape[0], s_up.shape[0]
+
+    def fetch_group(layer, at):
+        cols = [pl.ds(pl.multiple_of((which * n_group + at) * GROUP, GROUP), GROUP) for which in range(3)]
+        pieces = [pltpu.make_async_copy(w_qkv.at[layer, :, cols[which]], s_qkv.at[which, at], sem_qkv.at[which, at]) for which in range(3)]
+        return pieces + [pltpu.make_async_copy(w_out.at[layer, pl.ds(pl.multiple_of(at * GROUP, GROUP), GROUP), :], s_out.at[at], sem_out.at[at])]
+
+    def fetch_up(layer, at):
+        return pltpu.make_async_copy(w_up.at[layer, :, pl.ds(pl.multiple_of(at * FF_BLOCK, FF_BLOCK), FF_BLOCK)], s_up.at[at], sem_up.at[at])
+
+    def fetch_down(layer, at):
+        return pltpu.make_async_copy(w_down.at[layer, pl.ds(pl.multiple_of(at * FF_BLOCK, FF_BLOCK), FF_BLOCK), :], s_down.at[at], sem_down.at[at])
+
+    def start_groups(layer):
+        for at in range(n_group):
+            for piece in fetch_group(layer, at):
+                piece.start()
+
+    def start_all(fetch, layer):
+        for at in range(n_ff):
+            fetch(layer, at).start()
+
+    n_put, sent, waiting = [0], [], []
+
+    def put(src, dst):
+        copy = pltpu.make_async_copy(src, dst, sem_put.at[n_put[0]])
+        n_put[0] += 1
+        copy.start()
+        return copy
+
+    def put_blocks(src, dst):
+        count, _, cols = src.shape
+        return [put(src.at[at], dst.at[:, pl.ds(at * cols, cols)]) for at in range(count)]
+
+    def exchange(mat, layer, which):
+        if (mat, layer) in LATE:
+            return
+        axis, split = first_axis(mat, layer), MATRICES[mat][2]
+        name = FACTORS[mat][which]
+        src = grad_in.at[0] if (name, layer) == ('grad', n_layers - 1) else kept[layer][name]
+        if which == split:
+            dst = from_chip[(mat, layer)][0]
+            src = src.at[:, pl.ds(pl.multiple_of((1 - place[axis]) * dst.shape[1], 128), dst.shape[1])]
+        else:
+            dst = from_chip[(mat, layer)][1]
+        copy = pltpu.make_async_remote_copy(src_ref=src, dst_ref=dst, send_sem=sem_send.at[len(sent)], recv_sem=sem_recv.at[len(sent)],
+                                            device_id=(to[axis],), device_id_type=pl.DeviceIdType.MESH)
+        sent.append(copy)
+        copy.start()
+
+    def save(name, layer, copies):
+        waiting.append((name, layer, copies))
+
+    def flush():
+        for name, layer, copies in waiting:
+            for copy in copies:
+                copy.wait()
+            for mat, names in enumerate(FACTORS):
+                if name in names:
+                    exchange(mat, layer, names.index(name))
+        waiting.clear()
+
+    def gain_row(gain, layer):
+        return gain.at[pl.ds(layer, 1), :]
+
+    def attention_forward(layer):
+        flush()
+        norm_forward(rows[layer], gain_row(gain_one, layer), unit_rows)
+        save('u_one', layer, [put(unit_rows, kept[layer]['u_one'])])
         acc[...] = jnp.zeros_like(acc)
-
-    grad_a = rounded(dot_nt(grad_ref[...], w2_ref[...])).astype(jnp.float32)
-    rows_f = z_ref[...].astype(jnp.float32)
-    square = rows_f * rows_f
-    bend = jnp.tanh(GELU_C * (rows_f + GELU_D * (square * rows_f)))
-    slope = 0.5 * (1.0 + bend) + (0.5 * GELU_C) * rows_f * (1.0 - bend * bend) * (1.0 + (3.0 * GELU_D) * square)
-    dz_ref[...] = (slope * grad_a).astype(jnp.bfloat16)
-    acc[...] += dot_nt(dz_ref[...], w1_ref[...])
-
-    @pl.when(pl.program_id(0) == pl.num_programs(0) - 1)
-    def _():
-        norm_backward(h_ref, gain_ref, acc, grad_ref, dh_ref, dgain_ref)
-
-
-def whole_spec(shape):
-    return pl.BlockSpec(shape, lambda step: (0,) * len(shape))
-
-
-def cols_spec(rows, cols):
-    return pl.BlockSpec((rows, cols), lambda step: (0, step))
-
-
-def weight_cols(layer, rows, cols, shift=0):
-    return pl.BlockSpec((None, rows, cols), lambda step: (layer, 0, shift + step))
-
-
-def weight_rows(layer, rows, cols):
-    return pl.BlockSpec((None, rows, cols), lambda step: (layer, step, 0))
-
-
-def lo(*shape):
-    return jax.ShapeDtypeStruct(shape, jnp.bfloat16)
-
-
-def block_call(kernel, grid, in_specs, out_specs, out_shape, scratch, flops, *args):
-    return pl.pallas_call(kernel, grid=(grid,), in_specs=in_specs, out_specs=out_specs, out_shape=out_shape,
-                          scratch_shapes=[pltpu.VMEM(shape, jnp.float32) if isinstance(shape, tuple) else shape for shape in scratch],
-                          cost_estimate=pl.CostEstimate(flops=flops, bytes_accessed=flops // 500, transcendentals=0),
-                          compiler_params=pltpu.CompilerParams(dimension_semantics=('arbitrary',), vmem_limit_bytes=48 * 1024 * 1024))(*args)
-
-
-def attn_forward(layer, x_rows, gain, w_qkv, w_out):
-    seq_len, width = x_rows.shape
-    full, cols, steps = whole_spec((seq_len, width)), cols_spec(seq_len, GROUP), width // GROUP
-    weights = [weight_cols(layer, width, GROUP, which * steps) for which in range(3)]
-    return block_call(attn_forward_kernel, steps, [full, whole_spec((1, width))] + weights + [weight_rows(layer, GROUP, width)],
-                      [full, cols, cols, cols, cols, full], [lo(seq_len, width)] * 6, [(seq_len, width)], 8 * seq_len * width * width,
-                      x_rows, gain[None], w_qkv, w_qkv, w_qkv, w_out)
-
-
-def attn_backward(layer, grad, x_rows, gain, q_rows, k_rows, v_rows, w_qkv, w_out):
-    seq_len, width = grad.shape
-    full, cols, steps = whole_spec((seq_len, width)), cols_spec(seq_len, GROUP), width // GROUP
-    weights = [weight_cols(layer, width, GROUP, which * steps) for which in range(3)]
-    return block_call(attn_backward_kernel, steps,
-                      [full, full, whole_spec((1, width)), cols, cols, cols, weight_rows(layer, GROUP, width)] + weights,
-                      [whole_spec((seq_len, 3 * width)), full, whole_spec((1, width))],
-                      [lo(seq_len, 3 * width), lo(seq_len, width), jax.ShapeDtypeStruct((1, width), jnp.float32)],
-                      [pltpu.VMEM((seq_len, GROUP), jnp.bfloat16), (seq_len, GROUP), (seq_len, GROUP), (seq_len, width)], 11 * seq_len * width * width,
-                      grad, x_rows, gain[None], q_rows, k_rows, v_rows, w_out, w_qkv, w_qkv, w_qkv)
-
-
-def mlp_forward(layer, h_rows, gain, w_up, w_down, has_down):
-    seq_len, width = h_rows.shape
-    inner = w_up.shape[2]
-    full, cols = whole_spec((seq_len, width)), cols_spec(seq_len, FF_BLOCK)
-    more = [weight_rows(layer, FF_BLOCK, width)] if has_down else []
-    return block_call(functools.partial(mlp_forward_kernel, has_down), inner // FF_BLOCK, [full, whole_spec((1, width)), weight_cols(layer, width, FF_BLOCK)] + more,
-                      [full, cols, cols] + [full] * has_down, [lo(seq_len, width), lo(seq_len, inner), lo(seq_len, inner)] + [lo(seq_len, width)] * has_down,
-                      [(seq_len, width)] * has_down, (4 if has_down else 2) * seq_len * width * inner,
-                      h_rows, gain[None], w_up, *([w_down] * has_down))
-
-
-def mlp_backward(layer, grad, h_rows, gain, z_rows, w_up, w_down):
-    seq_len, width = grad.shape
-    inner = w_up.shape[2]
-    full, cols = whole_spec((seq_len, width)), cols_spec(seq_len, FF_BLOCK)
-    return block_call(mlp_backward_kernel, inner // FF_BLOCK,
-                      [full, full, whole_spec((1, width)), cols, weight_rows(layer, FF_BLOCK, width), weight_cols(layer, width, FF_BLOCK)],
-                      [cols, full, whole_spec((1, width))],
-                      [lo(seq_len, inner), lo(seq_len, width), jax.ShapeDtypeStruct((1, width), jnp.float32)], [(seq_len, width)], 4 * seq_len * width * inner,
-                      grad, h_rows, gain[None], z_rows, w_down, w_up)
-
-
-MATRICES = ((1024, 1024, 0), (1024, 1024, 1), (256, 1024, 0), (1024, 768, 1))
-KIND = ('yyYy', 'xxXX')
-LATE = ((2, 0), (3, 0))
-SEQ_LEN = 384
-TOKENS = 4 * SEQ_LEN
-TILE_ROWS = 256
-STREAM_ROWS = 64
-N_SEMS = 12
-ADD_ROWS = 32
-
-
-def read_chunks(text):
-    found = []
-    for mat, layer in zip(*[map(int, text)] * 2):
-        found.append((mat, layer, sum(chunk[:2] == (mat, layer) for chunk in found)))
-    return tuple(found)
-
-
-CHUNKS = read_chunks(CHUNK_UNITS)
-
-
-def first_axis(mat, layer):
-    kind = KIND[layer][mat]
-    return kind if kind in 'xy' else 'z'
-
-
-def chunk_count(mat, layer):
-    return sum(chunk[:2] == (mat, layer) for chunk in CHUNKS)
+        q_all, k_all, v_all = (qkv[layer].at[which] for which in range(3))
+
+        @pl.loop(0, n_group)
+        def _(at):
+            for piece in fetch_group(layer, at):
+                piece.wait()
+            for which in range(3):
+                qkv[layer][which, at] = rounded(dot_nn(unit_rows[...], s_qkv[which, at]))
+            attend(q_all.at[at], k_all.at[at], v_all.at[at], mixed.at[at])
+            acc[...] += dot_nn(mixed[at], s_out[at])
+        save('mixed', layer, put_blocks(mixed, kept[layer]['mixed']))
+        hidden[layer][...] = rows[layer][...] + rounded(acc[...])
+
+    def mlp_forward(layer):
+        last = layer + 1 == n_layers
+        flush()
+        norm_forward(hidden[layer], gain_row(gain_two, layer), unit_rows)
+        save('u_two', layer, [put(unit_rows, kept[layer]['u_two'])])
+        acc[...] = jnp.zeros_like(acc)
+
+        @pl.loop(0, n_ff)
+        def _(at):
+            fetch_up(layer, at).wait()
+            pre[layer][at] = rounded(dot_nn(unit_rows[...], s_up[at]))
+            rows_f = wide_float(pre[layer][at])
+            bend = jnp.tanh(GELU_C * (rows_f + GELU_D * (rows_f * rows_f * rows_f)))
+            act[at] = rounded(rows_f * (0.5 * (1.0 + bend)))
+            if not last:
+                fetch_down(layer, at).wait()
+                acc[...] += dot_nn(act[at], s_down[at])
+        save('act', layer, put_blocks(act, kept[layer]['act']))
+        if not last:
+            rows[layer + 1][...] = hidden[layer][...] + rounded(acc[...])
+
+    def mlp_backward(layer, fetched):
+        acc[...] = jnp.zeros_like(acc)
+
+        @pl.loop(0, n_ff)
+        def _(at):
+            fetch_down(layer, at).wait()
+            if not fetched:
+                fetch_up(layer, at).wait()
+            grad_a = wide_float(rounded(dot_nt(grad[...], s_down[at])))
+            rows_f = wide_float(pre[layer][at])
+            square = rows_f * rows_f
+            bend = jnp.tanh(GELU_C * (rows_f + GELU_D * (square * rows_f)))
+            slope = 0.5 * (1.0 + bend) + (0.5 * GELU_C) * rows_f * (1.0 - bend * bend) * (1.0 + (3.0 * GELU_D) * square)
+            pre[layer][at] = rounded(slope * grad_a)
+            acc[...] += dot_nt(pre[layer][at], s_up[at])
+        flush()
+        save('grad_pre', layer, put_blocks(pre[layer], kept[layer]['grad_pre']))
+        norm_backward(hidden[layer], gain_row(gain_two, layer), acc, grad, grad_hidden, gain_row(gain_out, n_layers + layer))
+        save('grad_hidden', layer, [put(grad_hidden, kept[layer]['grad_hidden'])])
+
+    def attention_backward(layer, fetched):
+        acc[...] = jnp.zeros_like(acc)
+
+        @pl.loop(0, n_group)
+        def _(at):
+            if not fetched:
+                for piece in fetch_group(layer, at):
+                    piece.wait()
+            do_ref[...] = rounded(dot_nt(grad_hidden[...], s_out[at]))
+            attend_backward(do_ref, *(qkv[layer].at[which, at] for which in range(3)), k_acc, v_acc)
+            for which in range(3):
+                acc[...] += dot_nt(qkv[layer][which, at], s_qkv[which, at])
+        flush()
+        copies = []
+        for which in range(3):
+            width = grad.shape[1]
+            copies += [put(qkv[layer].at[which, at], kept[layer]['grad_qkv'].at[:, pl.ds(which * width + at * GROUP, GROUP)]) for at in range(n_group)]
+        save('grad_qkv', layer, copies)
+        norm_backward(rows[layer], gain_row(gain_one, layer), acc, grad_hidden, grad, gain_row(gain_out, layer))
+
+    first = pltpu.make_async_copy(x_in.at[0], rows[0], sem_in.at[0])
+    second = pltpu.make_async_copy(grad_in.at[0], grad, sem_in.at[1])
+    first.start()
+    start_groups(0)
+    start_all(fetch_up, 0)
+    start_all(fetch_down, 0)
+    second.start()
+    exchange(0, n_layers - 1, 1)
+    gain_out[...] = jnp.zeros_like(gain_out)
+    first.wait()
+    for layer in range(n_layers):
+        attention_forward(layer)
+        if layer + 1 < n_layers:
+            start_groups(layer + 1)
+        mlp_forward(layer)
+        if layer + 1 < n_layers:
+            start_all(fetch_up, layer + 1)
+            start_all(fetch_down, layer + 1)
+    second.wait()
+    flush()
+    for layer in reversed(range(n_layers)):
+        top = layer + 1 == n_layers
+        mlp_backward(layer, top)
+        if layer > 0:
+            start_all(fetch_up, layer - 1)
+            start_all(fetch_down, layer - 1)
+        flush()
+        attention_backward(layer, top)
+        if layer > 0:
+            start_groups(layer - 1)
+            save('grad', layer - 1, [put(grad, kept[layer - 1]['grad'])])
+            flush()
+    done = put(grad, grad_out)
+    flush()
+    done.wait()
+    for copy in sent:
+        copy.wait()
+
+
+def compute(x_loc, grad_loc, gain_one, gain_two, w_qkv, w_out, w_up, w_down):
+    n_layers, width, inner = w_up.shape
+    seq_len = x_loc.shape[1]
+    f32, bf16 = jnp.float32, jnp.bfloat16
+    n_group, n_ff = width // GROUP, inner // FF_BLOCK
+    units = [(mat, layer) for layer in range(n_layers) for mat in range(len(MATRICES))]
+    early = [unit for unit in units if unit not in LATE]
+
+    def lo(*shape):
+        return jax.ShapeDtypeStruct(shape, bf16)
+    outs = [lo(seq_len, width), jax.ShapeDtypeStruct((8, width), f32)]
+    outs += [lo(seq_len, cols * width) for _ in range(n_layers) for cols in KEPT.values()]
+    shapes = [[KEPT[name] * width for name in FACTORS[mat]] for mat, _ in early]
+    outs += [lo(seq_len, shape[MATRICES[mat][2]] // 2) for shape, (mat, _) in zip(shapes, early)]
+    outs += [lo(seq_len, shape[1 - MATRICES[mat][2]]) for shape, (mat, _) in zip(shapes, early)]
+    wide_rows, groups = (seq_len, width), (n_group, seq_len, GROUP)
+    vmem = [wide_rows] * (2 * n_layers) + [(3,) + groups] * n_layers + [(n_ff, seq_len, FF_BLOCK)] * n_layers
+    vmem += [wide_rows, groups, (n_ff, seq_len, FF_BLOCK), wide_rows, wide_rows, (seq_len, GROUP)]
+    scratch = [pltpu.VMEM(shape, bf16) for shape in vmem] + [pltpu.VMEM(shape, f32) for shape in ((seq_len, GROUP), (seq_len, GROUP), wide_rows)]
+    scratch += [pltpu.VMEM(shape, bf16) for shape in ((3, n_group, width, GROUP), (n_group, GROUP, width), (n_ff, width, FF_BLOCK), (n_ff, FF_BLOCK, width))]
+    scratch += [pltpu.SemaphoreType.DMA(shape) for shape in ((3, n_group), (n_group,), (n_ff,), (n_ff,), (2,), (100,), (2 * len(early),), (2 * len(early),))]
+    hbm, near = pl.BlockSpec(memory_space=pl.ANY), pl.BlockSpec(memory_space=pltpu.VMEM)
+    results = pl.pallas_call(
+        functools.partial(compute_kernel, n_layers), out_shape=tuple(outs), in_specs=[hbm, hbm, near, near] + [hbm] * 4,
+        out_specs=tuple([hbm, near] + [hbm] * (len(outs) - 2)), scratch_shapes=scratch,
+        compiler_params=pltpu.CompilerParams(has_side_effects=True, vmem_limit_bytes=VMEM_LIMIT),
+    )(x_loc, grad_loc, gain_one, gain_two, w_qkv, w_out, w_up, w_down)
+    grad_x, gains = results[:2]
+    kept = [dict(zip(KEPT, results[2 + layer * len(KEPT):])) for layer in range(n_layers)]
+    kept[-1]['grad'] = grad_loc[0]
+    tail = results[2 + n_layers * len(KEPT):]
+    from_chip = dict(zip(early, zip(tail, tail[len(early):])))
+    operands = []
+    for mat, layer in units:
+        pair = [kept[layer][name] for name in FACTORS[mat]]
+        split = MATRICES[mat][2]
+        operands.append((pair[split], pair[1 - split]) + from_chip.get((mat, layer), ()))
+    return grad_x, gains, operands
 
 
 def add_rows(dst, src, cols, scale=None):
@@ -362,14 +452,8 @@
     row_op, col_op, product, stream, gain_buf, gain_land, send_sems, recv_sems, local_sems, stream_sems, gain_send, gain_recv, op_send, op_recv, op_local = refs
 
     me = lax.axis_index(AXIS)
-    core, x_at, y_at, z_at = lax.rem(me, 2), lax.rem(lax.div(me, 2), 2), lax.rem(lax.div(me, 4), 2), lax.div(me, 8)
-    half = lax.div(z_at, 2)
-    middle = lax.div(z_at + 1, 2) == 1
-    edge = lax.div(z_at + 1, 2) != 1
-    place = {'x': x_at, 'y': y_at, 'z': lax.rem(z_at, 2)}
-    to = {'core': me + 1 - 2 * core, 'x': me + 2 * (1 - 2 * x_at), 'y': me + 4 * (1 - 2 * y_at),
-          'mid': me + 8 * (1 - 2 * half), 'end': me - 8 * (1 - 2 * half),
-          'z': me + 8 * (1 - 2 * place['z']), 'far': me + 16 * (1 - 2 * half)}
+    place, to, middle, edge = own_place(me)
+    core, half = place['core'], place['half']
 
     def remote(src, dst, i, sem, dev):
         return pltpu.make_async_remote_copy(src_ref=src, dst_ref=dst, send_sem=send_sems.at[i, sem], recv_sem=recv_sems.at[i, sem],
@@ -392,7 +476,6 @@
 
         def fetch(step, slot):
             return pltpu.make_async_copy(src.at[pl.ds(pl.multiple_of(step * size, size), size), :], stream.at[slot, pl.ds(0, size), pl.ds(0, cols)], stream_sems.at[slot])
-
         fetch(0, 0).start()
 
         @pl.loop(0, steps)
@@ -402,7 +485,6 @@
             @pl.when(step + 1 < steps)
             def _():
                 fetch(step + 1, 1 - slot).start()
-
             fetch(step, slot).wait()
             at = pl.ds(pl.multiple_of(step * size, size), size)
             dst[at, :] = dst[at, :] + stream[slot, pl.ds(0, size), pl.ds(0, cols)]
@@ -428,7 +510,6 @@
                 if dr is not None:
                     row, count = row + flip(r_at, dr) * (rows // 4), rows // 4
                 return out_block(i, flip(p_at, dp), flip(core, dc), row, count, None if dh is None else flip(half, dh))
-
             return ref
 
         def pass_on(blk, sems, cond=None):
@@ -540,7 +621,7 @@
 
     def operand_copies(u):
         unit = units[u]
-        _, _, p_name, split, wide_w, _ = unit_sizes(unit)
+        rows, cols, p_name, split, wide_w, _ = unit_sizes(unit)
         p_at = place[p_name]
         wide, thin = given[u][:2]
         core_wide, core_thin = from_core[2 * u:2 * u + 2]
@@ -553,7 +634,6 @@
 
         def lanes(at, count):
             return pl.ds(pl.multiple_of(at, 128), count)
-
         other = 1 - core
         copies = {
             'own': (operand_copy(u, 0, wide.at[:, lanes((p_at * 2 + other) * wide_w, wide_w)], core_wide.at[first, :], 'core'),
@@ -611,7 +691,6 @@
             for side in range(2):
                 lanes = pl.ds(side * half_w, half_w)
                 product[at, lanes] = dot_tn(row_op[:, at], col_op[:, lanes])
-
         store = pltpu.make_async_copy(product.at[pl.ds(0, rows), pl.ds(0, cols)], part_refs[u], op_local.at[u, 6])
         store.start()
         store.wait()
@@ -665,7 +744,6 @@
     for cond, src, i, sem in pending:
         def finish(src=src, i=i, sem=sem):
             remote(src(), src(), i, sem, me).wait_send()
-
         if cond is None:
             finish()
         else:
@@ -706,7 +784,7 @@
         in_specs=[hbm] * len(flat) + [vmem],
         out_specs=tuple([hbm] * 4 + [vmem] + [hbm] * (len(outs) - 5)),
         scratch_shapes=scratch,
-        compiler_params=pltpu.CompilerParams(has_side_effects=True, vmem_limit_bytes=63 * 1024 * 1024),
+        compiler_params=pltpu.CompilerParams(has_side_effects=True, vmem_limit_bytes=VMEM_LIMIT),
     )(*flat, gains)
     return results[:5]
 
@@ -714,38 +792,12 @@
 def solution(mesh):
     n_dev = mesh.shape[AXIS]
 
-    def whole_step(x_loc, grad_y_loc, gain_one, gain_two, w_qkv, w_out, w_up, w_down):
-        place = Place(n_dev)
+    def local_step(x_loc, grad_y_loc, gain_one, gain_two, w_qkv, w_out, w_up, w_down):
         n_layers = w_qkv.shape[0]
-        rows, saved = x_loc[0], []
-        for layer in range(n_layers):
-            u_one, q_all, k_all, v_all, mixed, hidden = attn_forward(layer, rows, gain_one[layer], w_qkv, w_out)
-            u_two, pre, act, *after = mlp_forward(layer, hidden, gain_two[layer], w_up, w_down, layer + 1 < n_layers)
-            saved.append((rows, u_one, q_all, k_all, v_all, mixed, hidden, u_two, pre, act))
-            rows = after[0] if after else None
-        operands = [None] * (n_layers * len(MATRICES))
-
-        def reduce_grad(mat, layer_idx, lhs, rhs):
-            color, split = first_axis(mat, layer_idx), MATRICES[mat][2]
-            if (mat, layer_idx) in LATE:
-                operands[layer_idx * len(MATRICES) + mat] = (lhs, rhs) if split == 0 else (rhs, lhs)
-            else:
-                operands[layer_idx * len(MATRICES) + mat] = neighbour_operands(place, color, split, lhs, rhs)
-
-        gain_grads = [None] * (2 * n_layers)
-        grad = grad_y_loc[0]
-        for layer in reversed(range(n_layers)):
-            rows, u_one, q_all, k_all, v_all, mixed, hidden, u_two, pre, act = saved[layer]
-            reduce_grad(0, layer, act, grad)
-            grad_pre, grad_hidden, gain_grads[n_layers + layer] = mlp_backward(layer, grad, hidden, gain_two[layer], pre, w_up, w_down)
-            reduce_grad(1, layer, u_two, grad_pre)
-            reduce_grad(2, layer, mixed, grad_hidden)
-            grad_qkv, grad, gain_grads[layer] = attn_backward(layer, grad_hidden, rows, gain_one[layer], q_all, k_all, v_all, w_qkv, w_out)
-            reduce_grad(3, layer, u_one, grad_qkv)
-        gains = jnp.concatenate(gain_grads + [jnp.zeros((8 - 2 * n_layers, gain_grads[0].shape[1]), jnp.float32)])
+        grad_x, gains, operands = compute(x_loc, grad_y_loc, gain_one, gain_two, w_qkv, w_out, w_up, w_down)
         down, up, out, qkv, gains = combine(operands, gains, n_dev, n_layers)
-        return (grad[None], gains[:n_layers], gains[n_layers:2 * n_layers], qkv, out, up, down)
+        return (grad_x[None], gains[:n_layers], gains[n_layers:2 * n_layers], qkv, out, up, down)
 
     batch_spec = P(AXIS)
     full_spec = P()
-    return jax.shard_map(whole_step, mesh=mesh, in_specs=(batch_spec, batch_spec) + (full_spec,) * 6, out_specs=(batch_spec,) + (full_spec,) * 6, check_vma=False)
+    return jax.shard_map(local_step, mesh=mesh, in_specs=(batch_spec, batch_spec) + (full_spec,) * 6, out_specs=(batch_spec,) + (full_spec,) * 6, check_vma=False)

time: 878 us -> 802 us (0.913)
  waiting for transfers between devices: 50.1 us -> 0 us
  local copies, waits for them, and re-layouts: 94.5 us -> 69.8 us
  Pallas kernels: 717 us -> 728 us
  starting transfers between devices: 9.68 us -> 0 us
    ppermute x12 -> x0, waiting for transfers between devices: 50.1 us -> none  [send(): return lax.ppermute(val, AXIS, pairs)]
    pallas_call x8 -> x1, Pallas kernels: 141 us -> 155 us  [compute(): pl.pallas_call(functools.partial(compute_kernel, n_layers), out_shape=tup...]
    unnamed x70 -> x23, local copies, waits for them, and re-layouts: 80.8 us -> 68.3 us
    dynamic_slice x6 -> x0, local copies, waits for them, and re-layouts: 10 us -> none  [part(): return lax.dynamic_slice_in_dim(val, which * size, size, axis)]
    ppermute x12 -> x0, starting transfers between devices: 9.68 us -> none  [send(): return lax.ppermute(val, AXIS, pairs)]
  transfers between devices with their start and end apart: 12 -> 0, of which waited for: 3 -> 0; matrix products, arithmetic and copies ran while one was open for 1% -> 0% of each run, Pallas kernels for 16% -> 0%
where the time goes in v2:
time: 802 us; the launch traced here: 798 us
  Pallas kernels  728 us (91%)
  local copies, waits for them, and re-layouts  69.8 us (9%)
    pallas_call x1, Pallas kernels, combine(): pl.pallas_call(functools.partial(combine_kernel, n_dev, n_layers), out_sh...  573 us
    pallas_call x1, Pallas kernels, compute(): pl.pallas_call(functools.partial(compute_kernel, n_layers), out_shape=tup...  155 us
    unnamed x23, local copies, waits for them, and re-layouts  68.3 us

profile of v2, /device:TPU:1, one launch (start us, length us, event | category | flops | bytes accessed | tf_op | source)
XLA Modules:
  0.0 798.2 jit_solution(3508943544082479021)
XLA Ops:
  0.6 154.9 %shard_map.135 = (bf16[384,1024]{1,0:T(8,128)(2,1)}, f32[8,1024]{1,0:T(8,128)}, bf16[384,1024]{1,0:T(8,128)(2,1)}, bf16[384,1024]{1,0:T(8,128)(2,1)}, bf16[384,1...) custom-call(bf16[1,384,1024]{2,1,0:T(8,128)(2,1)} %x_in.1, ...), custom_call_target="tpu_custom_call" | custom-call | tf_op jit(solution)/shard_map/pallas_call | solution.py:406
  155.5 0.0 copy-start
  155.5 572.8 %shard_map.136 = (f32[2,4096,1024]{2,1,0:T(8,128)}, f32[2,1024,4096]{2,1,0:T(8,128)}, f32[2,1024,1024]{2,1,0:T(8,128)}, f32[2,1024,3072]{2,1,0:T(8,128)}, f32[8,...) custom-call(bf16[384,4096]{1,0:T(8,128)(2,1)} %get-tuple-element.42., ...), custom_call_target="tpu_custom_call" | custom-call | tf_op jit(solution)/shard_map/pallas_call | solution.py:781
  728.3 1.4 fusion
  729.8 0.0 copy-done
  729.8 0.9 copy.20
  730.7 17.7 %copy.21 = f32[2,1024,3072]{2,1,0:T(8,128)} copy(f32[2,1024,3072]{2,1,0:T(8,128)} %get-tuple-element.87) | data formatting | bytes 50331648
  748.4 0.0 slice-start
  748.4 0.0 slice-start.1
  748.4 8.6 %copy.22 = f32[2,1024,1024]{2,1,0:T(8,128)} copy(f32[2,1024,1024]{2,1,0:T(8,128)} %get-tuple-element.88) | data formatting | bytes 16777216
  757.0 0.0 slice-start.2
  757.0 0.0 slice-start.3
  757.0 0.0 slice-start.4
  757.0 0.0 slice-start.5
  757.0 0.0 slice-start.6
  757.0 0.0 slice-start.7
  757.0 26.7 %copy.23 = f32[2,1024,4096]{2,1,0:T(8,128)} copy(f32[2,1024,4096]{2,1,0:T(8,128)} %get-tuple-element.89) | data formatting | bytes 67108864
  783.7 0.0 slice-done
  783.7 0.0 slice-done.1
  783.7 0.0 slice-done.2
  783.7 0.0 slice-done.3
  783.7 0.0 slice-done.4
  783.7 0.0 slice-done.5
  783.7 1.6 slice-done.6
  785.3 1.2 slice-done.7
  786.5 11.7 %copy.24 = f32[2,4096,1024]{2,1,0:T(8,128)} copy(f32[2,4096,1024]{2,1,0:T(8,128)S(1)} %bitcast.3) | data formatting | bytes 67108864
  (1 shorter events, 0.0 us)
Async XLA Ops:
  155.5 574.3 %copy-start = (bf16[384,1024]{1,0:T(8,128)(2,1)S(1)}, bf16[384,1024]{1,0:T(8,128)(2,1)}, u32[]{:S(2)}) copy-start(bf16[384,1024]{1,0:T(8,128)(2,1)} %get-tuple-element.41) | copy-start | bytes 2359300
  748.4 35.3 %slice-start = ((s8[33554432]{0:T(1024)(128)(4,1)}), s8[4194304]{0:T(1024)(128)(4,1)S(1)}, s32[]{:S(2)}) async-start(s8[33554432]{0:T(1024)(128)(4,1)} %bitcast.2), calls=%async_computation | async-start | bytes 8388608
  748.4 35.3 %slice-start.1 = ((s8[33554432]{0:T(1024)(128)(4,1)}), s8[4194304]{0:T(1024)(128)(4,1)S(1)}, s32[]{:S(2)}) async-start(s8[33554432]{0:T(1024)(128)(4,1)} %bitcast.2), calls=%async_computation.1 | async-start | bytes 8388608
  757.0 26.7 %slice-start.2 = ((s8[33554432]{0:T(1024)(128)(4,1)}), s8[4194304]{0:T(1024)(128)(4,1)S(1)}, s32[]{:S(2)}) async-start(s8[33554432]{0:T(1024)(128)(4,1)} %bitcast.2), calls=%async_computation.2 | async-start | bytes 8388608
  757.0 26.7 %slice-start.3 = ((s8[33554432]{0:T(1024)(128)(4,1)}), s8[4194304]{0:T(1024)(128)(4,1)S(1)}, s32[]{:S(2)}) async-start(s8[33554432]{0:T(1024)(128)(4,1)} %bitcast.2), calls=%async_computation.3 | async-start | bytes 8388608
  757.0 26.7 %slice-start.4 = ((s8[33554432]{0:T(1024)(128)(4,1)}), s8[4194304]{0:T(1024)(128)(4,1)S(1)}, s32[]{:S(2)}) async-start(s8[33554432]{0:T(1024)(128)(4,1)} %bitcast.2), calls=%async_computation.4 | async-start | bytes 8388608
  757.0 26.7 %slice-start.5 = ((s8[33554432]{0:T(1024)(128)(4,1)}), s8[4194304]{0:T(1024)(128)(4,1)S(1)}, s32[]{:S(2)}) async-start(s8[33554432]{0:T(1024)(128)(4,1)} %bitcast.2), calls=%async_computation.5 | async-start | bytes 8388608
  757.0 28.3 %slice-start.6 = ((s8[33554432]{0:T(1024)(128)(4,1)}), s8[4194304]{0:T(1024)(128)(4,1)S(1)}, s32[]{:S(2)}) async-start(s8[33554432]{0:T(1024)(128)(4,1)} %bitcast.2), calls=%async_computation.6 | async-start | bytes 8388608
  757.0 29.5 %slice-start.7 = ((s8[33554432]{0:T(1024)(128)(4,1)}), s8[4194304]{0:T(1024)(128)(4,1)S(1)}, s32[]{:S(2)}) async-start(s8[33554432]{0:T(1024)(128)(4,1)} %bitcast.2), calls=%async_computation.7 | async-start | bytes 8388608

commit v3 on v2

--- a/solution.py
+++ b/solution.py
@@ -10,20 +10,20 @@
 NORM_EPS = 1e-6
 HEAD_DIM = 64
 AXIS = 'data'
-CHUNK_UNITS = '003010111100300001102000313110102101'
+CHUNK_UNITS = '21011010113000000131100120011110'
 ORDER = (
-    'a9a0c9d9kaa1c0d0e0baa2c1f0b9b0a3c2f1g0d1a4i9c3h0f2b1i0f3c4e1',
-    'k9g1j0k0d2f4a5h1a6d3b2i1m9l0m0c5j1b3e2d4n0c6k1o0f5g2f6b4e3l1',
-    'q9p0h2g3a7a8m1q0h3i2e4c7c8j2d5k2g4l2n1f7h4f8r0d6i3b6j3o1k3l3',
-    'm2b5o2p1k4e5i4p2j4n2o3m3l4q1p3e6g6n3m4h6r1o4d7n4r2d8p4g5b7r3',
-    'b8h5i5r4q2j6q3i6e7q4k5e8l6m5j5o6k7l5n5m7p6o5g7g8p5n7h7h8r6i7',
-    'q5i8r5k6q7j7j8m6kel7l8n6mem8o7k8o8p7p8q6ner7n8r8qeq8',
+    'a9a0b9c9e9maa1b0c0d0e0a2fab1g9f9a3c1f0g0b2e1h0d1a4j9b3i0c2g1',
+    'j0c3b4e2f1k0c4h1m9a5e3i1d2l0m0b5g2d3e4c5k1b6n0g3a7h2j1a6d4o0',
+    'i2l1p0h3c6m1i3g4f2aek2a8b7b8n1l2e6c7h4c8j2e5f3m2d5k3n2i4d6l3',
+    'o1p1m3g6f4j3p2g5n3k4o2h6e7e8h5d7d8j4p3l4i5i6m4f5o3n4g7k6k5g8',
+    'l6p4m6i7f7i8h7n6o4h8j5l5k7m5k8j7p6n5f6o5j6l7l8p5m7fem8f8n7n8',
+    'o6o7p7jeo8p8j8',
 )
 VMEM_LIMIT = 63 * 1024 * 1024
 
 
 MATRICES = ((1024, 1024, 0), (1024, 1024, 1), (256, 1024, 0), (1024, 768, 1))
-KIND = ('yyYy', 'xxXX')
+KIND = ('xyyX', 'yxXY')
 LATE = ((2, 0), (3, 0))
 SEQ_LEN = 384
 TOKENS = 4 * SEQ_LEN
@@ -57,6 +57,8 @@
 Q_BLOCK = 128
 FF_BLOCK = 512
 NORM_ROWS = 64
+FORWARD_STEPS = ((0, 1, 2),)
+BACKWARD_STEPS = ((2, 1, 0),)
 GELU_C = 0.7978845608028654
 GELU_D = 0.044715
 
@@ -122,41 +124,54 @@
     return jnp.where(first, rows[:half], rows[half:])
 
 
-def softmax_block(q_two, k_rows, block):
-    n_keys = k_rows.shape[0]
-    scores = dot_nt(q_two, k_rows) * HEAD_DIM ** -0.5
-    last = scores[:, n_keys - Q_BLOCK:]
-    row = lax.rem(lax.broadcasted_iota(jnp.int32, last.shape, 0), Q_BLOCK)
-    last = jnp.where(row >= lax.broadcasted_iota(jnp.int32, last.shape, 1), last, -1e30)
-    scores = last if block == 0 else jnp.concatenate([scores[:, :n_keys - Q_BLOCK], last], axis=1)
-    weights = jnp.exp(scores - jnp.max(scores, axis=-1, keepdims=True))
-    return weights * (1.0 / jnp.sum(weights, axis=-1, keepdims=True))
+def in_step(step, *lists):
+    return [step(*args) for args in zip(*lists)]
+
+
+def softmax_blocks(q_twos, k_all):
+    scores = in_step(lambda q_two, k_rows: dot_nt(q_two, k_rows) * HEAD_DIM ** -0.5, q_twos, k_all)
+    shape = (2 * Q_BLOCK, Q_BLOCK)
+    seen = lax.rem(lax.broadcasted_iota(jnp.int32, shape, 0), Q_BLOCK) >= lax.broadcasted_iota(jnp.int32, shape, 1)
+
+    def masked(score):
+        before = score.shape[1] - Q_BLOCK
+        last = jnp.where(seen, score[:, before:], -1e30)
+        return jnp.concatenate([score[:, :before], last], axis=1) if before else last
+    scores = in_step(masked, scores)
+    peaks = in_step(lambda score: jnp.max(score, axis=-1, keepdims=True), scores)
+    weights = in_step(lambda score, peak: jnp.exp(score - peak), scores, peaks)
+    totals = in_step(lambda weight: 1.0 / jnp.sum(weight, axis=-1, keepdims=True), weights)
+    return in_step(lambda weight, total: weight * total, weights, totals)
+
+
+def jobs_of(blocks):
+    return [(pl.ds(block * Q_BLOCK, Q_BLOCK), pl.ds(0, (block + 1) * Q_BLOCK), pl.ds(pair * PAIR, PAIR)) for block in blocks for pair in range(GROUP // PAIR)]
 
 
 def attend(q_ref, k_ref, v_ref, o_ref):
-    for block in range(q_ref.shape[0] // Q_BLOCK):
-        rows, keys = pl.ds(block * Q_BLOCK, Q_BLOCK), pl.ds(0, (block + 1) * Q_BLOCK)
-        for pair in range(GROUP // PAIR):
-            lanes = pl.ds(pair * PAIR, PAIR)
-            prob = softmax_block(two_heads(q_ref[rows, lanes]), k_ref[keys, lanes], block)
-            o_ref[rows, lanes] = rounded(one_pair(dot_nn(rounded(prob), v_ref[keys, lanes])))
+    for blocks in FORWARD_STEPS:
+        jobs = jobs_of(blocks)
+        probs = softmax_blocks([two_heads(q_ref[rows, lanes]) for rows, _, lanes in jobs], [k_ref[keys, lanes] for _, keys, lanes in jobs])
+        results = in_step(lambda prob, job: dot_nn(rounded(prob), v_ref[job[1], job[2]]), probs, jobs)
+        for result, (rows, _, lanes) in zip(results, jobs):
+            o_ref[rows, lanes] = rounded(one_pair(result))
 
 
 def attend_backward(do_ref, q_ref, k_ref, v_ref, k_acc, v_acc):
-    n_block = q_ref.shape[0] // Q_BLOCK
-    for pair in range(GROUP // PAIR):
-        lanes = pl.ds(pair * PAIR, PAIR)
-        for block in reversed(range(n_block)):
-            rows, keys = pl.ds(block * Q_BLOCK, Q_BLOCK), pl.ds(0, (block + 1) * Q_BLOCK)
-            q_two, g_two = two_heads(q_ref[rows, lanes]), two_heads(do_ref[rows, lanes])
-            k_rows = k_ref[keys, lanes]
-            prob = softmax_block(q_two, k_rows, block)
-            grad_prob = dot_nt(g_two, v_ref[keys, lanes])
-            mean = jnp.sum(prob * grad_prob, axis=-1, keepdims=True)
-            grad_s = rounded(prob * (grad_prob - mean) * HEAD_DIM ** -0.5)
-            q_ref[rows, lanes] = rounded(one_pair(dot_nn(grad_s, k_rows)))
-            k_part, v_part = dot_tn(grad_s, q_two), dot_tn(rounded(prob), g_two)
-            if block == n_block - 1:
+    for blocks in BACKWARD_STEPS:
+        jobs = jobs_of(blocks)
+        q_twos, g_twos = ([two_heads(ref[rows, lanes]) for rows, _, lanes in jobs] for ref in (q_ref, do_ref))
+        k_rows = [k_ref[keys, lanes] for _, keys, lanes in jobs]
+        grad_probs = in_step(lambda g_two, job: dot_nt(g_two, v_ref[job[1], job[2]]), g_twos, jobs)
+        probs = softmax_blocks(q_twos, k_rows)
+        means = in_step(lambda prob, grad_prob: jnp.sum(prob * grad_prob, axis=-1, keepdims=True), probs, grad_probs)
+        grad_s = in_step(lambda prob, grad_prob, mean: rounded(prob * (grad_prob - mean) * HEAD_DIM ** -0.5), probs, grad_probs, means)
+        q_grads = in_step(dot_nn, grad_s, k_rows)
+        k_parts = in_step(dot_tn, grad_s, q_twos)
+        v_parts = in_step(lambda prob, g_two: dot_tn(rounded(prob), g_two), probs, g_twos)
+        for q_grad, k_part, v_part, (rows, keys, lanes) in zip(q_grads, k_parts, v_parts, jobs):
+            q_ref[rows, lanes] = rounded(one_pair(q_grad))
+            if keys.size == q_ref.shape[0]:
                 k_acc[:, lanes] = k_part
                 v_acc[:, lanes] = v_part
             else:

time: 802 us -> 782 us (0.975)
  Pallas kernels: 728 us -> 709 us
    pallas_call x1, Pallas kernels: 155 us -> 142 us  [compute(): pl.pallas_call(functools.partial(compute_kernel, n_layers), out_shape=tup...]
where the time goes in v3:
time: 782 us; the launch traced here: 780 us
  Pallas kernels  709 us (91%)
  local copies, waits for them, and re-layouts  69.8 us (9%)
    pallas_call x1, Pallas kernels, combine(): pl.pallas_call(functools.partial(combine_kernel, n_dev, n_layers), out_sh...  568 us
    pallas_call x1, Pallas kernels, compute(): pl.pallas_call(functools.partial(compute_kernel, n_layers), out_shape=tup...  142 us
    unnamed x23, local copies, waits for them, and re-layouts  68.3 us

profile of v3, /device:TPU:1, one launch (start us, length us, event | category | flops | bytes accessed | tf_op | source)
XLA Modules:
  0.0 779.9 jit_solution(10380544554253457063)
XLA Ops:
  0.6 141.6 %shard_map.135 = (bf16[384,1024]{1,0:T(8,128)(2,1)}, f32[8,1024]{1,0:T(8,128)}, bf16[384,1024]{1,0:T(8,128)(2,1)}, bf16[384,1024]{1,0:T(8,128)(2,1)}, bf16[384,1...) custom-call(bf16[1,384,1024]{2,1,0:T(8,128)(2,1)} %x_in.1, ...), custom_call_target="tpu_custom_call" | custom-call | tf_op jit(solution)/shard_map/pallas_call | solution.py:421
  142.2 0.0 copy-start
  142.2 567.8 %shard_map.136 = (f32[2,4096,1024]{2,1,0:T(8,128)}, f32[2,1024,4096]{2,1,0:T(8,128)}, f32[2,1024,1024]{2,1,0:T(8,128)}, f32[2,1024,3072]{2,1,0:T(8,128)}, f32[8,...) custom-call(bf16[384,4096]{1,0:T(8,128)(2,1)} %get-tuple-element.42., ...), custom_call_target="tpu_custom_call" | custom-call | tf_op jit(solution)/shard_map/pallas_call | solution.py:796
  710.1 1.4 fusion
  711.5 0.0 copy-done
  711.5 0.9 copy.20
  712.4 17.7 %copy.21 = f32[2,1024,3072]{2,1,0:T(8,128)} copy(f32[2,1024,3072]{2,1,0:T(8,128)} %get-tuple-element.87) | data formatting | bytes 50331648
  730.1 0.0 slice-start
  730.1 0.0 slice-start.1
  730.1 8.6 %copy.22 = f32[2,1024,1024]{2,1,0:T(8,128)} copy(f32[2,1024,1024]{2,1,0:T(8,128)} %get-tuple-element.88) | data formatting | bytes 16777216
  738.7 0.0 slice-start.2
  738.7 0.0 slice-start.3
  738.7 0.0 slice-start.4
  738.7 0.0 slice-start.5
  738.7 0.0 slice-start.6
  738.7 0.0 slice-start.7
  738.7 26.7 %copy.23 = f32[2,1024,4096]{2,1,0:T(8,128)} copy(f32[2,1024,4096]{2,1,0:T(8,128)} %get-tuple-element.89) | data formatting | bytes 67108864
  765.4 0.0 slice-done
  765.4 0.0 slice-done.1
  765.4 0.0 slice-done.2
  765.4 0.0 slice-done.3
  765.4 0.0 slice-done.4
  765.4 0.0 slice-done.5
  765.5 1.6 slice-done.6
  767.0 1.2 slice-done.7
  768.2 11.7 %copy.24 = f32[2,4096,1024]{2,1,0:T(8,128)} copy(f32[2,4096,1024]{2,1,0:T(8,128)S(1)} %bitcast.3) | data formatting | bytes 67108864
  (1 shorter events, 0.0 us)
Async XLA Ops:
  142.2 569.3 %copy-start = (bf16[384,1024]{1,0:T(8,128)(2,1)S(1)}, bf16[384,1024]{1,0:T(8,128)(2,1)}, u32[]{:S(2)}) copy-start(bf16[384,1024]{1,0:T(8,128)(2,1)} %get-tuple-element.41) | copy-start | bytes 2359300
  730.1 35.3 %slice-start = ((s8[33554432]{0:T(1024)(128)(4,1)}), s8[4194304]{0:T(1024)(128)(4,1)S(1)}, s32[]{:S(2)}) async-start(s8[33554432]{0:T(1024)(128)(4,1)} %bitcast.2), calls=%async_computation | async-start | bytes 8388608
  730.1 35.3 %slice-start.1 = ((s8[33554432]{0:T(1024)(128)(4,1)}), s8[4194304]{0:T(1024)(128)(4,1)S(1)}, s32[]{:S(2)}) async-start(s8[33554432]{0:T(1024)(128)(4,1)} %bitcast.2), calls=%async_computation.1 | async-start | bytes 8388608
  738.7 26.7 %slice-start.2 = ((s8[33554432]{0:T(1024)(128)(4,1)}), s8[4194304]{0:T(1024)(128)(4,1)S(1)}, s32[]{:S(2)}) async-start(s8[33554432]{0:T(1024)(128)(4,1)} %bitcast.2), calls=%async_computation.2 | async-start | bytes 8388608
  738.7 26.7 %slice-start.3 = ((s8[33554432]{0:T(1024)(128)(4,1)}), s8[4194304]{0:T(1024)(128)(4,1)S(1)}, s32[]{:S(2)}) async-start(s8[33554432]{0:T(1024)(128)(4,1)} %bitcast.2), calls=%async_computation.3 | async-start | bytes 8388608
  738.7 26.7 %slice-start.4 = ((s8[33554432]{0:T(1024)(128)(4,1)}), s8[4194304]{0:T(1024)(128)(4,1)S(1)}, s32[]{:S(2)}) async-start(s8[33554432]{0:T(1024)(128)(4,1)} %bitcast.2), calls=%async_computation.4 | async-start | bytes 8388608
  738.7 26.7 %slice-start.5 = ((s8[33554432]{0:T(1024)(128)(4,1)}), s8[4194304]{0:T(1024)(128)(4,1)S(1)}, s32[]{:S(2)}) async-start(s8[33554432]{0:T(1024)(128)(4,1)} %bitcast.2), calls=%async_computation.5 | async-start | bytes 8388608
  738.7 28.3 %slice-start.6 = ((s8[33554432]{0:T(1024)(128)(4,1)}), s8[4194304]{0:T(1024)(128)(4,1)S(1)}, s32[]{:S(2)}) async-start(s8[33554432]{0:T(1024)(128)(4,1)} %bitcast.2), calls=%async_computation.6 | async-start | bytes 8388608
  738.7 29.5 %slice-start.7 = ((s8[33554432]{0:T(1024)(128)(4,1)}), s8[4194304]{0:T(1024)(128)(4,1)S(1)}, s32[]{:S(2)}) async-start(s8[33554432]{0:T(1024)(128)(4,1)} %bitcast.2), calls=%async_computation.7 | async-start | bytes 8388608

commit v4 on v3

--- a/solution.py
+++ b/solution.py
@@ -10,20 +10,21 @@
 NORM_EPS = 1e-6
 HEAD_DIM = 64
 AXIS = 'data'
-CHUNK_UNITS = '21011010113000000131100120011110'
+CHUNK_UNITS = '1111110000100110012131303120113000003030'
 ORDER = (
-    'a9a0b9c9e9maa1b0c0d0e0a2fab1g9f9a3c1f0g0b2e1h0d1a4j9b3i0c2g1',
-    'j0c3b4e2f1k0c4h1m9a5e3i1d2l0m0b5g2d3e4c5k1b6n0g3a7h2j1a6d4o0',
-    'i2l1p0h3c6m1i3g4f2aek2a8b7b8n1l2e6c7h4c8j2e5f3m2d5k3n2i4d6l3',
-    'o1p1m3g6f4j3p2g5n3k4o2h6e7e8h5d7d8j4p3l4i5i6m4f5o3n4g7k6k5g8',
-    'l6p4m6i7f7i8h7n6o4h8j5l5k7m5k8j7p6n5f6o5j6l7l8p5m7fem8f8n7n8',
-    'o6o7p7jeo8p8j8',
+    'a9d9a0b0c0d0naa1f9e0lab1g9f0a2d1g0c1h0b2a3e1j9i0b3d2f1a4k9d3',
+    'c2g1j0b4l9k0e2c3h1l0d4e3i1n9a5m0f2c4a6e4f3b5b6j1g2k1d6n0d5l1',
+    'o0g3f4a7p0h2a8c6c5h3m1g4i2q0l2e5e6b7b8k2h4j2i3l3d7d8n1k3f6o1',
+    'j3p1r0f5s0i4o2j4t0p2l4k4o3m2p3c7c8q1g5g6m3o4e7m4e8q2p4q3h5h6',
+    'n2q4n3n4s1f7i6f8t1r1l5k5s2j5i5s3r2s4t2l6k7r3g7j7t3g8o6o5p5p6',
+    'm5r4t4n5h7q6h8m7n7q5k6i7l7i8l8s5s6keo7j6o8k8r6p7m6r5jet5p8t6',
+    'n6meq7m8q8j8r7s7r8nes8t7n8t8',
 )
 VMEM_LIMIT = 63 * 1024 * 1024
 
 
 MATRICES = ((1024, 1024, 0), (1024, 1024, 1), (256, 1024, 0), (1024, 768, 1))
-KIND = ('xyyX', 'yxXY')
+KIND = ('xyYy', 'xyYX')
 LATE = ((2, 0), (3, 0))
 SEQ_LEN = 384
 TOKENS = 4 * SEQ_LEN
@@ -56,7 +57,7 @@
 GROUP = 2 * PAIR
 Q_BLOCK = 128
 FF_BLOCK = 512
-NORM_ROWS = 64
+NORM_ROWS = 128
 FORWARD_STEPS = ((0, 1, 2),)
 BACKWARD_STEPS = ((2, 1, 0),)
 GELU_C = 0.7978845608028654
@@ -211,7 +212,7 @@
     from_chip = dict(zip(early, zip(take(len(early)), take(len(early)))))
     rows, hidden, qkv, pre = (take(n_layers) for _ in range(4))
     unit_rows, mixed, act, grad_hidden, grad, do_ref, k_acc, v_acc, acc, s_qkv, s_out, s_up, s_down = take(13)
-    sem_qkv, sem_out, sem_up, sem_down, sem_in, sem_put, sem_send, sem_recv = refs
+    sem_qkv, sem_out, sem_up, sem_down, sem_in, sem_put, sem_send, sem_recv, sem_out_blocks, sem_in_blocks = refs
     place, to, _, _ = own_place(lax.axis_index(AXIS))
     n_group, n_ff = s_out.shape[0], s_up.shape[0]
 
@@ -235,7 +236,7 @@
         for at in range(n_ff):
             fetch(layer, at).start()
 
-    n_put, sent, waiting = [0], [], []
+    n_put, sent, waiting, streams = [0], [], [], []
 
     def put(src, dst):
         copy = pltpu.make_async_copy(src, dst, sem_put.at[n_put[0]])
@@ -248,7 +249,7 @@
         return [put(src.at[at], dst.at[:, pl.ds(at * cols, cols)]) for at in range(count)]
 
     def exchange(mat, layer, which):
-        if (mat, layer) in LATE:
+        if (mat, layer) in LATE or (mat, which) == (1, 1):
             return
         axis, split = first_axis(mat, layer), MATRICES[mat][2]
         name = FACTORS[mat][which]
@@ -281,14 +282,26 @@
     def attention_forward(layer):
         flush()
         norm_forward(rows[layer], gain_row(gain_one, layer), unit_rows)
+        if layer == 0:
+            for piece in fetch_group(layer, n_group - 1):
+                piece.wait()
+            start_all(fetch_up, 0)
+            start_all(fetch_down, 0)
+            second.start()
         save('u_one', layer, [put(unit_rows, kept[layer]['u_one'])])
         acc[...] = jnp.zeros_like(acc)
         q_all, k_all, v_all = (qkv[layer].at[which] for which in range(3))
 
         @pl.loop(0, n_group)
         def _(at):
-            for piece in fetch_group(layer, at):
-                piece.wait()
+            if layer > 0:
+                for piece in fetch_group(layer, at):
+                    piece.wait()
+            else:
+                @pl.when(at < n_group - 1)
+                def _():
+                    for piece in fetch_group(layer, at):
+                        piece.wait()
             for which in range(3):
                 qkv[layer][which, at] = rounded(dot_nn(unit_rows[...], s_qkv[which, at]))
             attend(q_all.at[at], k_all.at[at], v_all.at[at], mixed.at[at])
@@ -296,43 +309,65 @@
         save('mixed', layer, put_blocks(mixed, kept[layer]['mixed']))
         hidden[layer][...] = rows[layer][...] + rounded(acc[...])
 
-    def mlp_forward(layer):
-        last = layer + 1 == n_layers
+    def bent(rows_f):
+        return jnp.tanh(GELU_C * (rows_f + GELU_D * (rows_f * rows_f * rows_f)))
+
+    def gelu(rows_f, bend):
+        return rounded(rows_f * (0.5 * (1.0 + bend)))
+
+    def gelu_slope(rows_f, bend):
+        return 0.5 * (1.0 + bend) + (0.5 * GELU_C) * rows_f * (1.0 - bend * bend) * (1.0 + (3.0 * GELU_D) * (rows_f * rows_f))
+
+    def mlp_norm(layer):
         flush()
         norm_forward(hidden[layer], gain_row(gain_two, layer), unit_rows)
         save('u_two', layer, [put(unit_rows, kept[layer]['u_two'])])
         acc[...] = jnp.zeros_like(acc)
 
+    def mlp_forward(layer):
+        mlp_norm(layer)
+
         @pl.loop(0, n_ff)
         def _(at):
             fetch_up(layer, at).wait()
+            fetch_down(layer, at).wait()
             pre[layer][at] = rounded(dot_nn(unit_rows[...], s_up[at]))
             rows_f = wide_float(pre[layer][at])
-            bend = jnp.tanh(GELU_C * (rows_f + GELU_D * (rows_f * rows_f * rows_f)))
-            act[at] = rounded(rows_f * (0.5 * (1.0 + bend)))
-            if not last:
-                fetch_down(layer, at).wait()
-                acc[...] += dot_nn(act[at], s_down[at])
+            act[at] = gelu(rows_f, bent(rows_f))
+            acc[...] += dot_nn(act[at], s_down[at])
         save('act', layer, put_blocks(act, kept[layer]['act']))
-        if not last:
-            rows[layer + 1][...] = hidden[layer][...] + rounded(acc[...])
-
-    def mlp_backward(layer, fetched):
+        rows[layer + 1][...] = hidden[layer][...] + rounded(acc[...])
+
+    def mlp_backward(layer, top):
+        if top:
+            mlp_norm(layer)
         acc[...] = jnp.zeros_like(acc)
+        axis = first_axis(1, layer)
+
+        def stream(step, at):
+            return pltpu.make_async_remote_copy(
+                src_ref=pre[layer].at[at], dst_ref=from_chip[(1, layer)][0].at[:, pl.ds(pl.multiple_of(step * FF_BLOCK, FF_BLOCK), FF_BLOCK)],
+                send_sem=sem_out_blocks.at[layer, step], recv_sem=sem_in_blocks.at[layer, step], device_id=(to[axis],), device_id_type=pl.DeviceIdType.MESH)
 
         @pl.loop(0, n_ff)
-        def _(at):
+        def _(step):
+            at = lax.rem(step + (1 - place[axis]) * (n_ff // 2), n_ff)
             fetch_down(layer, at).wait()
-            if not fetched:
-                fetch_up(layer, at).wait()
+            fetch_up(layer, at).wait()
+            rows_f = wide_float(rounded(dot_nn(unit_rows[...], s_up[at])) if top else pre[layer][at])
+            bend = bent(rows_f)
+            if top:
+                act[at] = gelu(rows_f, bend)
             grad_a = wide_float(rounded(dot_nt(grad[...], s_down[at])))
-            rows_f = wide_float(pre[layer][at])
-            square = rows_f * rows_f
-            bend = jnp.tanh(GELU_C * (rows_f + GELU_D * (square * rows_f)))
-            slope = 0.5 * (1.0 + bend) + (0.5 * GELU_C) * rows_f * (1.0 - bend * bend) * (1.0 + (3.0 * GELU_D) * square)
-            pre[layer][at] = rounded(slope * grad_a)
+            pre[layer][at] = rounded(gelu_slope(rows_f, bend) * grad_a)
             acc[...] += dot_nt(pre[layer][at], s_up[at])
+            if (1, layer) not in LATE:
+                pl.when(step < n_ff // 2)(lambda: stream(step, at).start())
+        if (1, layer) not in LATE:
+            streams.extend(functools.partial(stream, step, step) for step in range(n_ff // 2))
         flush()
+        if top:
+            save('act', layer, put_blocks(act, kept[layer]['act']))
         save('grad_pre', layer, put_blocks(pre[layer], kept[layer]['grad_pre']))
         norm_backward(hidden[layer], gain_row(gain_two, layer), acc, grad, grad_hidden, gain_row(gain_out, n_layers + layer))
         save('grad_hidden', layer, [put(grad_hidden, kept[layer]['grad_hidden'])])
@@ -361,9 +396,6 @@
     second = pltpu.make_async_copy(grad_in.at[0], grad, sem_in.at[1])
     first.start()
     start_groups(0)
-    start_all(fetch_up, 0)
-    start_all(fetch_down, 0)
-    second.start()
     exchange(0, n_layers - 1, 1)
     gain_out[...] = jnp.zeros_like(gain_out)
     first.wait()
@@ -371,12 +403,10 @@
         attention_forward(layer)
         if layer + 1 < n_layers:
             start_groups(layer + 1)
-        mlp_forward(layer)
-        if layer + 1 < n_layers:
+            mlp_forward(layer)
             start_all(fetch_up, layer + 1)
             start_all(fetch_down, layer + 1)
     second.wait()
-    flush()
     for layer in reversed(range(n_layers)):
         top = layer + 1 == n_layers
         mlp_backward(layer, top)
@@ -392,7 +422,7 @@
     done = put(grad, grad_out)
     flush()
     done.wait()
-    for copy in sent:
+    for copy in sent + [make() for make in streams]:
         copy.wait()
 
 
@@ -416,7 +446,7 @@
     vmem += [wide_rows, groups, (n_ff, seq_len, FF_BLOCK), wide_rows, wide_rows, (seq_len, GROUP)]
     scratch = [pltpu.VMEM(shape, bf16) for shape in vmem] + [pltpu.VMEM(shape, f32) for shape in ((seq_len, GROUP), (seq_len, GROUP), wide_rows)]
     scratch += [pltpu.VMEM(shape, bf16) for shape in ((3, n_group, width, GROUP), (n_group, GROUP, width), (n_ff, width, FF_BLOCK), (n_ff, FF_BLOCK, width))]
-    scratch += [pltpu.SemaphoreType.DMA(shape) for shape in ((3, n_group), (n_group,), (n_ff,), (n_ff,), (2,), (100,), (2 * len(early),), (2 * len(early),))]
+    scratch += [pltpu.SemaphoreType.DMA(shape) for shape in ((3, n_group), (n_group,), (n_ff,), (n_ff,), (2,), (100,), (2 * len(early),), (2 * len(early),)) + ((n_layers, n_ff // 2),) * 2]
     hbm, near = pl.BlockSpec(memory_space=pl.ANY), pl.BlockSpec(memory_space=pltpu.VMEM)
     results = pl.pallas_call(
         functools.partial(compute_kernel, n_layers), out_shape=tuple(outs), in_specs=[hbm, hbm, near, near] + [hbm] * 4,

time: 782 us -> 773 us (0.988)
  Pallas kernels: 709 us -> 701 us
where the time goes in v4:
time: 773 us; the launch traced here: 772 us
  Pallas kernels  701 us (91%)
  local copies, waits for them, and re-layouts  69.8 us (9%)
    pallas_call x1, Pallas kernels, combine(): pl.pallas_call(functools.partial(combine_kernel, n_dev, n_layers), out_sh...  566 us
    pallas_call x1, Pallas kernels, compute(): pl.pallas_call(functools.partial(compute_kernel, n_layers), out_shape=tup...  136 us
    unnamed x23, local copies, waits for them, and re-layouts  68.3 us

profile of v4, /device:TPU:1, one launch (start us, length us, event | category | flops | bytes accessed | tf_op | source)
XLA Modules:
  0.0 771.6 jit_solution(16685729869018208069)
XLA Ops:
  0.6 135.6 %shard_map.135 = (bf16[384,1024]{1,0:T(8,128)(2,1)}, f32[8,1024]{1,0:T(8,128)}, bf16[384,1024]{1,0:T(8,128)(2,1)}, bf16[384,1024]{1,0:T(8,128)(2,1)}, bf16[384,1...) custom-call(bf16[1,384,1024]{2,1,0:T(8,128)(2,1)} %x_in.1, ...), custom_call_target="tpu_custom_call" | custom-call | tf_op jit(solution)/shard_map/pallas_call | solution.py:451
  136.2 0.0 copy-start
  136.2 565.5 %shard_map.136 = (f32[2,4096,1024]{2,1,0:T(8,128)}, f32[2,1024,4096]{2,1,0:T(8,128)}, f32[2,1024,1024]{2,1,0:T(8,128)}, f32[2,1024,3072]{2,1,0:T(8,128)}, f32[8,...) custom-call(bf16[384,4096]{1,0:T(8,128)(2,1)} %get-tuple-element.42., ...), custom_call_target="tpu_custom_call" | custom-call | tf_op jit(solution)/shard_map/pallas_call | solution.py:826
  701.8 1.4 fusion
  703.2 0.0 copy-done
  703.2 0.9 copy.20
  704.1 17.7 %copy.21 = f32[2,1024,3072]{2,1,0:T(8,128)} copy(f32[2,1024,3072]{2,1,0:T(8,128)} %get-tuple-element.87) | data formatting | bytes 50331648
  721.9 0.0 slice-start
  721.9 0.0 slice-start.1
  721.9 8.6 %copy.22 = f32[2,1024,1024]{2,1,0:T(8,128)} copy(f32[2,1024,1024]{2,1,0:T(8,128)} %get-tuple-element.88) | data formatting | bytes 16777216
  730.4 0.0 slice-start.2
  730.4 0.0 slice-start.3
  730.4 0.0 slice-start.4
  730.5 0.0 slice-start.5
  730.5 0.0 slice-start.6
  730.5 0.0 slice-start.7
  730.5 26.7 %copy.23 = f32[2,1024,4096]{2,1,0:T(8,128)} copy(f32[2,1024,4096]{2,1,0:T(8,128)} %get-tuple-element.89) | data formatting | bytes 67108864
  757.1 0.0 slice-done
  757.1 0.0 slice-done.1
  757.2 0.0 slice-done.2
  757.2 0.0 slice-done.3
  757.2 0.0 slice-done.4
  757.2 0.0 slice-done.5
  757.2 1.6 slice-done.6
  758.7 1.2 slice-done.7
  759.9 11.7 %copy.24 = f32[2,4096,1024]{2,1,0:T(8,128)} copy(f32[2,4096,1024]{2,1,0:T(8,128)S(1)} %bitcast.3) | data formatting | bytes 67108864
  (1 shorter events, 0.0 us)
Async XLA Ops:
  136.2 567.0 %copy-start = (bf16[384,1024]{1,0:T(8,128)(2,1)S(1)}, bf16[384,1024]{1,0:T(8,128)(2,1)}, u32[]{:S(2)}) copy-start(bf16[384,1024]{1,0:T(8,128)(2,1)} %get-tuple-element.41) | copy-start | bytes 2359300
  721.9 35.3 %slice-start = ((s8[33554432]{0:T(1024)(128)(4,1)}), s8[4194304]{0:T(1024)(128)(4,1)S(1)}, s32[]{:S(2)}) async-start(s8[33554432]{0:T(1024)(128)(4,1)} %bitcast.2), calls=%async_computation | async-start | bytes 8388608
  721.9 35.3 %slice-start.1 = ((s8[33554432]{0:T(1024)(128)(4,1)}), s8[4194304]{0:T(1024)(128)(4,1)S(1)}, s32[]{:S(2)}) async-start(s8[33554432]{0:T(1024)(128)(4,1)} %bitcast.2), calls=%async_computation.1 | async-start | bytes 8388608
  730.4 26.7 %slice-start.2 = ((s8[33554432]{0:T(1024)(128)(4,1)}), s8[4194304]{0:T(1024)(128)(4,1)S(1)}, s32[]{:S(2)}) async-start(s8[33554432]{0:T(1024)(128)(4,1)} %bitcast.2), calls=%async_computation.2 | async-start | bytes 8388608
  730.4 26.7 %slice-start.3 = ((s8[33554432]{0:T(1024)(128)(4,1)}), s8[4194304]{0:T(1024)(128)(4,1)S(1)}, s32[]{:S(2)}) async-start(s8[33554432]{0:T(1024)(128)(4,1)} %bitcast.2), calls=%async_computation.3 | async-start | bytes 8388608
  730.4 26.7 %slice-start.4 = ((s8[33554432]{0:T(1024)(128)(4,1)}), s8[4194304]{0:T(1024)(128)(4,1)S(1)}, s32[]{:S(2)}) async-start(s8[33554432]{0:T(1024)(128)(4,1)} %bitcast.2), calls=%async_computation.4 | async-start | bytes 8388608
  730.5 26.7 %slice-start.5 = ((s8[33554432]{0:T(1024)(128)(4,1)}), s8[4194304]{0:T(1024)(128)(4,1)S(1)}, s32[]{:S(2)}) async-start(s8[33554432]{0:T(1024)(128)(4,1)} %bitcast.2), calls=%async_computation.5 | async-start | bytes 8388608
  730.5 28.3 %slice-start.6 = ((s8[33554432]{0:T(1024)(128)(4,1)}), s8[4194304]{0:T(1024)(128)(4,1)S(1)}, s32[]{:S(2)}) async-start(s8[33554432]{0:T(1024)(128)(4,1)} %bitcast.2), calls=%async_computation.6 | async-start | bytes 8388608
  730.5 29.5 %slice-start.7 = ((s8[33554432]{0:T(1024)(128)(4,1)}), s8[4194304]{0:T(1024)(128)(4,1)S(1)}, s32[]{:S(2)}) async-start(s8[33554432]{0:T(1024)(128)(4,1)} %bitcast.2), calls=%async_computation.7 | async-start | bytes 8388608

commit v5 on v4

--- a/solution.py
+++ b/solution.py
@@ -249,59 +249,62 @@
         return [put(src.at[at], dst.at[:, pl.ds(at * cols, cols)]) for at in range(count)]
 
     def exchange(mat, layer, which):
-        if (mat, layer) in LATE or (mat, which) == (1, 1):
-            return
+        if (mat, layer) in LATE or (mat, which) == (1, 1) or (mat, layer, which) == (0, n_layers - 1, 0):
+            return []
         axis, split = first_axis(mat, layer), MATRICES[mat][2]
-        name = FACTORS[mat][which]
-        src = grad_in.at[0] if (name, layer) == ('grad', n_layers - 1) else kept[layer][name]
-        if which == split:
-            dst = from_chip[(mat, layer)][0]
-            src = src.at[:, pl.ds(pl.multiple_of((1 - place[axis]) * dst.shape[1], 128), dst.shape[1])]
-        else:
-            dst = from_chip[(mat, layer)][1]
-        copy = pltpu.make_async_remote_copy(src_ref=src, dst_ref=dst, send_sem=sem_send.at[len(sent)], recv_sem=sem_recv.at[len(sent)],
-                                            device_id=(to[axis],), device_id_type=pl.DeviceIdType.MESH)
-        sent.append(copy)
-        copy.start()
+        name, order = FACTORS[mat][which], len(sent)
+
+        def make():
+            src = grad_in.at[0] if (name, layer) == ('grad', n_layers - 1) else kept[layer][name]
+            dst = from_chip[(mat, layer)][which != split]
+            if which == split:
+                src = src.at[:, pl.ds(pl.multiple_of((1 - place[axis]) * dst.shape[1], 128), dst.shape[1])]
+            return pltpu.make_async_remote_copy(src_ref=src, dst_ref=dst, send_sem=sem_send.at[order], recv_sem=sem_recv.at[order],
+                                                device_id=(to[axis],), device_id_type=pl.DeviceIdType.MESH)
+        sent.append(make)
+        return [make]
 
     def save(name, layer, copies):
         waiting.append((name, layer, copies))
 
-    def flush():
-        for name, layer, copies in waiting:
+    def planned_flush():
+        copies = [copy for _, _, group in waiting for copy in group]
+        makes = []
+        for name, layer, _ in waiting:
+            for mat, names in enumerate(FACTORS):
+                if name in names:
+                    makes += exchange(mat, layer, names.index(name))
+        waiting.clear()
+
+        def run():
             for copy in copies:
                 copy.wait()
-            for mat, names in enumerate(FACTORS):
-                if name in names:
-                    exchange(mat, layer, names.index(name))
-        waiting.clear()
+            for make in makes:
+                make().start()
+        return run
 
     def gain_row(gain, layer):
         return gain.at[pl.ds(layer, 1), :]
 
     def attention_forward(layer):
-        flush()
         norm_forward(rows[layer], gain_row(gain_one, layer), unit_rows)
-        if layer == 0:
-            for piece in fetch_group(layer, n_group - 1):
-                piece.wait()
-            start_all(fetch_up, 0)
-            start_all(fetch_down, 0)
-            second.start()
         save('u_one', layer, [put(unit_rows, kept[layer]['u_one'])])
         acc[...] = jnp.zeros_like(acc)
+        flush = planned_flush()
         q_all, k_all, v_all = (qkv[layer].at[which] for which in range(3))
 
         @pl.loop(0, n_group)
         def _(at):
-            if layer > 0:
-                for piece in fetch_group(layer, at):
-                    piece.wait()
-            else:
-                @pl.when(at < n_group - 1)
-                def _():
-                    for piece in fetch_group(layer, at):
-                        piece.wait()
+            for piece in fetch_group(layer, at):
+                piece.wait()
+
+            @pl.when(at == 1)
+            def _():
+                flush()
+                if layer == 0:
+                    start_all(fetch_up, 0)
+                    start_all(fetch_down, 0)
+                    second.start()
             for which in range(3):
                 qkv[layer][which, at] = rounded(dot_nn(unit_rows[...], s_qkv[which, at]))
             attend(q_all.at[at], k_all.at[at], v_all.at[at], mixed.at[at])
@@ -319,18 +322,19 @@
         return 0.5 * (1.0 + bend) + (0.5 * GELU_C) * rows_f * (1.0 - bend * bend) * (1.0 + (3.0 * GELU_D) * (rows_f * rows_f))
 
     def mlp_norm(layer):
-        flush()
         norm_forward(hidden[layer], gain_row(gain_two, layer), unit_rows)
         save('u_two', layer, [put(unit_rows, kept[layer]['u_two'])])
         acc[...] = jnp.zeros_like(acc)
 
     def mlp_forward(layer):
         mlp_norm(layer)
+        flush = planned_flush()
 
         @pl.loop(0, n_ff)
         def _(at):
             fetch_up(layer, at).wait()
             fetch_down(layer, at).wait()
+            pl.when(at == 1)(flush)
             pre[layer][at] = rounded(dot_nn(unit_rows[...], s_up[at]))
             rows_f = wide_float(pre[layer][at])
             act[at] = gelu(rows_f, bent(rows_f))
@@ -342,18 +346,22 @@
         if top:
             mlp_norm(layer)
         acc[...] = jnp.zeros_like(acc)
-        axis = first_axis(1, layer)
-
-        def stream(step, at):
+        axis, axis_down = first_axis(1, layer), first_axis(0, layer)
+        flush = planned_flush()
+
+        def stream(mat, spot, at):
+            line = layer if mat else n_layers
             return pltpu.make_async_remote_copy(
-                src_ref=pre[layer].at[at], dst_ref=from_chip[(1, layer)][0].at[:, pl.ds(pl.multiple_of(step * FF_BLOCK, FF_BLOCK), FF_BLOCK)],
-                send_sem=sem_out_blocks.at[layer, step], recv_sem=sem_in_blocks.at[layer, step], device_id=(to[axis],), device_id_type=pl.DeviceIdType.MESH)
+                src_ref=(act, pre[layer])[mat].at[at], dst_ref=from_chip[(mat, layer)][0].at[:, pl.ds(pl.multiple_of(spot * FF_BLOCK, FF_BLOCK), FF_BLOCK)],
+                send_sem=sem_out_blocks.at[line, spot], recv_sem=sem_in_blocks.at[line, spot],
+                device_id=(to[(axis_down, axis)[mat]],), device_id_type=pl.DeviceIdType.MESH)
 
         @pl.loop(0, n_ff)
         def _(step):
             at = lax.rem(step + (1 - place[axis]) * (n_ff // 2), n_ff)
             fetch_down(layer, at).wait()
             fetch_up(layer, at).wait()
+            pl.when(step == 1)(flush)
             rows_f = wide_float(rounded(dot_nn(unit_rows[...], s_up[at])) if top else pre[layer][at])
             bend = bent(rows_f)
             if top:
@@ -361,11 +369,10 @@
             grad_a = wide_float(rounded(dot_nt(grad[...], s_down[at])))
             pre[layer][at] = rounded(gelu_slope(rows_f, bend) * grad_a)
             acc[...] += dot_nt(pre[layer][at], s_up[at])
-            if (1, layer) not in LATE:
-                pl.when(step < n_ff // 2)(lambda: stream(step, at).start())
-        if (1, layer) not in LATE:
-            streams.extend(functools.partial(stream, step, step) for step in range(n_ff // 2))
-        flush()
+            pl.when(step < n_ff // 2)(lambda: stream(1, step, at).start())
+            if top:
+                pl.when(lax.div(at, n_ff // 2) == 1 - place[axis_down])(lambda: stream(0, lax.rem(at, n_ff // 2), at).start())
+        streams.extend(functools.partial(stream, mat, spot, spot) for mat in ((0, 1) if top else (1,)) for spot in range(n_ff // 2))
         if top:
             save('act', layer, put_blocks(act, kept[layer]['act']))
         save('grad_pre', layer, put_blocks(pre[layer], kept[layer]['grad_pre']))
@@ -374,17 +381,18 @@
 
     def attention_backward(layer, fetched):
         acc[...] = jnp.zeros_like(acc)
+        flush = planned_flush()
 
         @pl.loop(0, n_group)
         def _(at):
             if not fetched:
                 for piece in fetch_group(layer, at):
                     piece.wait()
+            pl.when(at == 1)(flush)
             do_ref[...] = rounded(dot_nt(grad_hidden[...], s_out[at]))
             attend_backward(do_ref, *(qkv[layer].at[which, at] for which in range(3)), k_acc, v_acc)
             for which in range(3):
                 acc[...] += dot_nt(qkv[layer][which, at], s_qkv[which, at])
-        flush()
         copies = []
         for which in range(3):
             width = grad.shape[1]
@@ -396,7 +404,7 @@
     second = pltpu.make_async_copy(grad_in.at[0], grad, sem_in.at[1])
     first.start()
     start_groups(0)
-    exchange(0, n_layers - 1, 1)
+    exchange(0, n_layers - 1, 1)[0]().start()
     gain_out[...] = jnp.zeros_like(gain_out)
     first.wait()
     for layer in range(n_layers):
@@ -413,17 +421,15 @@
         if layer > 0:
             start_all(fetch_up, layer - 1)
             start_all(fetch_down, layer - 1)
-        flush()
         attention_backward(layer, top)
         if layer > 0:
             start_groups(layer - 1)
             save('grad', layer - 1, [put(grad, kept[layer - 1]['grad'])])
-            flush()
     done = put(grad, grad_out)
-    flush()
+    planned_flush()()
     done.wait()
-    for copy in sent + [make() for make in streams]:
-        copy.wait()
+    for make in sent + streams:
+        make().wait()
 
 
 def compute(x_loc, grad_loc, gain_one, gain_two, w_qkv, w_out, w_up, w_down):
@@ -446,7 +452,7 @@
     vmem += [wide_rows, groups, (n_ff, seq_len, FF_BLOCK), wide_rows, wide_rows, (seq_len, GROUP)]
     scratch = [pltpu.VMEM(shape, bf16) for shape in vmem] + [pltpu.VMEM(shape, f32) for shape in ((seq_len, GROUP), (seq_len, GROUP), wide_rows)]
     scratch += [pltpu.VMEM(shape, bf16) for shape in ((3, n_group, width, GROUP), (n_group, GROUP, width), (n_ff, width, FF_BLOCK), (n_ff, FF_BLOCK, width))]
-    scratch += [pltpu.SemaphoreType.DMA(shape) for shape in ((3, n_group), (n_group,), (n_ff,), (n_ff,), (2,), (100,), (2 * len(early),), (2 * len(early),)) + ((n_layers, n_ff // 2),) * 2]
+    scratch += [pltpu.SemaphoreType.DMA(shape) for shape in ((3, n_group), (n_group,), (n_ff,), (n_ff,), (2,), (100,), (2 * len(early),), (2 * len(early),)) + ((n_layers + 1, n_ff // 2),) * 2]
     hbm, near = pl.BlockSpec(memory_space=pl.ANY), pl.BlockSpec(memory_space=pltpu.VMEM)
     results = pl.pallas_call(
         functools.partial(compute_kernel, n_layers), out_shape=tuple(outs), in_specs=[hbm, hbm, near, near] + [hbm] * 4,

time: 773 us -> 765 us (0.990)
  no operation moved by 1% of the time
where the time goes in v5:
time: 765 us; the launch traced here: 764 us
  Pallas kernels  694 us (91%)
  local copies, waits for them, and re-layouts  69.8 us (9%)
    pallas_call x1, Pallas kernels, combine(): pl.pallas_call(functools.partial(combine_kernel, n_dev, n_layers), out_sh...  566 us
    pallas_call x1, Pallas kernels, compute(): pl.pallas_call(functools.partial(compute_kernel, n_layers), out_shape=tup...  128 us
    unnamed x23, local copies, waits for them, and re-layouts  68.3 us

profile of v5, /device:TPU:1, one launch (start us, length us, event | category | flops | bytes accessed | tf_op | source)
XLA Modules:
  0.0 764.4 jit_solution(9242681985911864659)
XLA Ops:
  0.6 128.4 %shard_map.135 = (bf16[384,1024]{1,0:T(8,128)(2,1)}, f32[8,1024]{1,0:T(8,128)}, bf16[384,1024]{1,0:T(8,128)(2,1)}, bf16[384,1024]{1,0:T(8,128)(2,1)}, bf16[384,1...) custom-call(bf16[1,384,1024]{2,1,0:T(8,128)(2,1)} %x_in.1, ...), custom_call_target="tpu_custom_call" | custom-call | tf_op jit(solution)/shard_map/pallas_call | solution.py:457
  129.0 0.0 copy-start
  129.0 565.5 %shard_map.136 = (f32[2,4096,1024]{2,1,0:T(8,128)}, f32[2,1024,4096]{2,1,0:T(8,128)}, f32[2,1024,1024]{2,1,0:T(8,128)}, f32[2,1024,3072]{2,1,0:T(8,128)}, f32[8,...) custom-call(bf16[384,4096]{1,0:T(8,128)(2,1)} %get-tuple-element.42., ...), custom_call_target="tpu_custom_call" | custom-call | tf_op jit(solution)/shard_map/pallas_call | solution.py:832
  694.6 1.4 fusion
  696.0 0.0 copy-done
  696.0 0.9 copy.20
  696.9 17.7 %copy.21 = f32[2,1024,3072]{2,1,0:T(8,128)} copy(f32[2,1024,3072]{2,1,0:T(8,128)} %get-tuple-element.87) | data formatting | bytes 50331648
  714.6 0.0 slice-start
  714.6 0.0 slice-start.1
  714.6 8.6 %copy.22 = f32[2,1024,1024]{2,1,0:T(8,128)} copy(f32[2,1024,1024]{2,1,0:T(8,128)} %get-tuple-element.88) | data formatting | bytes 16777216
  723.2 0.0 slice-start.2
  723.2 0.0 slice-start.3
  723.2 0.0 slice-start.4
  723.2 0.0 slice-start.5
  723.2 0.0 slice-start.6
  723.2 0.0 slice-start.7
  723.3 26.7 %copy.23 = f32[2,1024,4096]{2,1,0:T(8,128)} copy(f32[2,1024,4096]{2,1,0:T(8,128)} %get-tuple-element.89) | data formatting | bytes 67108864
  749.9 0.0 slice-done
  749.9 0.0 slice-done.1
  749.9 0.0 slice-done.2
  749.9 0.0 slice-done.3
  750.0 0.0 slice-done.4
  750.0 0.0 slice-done.5
  750.0 1.6 slice-done.6
  751.5 1.2 slice-done.7
  752.7 11.7 %copy.24 = f32[2,4096,1024]{2,1,0:T(8,128)} copy(f32[2,4096,1024]{2,1,0:T(8,128)S(1)} %bitcast.3) | data formatting | bytes 67108864
  (1 shorter events, 0.0 us)
Async XLA Ops:
  129.0 567.0 %copy-start = (bf16[384,1024]{1,0:T(8,128)(2,1)S(1)}, bf16[384,1024]{1,0:T(8,128)(2,1)}, u32[]{:S(2)}) copy-start(bf16[384,1024]{1,0:T(8,128)(2,1)} %get-tuple-element.41) | copy-start | bytes 2359300
  714.6 35.3 %slice-start = ((s8[33554432]{0:T(1024)(128)(4,1)}), s8[4194304]{0:T(1024)(128)(4,1)S(1)}, s32[]{:S(2)}) async-start(s8[33554432]{0:T(1024)(128)(4,1)} %bitcast.2), calls=%async_computation | async-start | bytes 8388608
  714.6 35.3 %slice-start.1 = ((s8[33554432]{0:T(1024)(128)(4,1)}), s8[4194304]{0:T(1024)(128)(4,1)S(1)}, s32[]{:S(2)}) async-start(s8[33554432]{0:T(1024)(128)(4,1)} %bitcast.2), calls=%async_computation.1 | async-start | bytes 8388608
  723.2 26.7 %slice-start.2 = ((s8[33554432]{0:T(1024)(128)(4,1)}), s8[4194304]{0:T(1024)(128)(4,1)S(1)}, s32[]{:S(2)}) async-start(s8[33554432]{0:T(1024)(128)(4,1)} %bitcast.2), calls=%async_computation.2 | async-start | bytes 8388608
  723.2 26.7 %slice-start.3 = ((s8[33554432]{0:T(1024)(128)(4,1)}), s8[4194304]{0:T(1024)(128)(4,1)S(1)}, s32[]{:S(2)}) async-start(s8[33554432]{0:T(1024)(128)(4,1)} %bitcast.2), calls=%async_computation.3 | async-start | bytes 8388608
  723.2 26.7 %slice-start.4 = ((s8[33554432]{0:T(1024)(128)(4,1)}), s8[4194304]{0:T(1024)(128)(4,1)S(1)}, s32[]{:S(2)}) async-start(s8[33554432]{0:T(1024)(128)(4,1)} %bitcast.2), calls=%async_computation.4 | async-start | bytes 8388608
  723.2 26.7 %slice-start.5 = ((s8[33554432]{0:T(1024)(128)(4,1)}), s8[4194304]{0:T(1024)(128)(4,1)S(1)}, s32[]{:S(2)}) async-start(s8[33554432]{0:T(1024)(128)(4,1)} %bitcast.2), calls=%async_computation.5 | async-start | bytes 8388608
  723.2 28.3 %slice-start.6 = ((s8[33554432]{0:T(1024)(128)(4,1)}), s8[4194304]{0:T(1024)(128)(4,1)S(1)}, s32[]{:S(2)}) async-start(s8[33554432]{0:T(1024)(128)(4,1)} %bitcast.2), calls=%async_computation.6 | async-start | bytes 8388608
  723.2 29.5 %slice-start.7 = ((s8[33554432]{0:T(1024)(128)(4,1)}), s8[4194304]{0:T(1024)(128)(4,1)S(1)}, s32[]{:S(2)}) async-start(s8[33554432]{0:T(1024)(128)(4,1)} %bitcast.2), calls=%async_computation.7 | async-start | bytes 8388608

commit v6 on v5

--- a/solution.py
+++ b/solution.py
@@ -58,8 +58,6 @@
 Q_BLOCK = 128
 FF_BLOCK = 512
 NORM_ROWS = 128
-FORWARD_STEPS = ((0, 1, 2),)
-BACKWARD_STEPS = ((2, 1, 0),)
 GELU_C = 0.7978845608028654
 GELU_D = 0.044715
 
@@ -150,34 +148,32 @@
 
 
 def attend(q_ref, k_ref, v_ref, o_ref):
-    for blocks in FORWARD_STEPS:
-        jobs = jobs_of(blocks)
-        probs = softmax_blocks([two_heads(q_ref[rows, lanes]) for rows, _, lanes in jobs], [k_ref[keys, lanes] for _, keys, lanes in jobs])
-        results = in_step(lambda prob, job: dot_nn(rounded(prob), v_ref[job[1], job[2]]), probs, jobs)
-        for result, (rows, _, lanes) in zip(results, jobs):
-            o_ref[rows, lanes] = rounded(one_pair(result))
+    jobs = jobs_of(range(q_ref.shape[0] // Q_BLOCK))
+    probs = softmax_blocks([two_heads(q_ref[rows, lanes]) for rows, _, lanes in jobs], [k_ref[keys, lanes] for _, keys, lanes in jobs])
+    results = in_step(lambda prob, job: dot_nn(rounded(prob), v_ref[job[1], job[2]]), probs, jobs)
+    for result, (rows, _, lanes) in zip(results, jobs):
+        o_ref[rows, lanes] = rounded(one_pair(result))
 
 
 def attend_backward(do_ref, q_ref, k_ref, v_ref, k_acc, v_acc):
-    for blocks in BACKWARD_STEPS:
-        jobs = jobs_of(blocks)
-        q_twos, g_twos = ([two_heads(ref[rows, lanes]) for rows, _, lanes in jobs] for ref in (q_ref, do_ref))
-        k_rows = [k_ref[keys, lanes] for _, keys, lanes in jobs]
-        grad_probs = in_step(lambda g_two, job: dot_nt(g_two, v_ref[job[1], job[2]]), g_twos, jobs)
-        probs = softmax_blocks(q_twos, k_rows)
-        means = in_step(lambda prob, grad_prob: jnp.sum(prob * grad_prob, axis=-1, keepdims=True), probs, grad_probs)
-        grad_s = in_step(lambda prob, grad_prob, mean: rounded(prob * (grad_prob - mean) * HEAD_DIM ** -0.5), probs, grad_probs, means)
-        q_grads = in_step(dot_nn, grad_s, k_rows)
-        k_parts = in_step(dot_tn, grad_s, q_twos)
-        v_parts = in_step(lambda prob, g_two: dot_tn(rounded(prob), g_two), probs, g_twos)
-        for q_grad, k_part, v_part, (rows, keys, lanes) in zip(q_grads, k_parts, v_parts, jobs):
-            q_ref[rows, lanes] = rounded(one_pair(q_grad))
-            if keys.size == q_ref.shape[0]:
-                k_acc[:, lanes] = k_part
-                v_acc[:, lanes] = v_part
-            else:
-                k_acc[keys, lanes] += k_part
-                v_acc[keys, lanes] += v_part
+    jobs = jobs_of(reversed(range(q_ref.shape[0] // Q_BLOCK)))
+    q_twos, g_twos = ([two_heads(ref[rows, lanes]) for rows, _, lanes in jobs] for ref in (q_ref, do_ref))
+    k_rows = [k_ref[keys, lanes] for _, keys, lanes in jobs]
+    grad_probs = in_step(lambda g_two, job: dot_nt(g_two, v_ref[job[1], job[2]]), g_twos, jobs)
+    probs = softmax_blocks(q_twos, k_rows)
+    means = in_step(lambda prob, grad_prob: jnp.sum(prob * grad_prob, axis=-1, keepdims=True), probs, grad_probs)
+    grad_s = in_step(lambda prob, grad_prob, mean: rounded(prob * (grad_prob - mean) * HEAD_DIM ** -0.5), probs, grad_probs, means)
+    q_grads = in_step(dot_nn, grad_s, k_rows)
+    k_parts = in_step(dot_tn, grad_s, q_twos)
+    v_parts = in_step(lambda prob, g_two: dot_tn(rounded(prob), g_two), probs, g_twos)
+    for q_grad, k_part, v_part, (rows, keys, lanes) in zip(q_grads, k_parts, v_parts, jobs):
+        q_ref[rows, lanes] = rounded(one_pair(q_grad))
+        if keys.size == q_ref.shape[0]:
+            k_acc[:, lanes] = k_part
+            v_acc[:, lanes] = v_part
+        else:
+            k_acc[keys, lanes] += k_part
+            v_acc[keys, lanes] += v_part
     k_ref[...] = rounded(k_acc[...])
     v_ref[...] = rounded(v_acc[...])
 
@@ -840,13 +836,60 @@
     return results[:5]
 
 
+COPY_SLOTS = 8
+COPY_AHEAD = COPY_SLOTS // 2
+COPY_WORDS = 512 * 1024
+
+
+def copy_kernel(n_job, *refs):
+    count = len(MATRICES)
+    pairs, (*slots, in_sems, out_sems) = zip(refs[:count], refs[count:count + count]), refs[count + count:]
+    loads, stores, reused, used = [], [], [], {}
+    for src, dst in pairs:
+        layers, height, cols = src.shape
+        slot, = [ref for ref in slots if ref.shape[-1] == cols]
+        _, size, _ = slot.shape
+        for layer in range(layers):
+            for start in range(0, height, size):
+                turn = used.setdefault(cols, [])
+                at, rows, order = len(turn) % COPY_SLOTS, pl.ds(start, size), len(loads)
+                reused.append(turn[-COPY_SLOTS] if len(turn) >= COPY_SLOTS else None)
+                turn.append(order)
+                loads.append(pltpu.make_async_copy(src.at[layer, rows, :], slot.at[at], in_sems.at[order]))
+                stores.append(pltpu.make_async_copy(slot.at[at], dst.at[layer, rows, :], out_sems.at[order]))
+    left = set(range(n_job))
+    for step in range(n_job + COPY_AHEAD):
+        if step < n_job:
+            if reused[step] is not None:
+                stores[reused[step]].wait()
+                left.remove(reused[step])
+            loads[step].start()
+        if step >= COPY_AHEAD:
+            loads[step - COPY_AHEAD].wait()
+            stores[step - COPY_AHEAD].start()
+    for order in sorted(left):
+        stores[order].wait()
+
+
+def copied(sums):
+    rows_of = {val.shape[-1]: COPY_WORDS // val.shape[-1] // PAIR * PAIR for val in sums}
+    n_job = sum(val.size // (rows_of[val.shape[-1]] * val.shape[-1]) for val in sums)
+    hbm = pl.BlockSpec(memory_space=pl.ANY)
+    return pl.pallas_call(
+        functools.partial(copy_kernel, n_job), out_shape=tuple(jax.ShapeDtypeStruct(val.shape, val.dtype) for val in sums),
+        in_specs=[hbm] * len(sums), out_specs=tuple([hbm] * len(sums)),
+        scratch_shapes=[pltpu.VMEM((COPY_SLOTS, rows, width), jnp.float32) for width, rows in rows_of.items()] + [pltpu.SemaphoreType.DMA((n_job,))] * 2,
+        compiler_params=pltpu.CompilerParams(vmem_limit_bytes=VMEM_LIMIT))(*sums)
+
+
 def solution(mesh):
     n_dev = mesh.shape[AXIS]
 
     def local_step(x_loc, grad_y_loc, gain_one, gain_two, w_qkv, w_out, w_up, w_down):
         n_layers = w_qkv.shape[0]
         grad_x, gains, operands = compute(x_loc, grad_y_loc, gain_one, gain_two, w_qkv, w_out, w_up, w_down)
-        down, up, out, qkv, gains = combine(operands, gains, n_dev, n_layers)
+        *sums, gains = combine(operands, gains, n_dev, n_layers)
+        down, up, out, qkv = copied(sums)
         return (grad_x[None], gains[:n_layers], gains[n_layers:2 * n_layers], qkv, out, up, down)
 
     batch_spec = P(AXIS)

time: 765 us -> 765 us (level)
  local copies, waits for them, and re-layouts: 69.8 us -> 2.33 us
  Pallas kernels: 694 us -> 761 us
    unnamed x23 -> x3, local copies, waits for them, and re-layouts: 68.3 us -> 0.89 us
    pallas_call x0 -> x1, Pallas kernels: none -> 66.8 us  [copied(): pl.pallas_call(functools.partial(copy_kernel, n_job), out_shape=tuple((ja...]
where the time goes in v6:
time: 765 us; the launch traced here: 764 us
  Pallas kernels  761 us (99%)
    pallas_call x1, Pallas kernels, combine(): pl.pallas_call(functools.partial(combine_kernel, n_dev, n_layers), out_sh...  566 us
    pallas_call x1, Pallas kernels, compute(): pl.pallas_call(functools.partial(compute_kernel, n_layers), out_shape=tup...  128 us
    pallas_call x1, Pallas kernels, copied(): pl.pallas_call(functools.partial(copy_kernel, n_job), out_shape=tuple((ja...  66.8 us

profile of v6, /device:TPU:1, one launch (start us, length us, event | category | flops | bytes accessed | tf_op | source)
XLA Modules:
  0.0 763.7 jit_solution(15382891707760843907)
XLA Ops:
  0.6 128.4 %shard_map.135 = (bf16[384,1024]{1,0:T(8,128)(2,1)}, f32[8,1024]{1,0:T(8,128)}, bf16[384,1024]{1,0:T(8,128)(2,1)}, bf16[384,1024]{1,0:T(8,128)(2,1)}, bf16[384,1...) custom-call(bf16[1,384,1024]{2,1,0:T(8,128)(2,1)} %x_in.1, ...), custom_call_target="tpu_custom_call" | custom-call | tf_op jit(solution)/shard_map/pallas_call | solution.py:453
  129.0 565.5 %shard_map.136 = (f32[2,4096,1024]{2,1,0:T(8,128)}, f32[2,1024,4096]{2,1,0:T(8,128)}, f32[2,1024,1024]{2,1,0:T(8,128)}, f32[2,1024,3072]{2,1,0:T(8,128)}, f32[8,...) custom-call(bf16[384,4096]{1,0:T(8,128)(2,1)} %get-tuple-element.46., ...), custom_call_target="tpu_custom_call" | custom-call | tf_op jit(solution)/shard_map/pallas_call | solution.py:828
  694.6 1.4 fusion
  696.0 0.0 copy-start
  696.0 66.8 %shard_map.137 = (f32[2,4096,1024]{2,1,0:T(8,128)}, f32[2,1024,4096]{2,1,0:T(8,128)}, f32[2,1024,1024]{2,1,0:T(8,128)}, f32[2,1024,3072]{2,1,0:T(8,128)}) custom-call(f32[2,4096,1024]{2,1,0:T(8,128)} %get-tuple-element.75.refs_0_, f32[2,1024,4096]{2,1,0:T(8,128)} %get-tuple-element.76.refs_1_, f32[2,1024,1024]{2,1,0:T(8,128)} %get-tuple-element.77.refs_2_, ...), custom_call_target="tpu_custom_call" | custom-call | tf_op jit(solution)/shard_map/pallas_call | solution.py:878
  762.8 0.0 copy-done
  762.8 0.9 copy.16
Async XLA Ops:
  696.0 66.8 %copy-start = (bf16[384,1024]{1,0:T(8,128)(2,1)S(1)}, bf16[384,1024]{1,0:T(8,128)(2,1)}, u32[]{:S(2)}) copy-start(bf16[384,1024]{1,0:T(8,128)(2,1)} %get-tuple-element.45) | copy-start | bytes 2359300
